TPU v7x, 16 devices: a whole 2x2x2 slice. The times are simulated.
16 devices in a mesh: dp: 4 (over z, y), tp: 4 (over x, core).
Axes of the slice: x: 2, y: 2, z: 2, core: 2. Of those that a mesh axis runs over, the one named last changes fastest.
Arguments:
- x_steps: bfloat16 [4, 4096, 512], P(None, 'dp'), parts along dimension 1
- conv_state: bfloat16 [4096, 1024, 3], P('dp', 'tp'), parts along dimension 0
- ssm_state: float32 [4096, 1024, 16], P('dp', 'tp'), parts along dimension 0
- expert_ids: int32 [4, 4096, 1], P(None, 'dp'), parts along dimension 1
- g_in: bfloat16 [512], replicated
- w_in: bfloat16 [512, 2, 1024], P(None, None, 'tp')
- conv_w: bfloat16 [1024, 4], P('tp')
- conv_b: bfloat16 [1024], P('tp')
- w_xp: bfloat16 [1024, 64], P('tp')
- g_dt: bfloat16 [32], replicated
- g_b: bfloat16 [16], replicated
- g_c: bfloat16 [16], replicated
- w_dt: bfloat16 [32, 1024], P(None, 'tp')
- b_dt: bfloat16 [1024], P('tp')
- a_log: float32 [1024, 16], P('tp')
- d_skip: float32 [1024], P('tp')
- w_out: bfloat16 [1024, 512], P('tp')
- g_ff: bfloat16 [512], replicated
- w_router: bfloat16 [512, 16], replicated
- w_gate: bfloat16 [16, 512, 2048], P(None, None, 'tp')
- w_up: bfloat16 [16, 512, 2048], P(None, None, 'tp')
- w_down: bfloat16 [16, 2048, 512], P(None, 'tp')
Outputs:
- output 1: bfloat16 [4, 4096, 512], P(None, 'dp'), parts along dimension 1
- output 2: bfloat16 [4096, 1024, 3], P('dp', 'tp'), parts along dimension 0
- output 3: float32 [4096, 1024, 16], P('dp', 'tp'), parts along dimension 0
There are 4 independent parts. A program takes and returns all parts, laid end to end along the dimension named above; an argument that names none is the same for every part.
All inputs are finite; a program needn't handle non-finite values.
Results may differ from a plain program's by a relative error of at most 0.0141754.
Values are sent between devices in bfloat16 or wider.
A program may use at most 1 GiB of HBM per device.

v0:
```python
import functools

import jax
import jax.numpy as jnp
from jax import lax
from jax.experimental import pallas as pl
from jax.experimental.pallas import tpu as pltpu
from jax.sharding import PartitionSpec as P


EPSILON = 1e-6
CHUNKS = 4
ROW_ALIGN = 16
TILE = 128
GROUP = 2
RING = 6
WHOLE = 2
F32 = jnp.float32
BF16 = jnp.bfloat16
HBM = pl.BlockSpec(memory_space=pl.ANY)


def params(**kw):
    return pltpu.CompilerParams(vmem_limit_bytes=56 * 1024 * 1024, **kw)


def row(ref):
    return ref[...].astype(F32).reshape(1, -1)


def norm_rows(v, gain):
    return v * lax.rsqrt(jnp.mean(v * v, axis=-1, keepdims=True) + EPSILON) * gain


def mm_t(a, b):
    return lax.dot_general(a, b, (((1,), (1,)), ((), ())), preferred_element_type=F32)


def silu(v):
    return v * jax.nn.sigmoid(v)


def routes_kernel(ids_ref, pos_ref, tab_ref):
    chunks, _, tokens = pos_ref.shape
    steps = ids_ref.shape[0]
    rows = tokens // steps
    experts = 16
    upper = (lax.broadcasted_iota(jnp.int32, (tokens, tokens), 0) <= lax.broadcasted_iota(jnp.int32, (tokens, tokens), 1)).astype(F32).astype(BF16)
    before = (lax.broadcasted_iota(jnp.int32, (experts, experts), 1) < lax.broadcasted_iota(jnp.int32, (experts, experts), 0)).astype(F32).astype(BF16)
    lane = lax.broadcasted_iota(jnp.int32, (experts, 128), 1)
    number = lax.broadcasted_iota(jnp.int32, (experts, 128), 0).astype(F32)
    for c in range(chunks):
        g, k = c // GROUP, c % GROUP
        ids = jnp.concatenate([ids_ref[s, :, c * rows:(c + 1) * rows] for s in range(steps)], axis=1)
        hit = lax.broadcasted_iota(jnp.int32, (experts, tokens), 0) == ids
        hot = hit.astype(F32)
        rank = jnp.dot(hot.astype(BF16), upper, preferred_element_type=F32)
        count = jnp.broadcast_to(jnp.sum(hot, axis=1, keepdims=True), (experts, 128))
        blocks = jnp.floor((count + (ROW_ALIGN - 1)) * (1.0 / ROW_ALIGN))
        start = ROW_ALIGN * jnp.dot(before, blocks.astype(BF16), preferred_element_type=F32)
        pos_ref[c] = jnp.sum(hot * (start[:, :1] + rank - 1.0), axis=0, keepdims=True).astype(jnp.int32)
        tab_ref[g, 16 * k:16 * k + 16, :] = jnp.where(lane == 0, start, count).astype(jnp.int32)
        total = count if k == 0 else total + count
        if k == GROUP - 1:
            active = (total > 0.0).astype(F32)
            place = jnp.dot(before, active.astype(BF16), preferred_element_type=F32)
            listed = jnp.sum(jnp.where((place == lane.astype(F32)) & (active > 0.0), number, 0.0), axis=0, keepdims=True)
            tab_ref[g, 16 * GROUP:16 * GROUP + 1, :] = listed.astype(jnp.int32)
            tab_ref[g, 16 * GROUP + 1:16 * GROUP + 2, :] = jnp.sum(active, axis=0, keepdims=True).astype(jnp.int32)


LOG2E = 1.4426950408889634


def mamba_kernel(x_hbm, cs_hbm, h_hbm, g_ref, win3_ref, cw_ref, cb_ref, wxp_ref, gdt_ref, gb_ref, gc_ref, wdt_ref, bdt_ref, alog_ref, dskip_ref, wout_ref,
                 uo_hbm, us_hbm, chip2_hbm, chip3_hbm, co_hbm, ho_hbm,
                 x_s, cs_s, co_s, h_s, xc_s, z_s, p_s, m_s, u_s, win_ref, g4_ref, wdt4, ones_s, even_s, odd_s, a_s, q_s, delta_s, dx_s, y_s,
                 in_sem, h_sem, out_sem, ho_sem, psend, precv, msend, mrecv):
    steps, batch, _ = x_s.shape
    inner = cs_s.shape[2]
    state = alog_ref.shape[0]
    rank = wdt_ref.shape[0]
    width = rank + 2 * state
    lanes = steps * width
    half = steps // 2
    rows = batch // CHUNKS
    tiles = inner // 128
    me = lax.axis_index("tp")
    core = lax.rem(me, 2)
    sibling = me + 1 - 2 * core
    partner = lax.rem(me + 2, 4)

    barrier = pltpu.get_barrier_semaphore()
    for peer in (sibling, partner):
        pl.semaphore_signal(barrier, inc=1, device_id={"tp": peer}, device_id_type=pl.DeviceIdType.MESH)

    def span(c):
        return pl.ds(c * rows, rows)

    def loads(c):
        return [
            pltpu.make_async_copy(x_hbm.at[:, span(c), :], x_s.at[:, span(c), :], in_sem.at[0, c]),
            pltpu.make_async_copy(cs_hbm.at[:, span(c), :], cs_s.at[:, span(c), :], in_sem.at[1, c]),
        ]

    def state_rows(c):
        return pl.ds(c * rows * state, rows * state)

    def h_loads(c):
        return [pltpu.make_async_copy(h_hbm.at[state_rows(c), pl.ds(l * 128, 128)], h_s.at[l, state_rows(c), :], h_sem.at[l, c]) for l in range(tiles)]

    def h_stores(c):
        return [pltpu.make_async_copy(h_s.at[l, state_rows(c), :], ho_hbm.at[state_rows(c), pl.ds(l * 128, 128)], ho_sem.at[l, c]) for l in range(tiles)]

    def co_store(c):
        return pltpu.make_async_copy(co_s.at[:, span(c), :], co_hbm.at[:, span(c), :], out_sem.at[0, c])

    def remote(buf, c, src, dst, send, recv, stage, peer):
        return pltpu.make_async_remote_copy(
            src_ref=buf.at[src, c], dst_ref=buf.at[dst, c], send_sem=send.at[stage, c], recv_sem=recv.at[stage, c],
            device_id={"tp": peer}, device_id_type=pl.DeviceIdType.MESH)

    def p_beside(c):
        return remote(p_s, c, 1, 2, psend, precv, 0, sibling)

    def p_across(c):
        return remote(p_s, c, 3, 4, psend, precv, 1, partner)

    def p_back(c):
        return remote(p_s, c, 5, 6, psend, precv, 2, sibling)

    def m_beside(c):
        return remote(m_s, c, 1, 2, msend, mrecv, 0, sibling)

    def m_across(c):
        return remote(m_s, c, 3, 4, msend, mrecv, 1, partner)

    def u_back(c):
        return pltpu.make_async_remote_copy(
            src_ref=u_s.at[0, c], dst_ref=u_s.at[1, c], send_sem=msend.at[2, c], recv_sem=mrecv.at[2, c],
            device_id={"tp": sibling}, device_id_type=pl.DeviceIdType.MESH)

    for c in range(CHUNKS):
        for cp in loads(c):
            cp.start()
    for c in range(CHUNKS):
        for cp in h_loads(c):
            cp.start()

    gain = row(g_ref)
    for k in range(2):
        win_ref[:, k * inner:(k + 1) * inner] = win3_ref[:, k, :]

    def project(c):
        for cp in loads(c):
            cp.wait()

        def block(i, carry):
            r = pl.multiple_of(c * rows + i * 128, 128)
            seq = [cs_s[j, pl.ds(r, 128), :].astype(F32) for j in range(3)]
            part = []
            for s in range(steps):
                x = x_s[s, pl.ds(r, 128), :].astype(F32)
                n = norm_rows(x, gain).astype(BF16)
                xz = jnp.dot(n, win_ref[...], preferred_element_type=F32).astype(BF16)
                z_s[s, pl.ds(r, 128), :] = xz[:, inner:]
                xi = xz[:, :inner]
                if s > 0:
                    co_s[s - 1, pl.ds(r, 128), :] = xi
                seq.append(xi.astype(F32))
                acc = seq[s] * cw_ref[0:1, :].astype(F32)
                for j in range(1, 4):
                    acc = acc + seq[s + j] * cw_ref[j:j + 1, :].astype(F32)
                xc = silu(acc + row(cb_ref)).astype(BF16)
                xc_s[s, pl.ds(r, 128), :] = xc
                part.append(mm_t(xc, wxp_ref[...]))
            low = jnp.concatenate(part[:2], axis=1)
            high = jnp.concatenate(part[2:], axis=1)
            q = pl.multiple_of(i * 128, 128)
            p_s[0, c, pl.ds(q, 128), :] = jnp.where(core == 0, low, high)
            p_s[1, c, pl.ds(q, 128), :] = jnp.where(core == 0, high, low)
            return carry

        lax.fori_loop(0, rows // 128, block, 0)
        co_store(c).start()

    def p_sum(c):
        p_beside(c).wait_recv()
        p_s[3, c] = p_s[0, c] + p_s[2, c]
        p_across(c).start()

    def p_whole(c):
        p_across(c).wait_recv()
        p_s[5, c] = p_s[3, c] + p_s[4, c]
        p_back(c).start()

    def scan(c):
        p_back(c).wait_recv()
        for cp in h_loads(c):
            cp.wait()

        def block(i, carry):
            r = pl.multiple_of(i * 128, 128)
            g = pl.multiple_of(c * rows + i * 128, 128)
            own, sib = p_s[5, c, pl.ds(r, 128), :], p_s[6, c, pl.ds(r, 128), :]
            p = jnp.concatenate([jnp.where(core == 0, own, sib), jnp.where(core == 0, sib, own)], axis=1)
            sq = p * p
            s1 = sq.astype(BF16)
            rest = sq - s1.astype(F32)
            s2 = rest.astype(BF16)
            s3 = (rest - s2.astype(F32)).astype(BF16)
            mean = sum(jnp.dot(v, ones_s[...], preferred_element_type=F32) for v in (s3, s2, s1))
            norm = p * lax.rsqrt(mean + EPSILON) * g4_ref[...]
            for s in range(steps):
                first = s * width + rank
                q_s[s] = jnp.concatenate([norm[:, first:first + 2 * state], jnp.zeros((128, 128 - 2 * state), F32)], axis=1)
            pre = jnp.dot(norm.astype(BF16), wdt4[...], preferred_element_type=F32)
            bias = row(bdt_ref)
            for s in range(steps):
                v = pre[:, s * inner:(s + 1) * inner] + bias
                delta = jnp.maximum(v, 0.0) + jnp.log1p(jnp.exp(-jnp.abs(v)))
                delta_s[s] = delta
                dx_s[s] = delta * xc_s[s, pl.ds(g, 128), :].astype(F32)

            def spread(t, wide):
                b = pl.multiple_of(t * 8, 8)
                qs = [q_s[s, pl.ds(b, 8), :] for s in range(steps)]
                for n in range(2 * state):
                    for s in range(steps):
                        wide[s, n] = jnp.broadcast_to(qs[s][:, n:n + 1], (8, 128))

            def advance(t, wide):
                b = pl.multiple_of(t * 8, 8)
                base = (g + b) * state
                cut = [slice(l * 128, (l + 1) * 128) for l in range(tiles)]
                dl = [[delta_s[s, pl.ds(b, 8), k] for k in cut] for s in range(steps)]
                dx = [[dx_s[s, pl.ds(b, 8), k] for k in cut] for s in range(steps)]
                ys = [[None] * tiles for _ in range(steps)]
                for n in range(state):
                    for l in range(tiles):
                        a = a_s[n:n + 1, cut[l]]
                        spot = (l, pl.ds(base + n, 8, stride=state))
                        h = h_s[spot]
                        for s in range(steps):
                            h = jnp.exp2(dl[s][l] * a) * h + dx[s][l] * wide[s, n]
                            hc = h * wide[s, n + state]
                            ys[s][l] = hc if n == 0 else ys[s][l] + hc
                        h_s[spot] = h
                for s in range(steps):
                    for l in range(tiles):
                        y_s[s, pl.ds(b, 8), cut[l]] = ys[s][l]

            def pair(i, carry2):
                t = 2 * i
                spread(t + 1, odd_s)
                advance(t, even_s)
                spread(jnp.minimum(t + 2, 14), even_s)
                advance(t + 1, odd_s)
                return carry2

            spread(0, even_s)
            lax.fori_loop(0, 8, pair, 0)
            for s in range(steps):
                xc = xc_s[s, pl.ds(g, 128), :].astype(F32)
                yg = ((y_s[s] + row(dskip_ref) * xc) * silu(z_s[s, pl.ds(g, 128), :].astype(F32))).astype(BF16)
                out = jnp.dot(yg, wout_ref[...], preferred_element_type=F32).astype(BF16)
                m_s[lax.rem(core + s // half, 2), c, s % half, pl.ds(r, 128), :] = out
            return carry

        lax.fori_loop(0, rows // 128, block, 0)
        for cp in h_stores(c):
            cp.start()
        m_beside(c).start()

    def chip_out(c):
        return pltpu.make_async_copy(m_s.at[3, c], (chip2_hbm, chip3_hbm)[c - WHOLE], out_sem.at[1, c])

    def m_sum(c):
        m_beside(c).wait_recv()
        for s in range(half):
            m_s[3, c, s] = (m_s[0, c, s].astype(F32) + m_s[2, c, s].astype(F32)).astype(BF16)
        if c < WHOLE:
            m_across(c).start()
        else:
            chip_out(c).start()

    def uo_out(c):
        return pltpu.make_async_copy(u_s.at[0, c], uo_hbm.at[c], out_sem.at[1, c])

    def us_out(c):
        return pltpu.make_async_copy(u_s.at[1, c], us_hbm.at[c], out_sem.at[2, c])

    def m_whole(c):
        m_across(c).wait_recv()
        for s in range(half):
            x = x_s[core * half + s, span(c), :].astype(F32)
            u_s[0, c, s] = (x + (m_s[3, c, s].astype(F32) + m_s[4, c, s].astype(F32))).astype(BF16)
        u_back(c).start()
        uo_out(c).start()

    project(0)
    pl.semaphore_wait(barrier, 2)
    p_beside(0).start()
    project(1)
    p_beside(1).start()
    p_sum(0)
    project(2)
    p_beside(2).start()
    p_sum(1)
    project(3)
    p_beside(3).start()
    p_sum(2)
    p_whole(0)

    wdt4[...] = jnp.zeros_like(wdt4)
    for s in range(steps):
        wdt4[s * width:s * width + rank, s * inner:(s + 1) * inner] = wdt_ref[...]

    def group(v):
        step, col = v // width, lax.rem(v, width)
        return step * 4 + (col >= rank).astype(jnp.int32) + (col >= rank + state).astype(jnp.int32)

    gi = group(lax.broadcasted_iota(jnp.int32, (lanes, lanes), 0))
    gj = group(lax.broadcasted_iota(jnp.int32, (lanes, lanes), 1))
    inv = jnp.where(lax.rem(gj, 4) == 0, 1.0 / rank, 1.0 / state)
    ones_s[...] = jnp.where(gi == gj, inv, 0.0).astype(BF16)
    for s in range(steps):
        for ref, at in ((gdt_ref, 0), (gb_ref, rank), (gc_ref, rank + state)):
            g4_ref[:, s * width + at:s * width + at + ref.shape[0]] = row(ref)
    a_s[...] = -LOG2E * jnp.exp(alog_ref[...])

    p_sum(3)
    p_whole(1)
    scan(0)
    p_whole(2)
    p_whole(3)
    m_sum(0)
    scan(1)
    m_sum(1)
    scan(2)
    m_sum(2)
    m_whole(0)
    scan(3)
    m_sum(3)
    for c in range(1, WHOLE):
        m_whole(c)
    for c in range(WHOLE):
        u_back(c).wait_recv()
        us_out(c).start()
    for c in range(CHUNKS):
        p_beside(c).wait_send()
        p_across(c).wait_send()
        p_back(c).wait_send()
        m_beside(c).wait_send()
        co_store(c).wait()
        for cp in h_stores(c):
            cp.wait()
        if c < WHOLE:
            m_across(c).wait_send()
            u_back(c).wait_send()
            uo_out(c).wait()
            us_out(c).wait()
        else:
            chip_out(c).wait()


def moe_kernel(g, *refs):
    tab_ref, pos_ref = refs[:2]
    us = refs[2:2 + 2 * GROUP]
    gff_ref, wr_ref, wg_ref, wu_ref, wd_ref, h_hbm, cv_hbm = refs[2 + 2 * GROUP:9 + 2 * GROUP]
    outs = refs[-14 - 2 * GROUP:-14]
    ho_hbm, co_hbm, wg, wu, wd, sems, m_s, hot_s, in_s, out_s, prob_s, h_s, cv_s, st_sem = refs[-14:]
    _, half, rows, d_model = us[0].shape
    experts = wr_ref.shape[0]
    tokens = 2 * half * rows
    slots = hot_s.shape[0] // GROUP
    room = in_s.shape[0] // GROUP
    core = lax.rem(lax.axis_index("tp"), 2)
    active = tab_ref[0, 16 * GROUP + 1, 0]

    def copies(i):
        e = tab_ref[0, 16 * GROUP, i]
        slot = lax.rem(i, RING)
        return [pltpu.make_async_copy(src.at[e], dst.at[slot], sems.at[k, slot]) for k, (src, dst) in enumerate(((wg_ref, wg), (wu_ref, wu), (wd_ref, wd)))]

    def fetch(i):
        @pl.when(i < active)
        def _():
            for cp in copies(i):
                cp.start()

    for i in range(RING - 1):
        fetch(i)
    h_span = pl.ds(g * h_s.shape[0], h_s.shape[0])
    cv_span = pl.ds(g * cv_s.shape[1], cv_s.shape[1])
    pulls = [pltpu.make_async_copy(h_hbm.at[h_span, :], h_s, st_sem.at[0]), pltpu.make_async_copy(cv_hbm.at[:, cv_span, :], cv_s, st_sem.at[1])]
    pushes = [pltpu.make_async_copy(h_s, ho_hbm.at[h_span, :], st_sem.at[2]), pltpu.make_async_copy(cv_s, co_hbm.at[:, cv_span, :], st_sem.at[3])]
    for cp in pulls:
        cp.start()
    gain = row(gff_ref)
    for j in range(GROUP):
        for k in range(2):
            src = us[k * GROUP + j]
            first = j * tokens + jnp.where(core == k, 0, half * rows)
            for s in range(half):
                u = src[0, s].astype(F32)
                m = norm_rows(u, gain)
                m_s[pl.ds(pl.multiple_of(first + s * rows, rows), rows), :] = m.astype(BF16)

    down = lax.broadcasted_iota(jnp.int32, (256, tokens), 0).astype(F32).astype(BF16)
    for j in range(GROUP):
        pos = pos_ref[j]

        def order(i, carry):
            r = pl.multiple_of(i * 256, 256)
            local = jnp.where((pos >= r) & (pos < r + 256), pos - r, -1).astype(F32).astype(BF16)
            hot = jnp.where(down == local, jnp.ones((), BF16), jnp.zeros((), BF16))
            hot_s[pl.ds(j * slots + r, 256), :] = hot
            m = jnp.dot(hot, m_s[j * tokens:(j + 1) * tokens, :], preferred_element_type=F32).astype(BF16)
            at = pl.ds(j * room + r, 256)
            in_s[at, :] = m
            out_s[at, :] = jnp.zeros((256, d_model), BF16)
            logits = mm_t(m, wr_ref[...])
            ex = jnp.exp(logits - jnp.max(logits, axis=-1, keepdims=True))
            prob_s[at, :] = ex / jnp.sum(ex, axis=-1, keepdims=True)
            return carry

        lax.fori_loop(0, slots // 256, order, 0)
    for pull, push in zip(pulls, pushes):
        pull.wait()
        push.start()

    def feed(e, slot, r, size):
        m = in_s[pl.ds(r, size), :]
        gate = jnp.dot(m, wg[slot], preferred_element_type=F32)
        up = jnp.dot(m, wu[slot], preferred_element_type=F32)
        q = (silu(gate) * up).astype(BF16)
        lane = lax.broadcasted_iota(jnp.int32, (size, experts), 1)
        prob = jnp.sum(jnp.where(lane == e, prob_s[pl.ds(r, size), :], 0.0), axis=-1, keepdims=True)
        out_s[pl.ds(r, size), :] = (prob * jnp.dot(q, wd[slot], preferred_element_type=F32)).astype(BF16)

    def expert(i, carry):
        e = tab_ref[0, 16 * GROUP, i]
        slot = lax.rem(i, RING)
        fetch(i + RING - 1)
        for cp in copies(i):
            cp.wait()

        def part(j, c1):
            start = tab_ref[0, 16 * j + e, 0] + j * room
            count = tab_ref[0, 16 * j + e, 1]
            big = (count + TILE - 1) // (2 * TILE)

            def tile(k, c2):
                feed(e, slot, pl.multiple_of(start + k * (2 * TILE), ROW_ALIGN), 2 * TILE)
                return c2

            lax.fori_loop(0, big, tile, 0)

            @pl.when(count > big * (2 * TILE))
            def _():
                feed(e, slot, pl.multiple_of(start + big * (2 * TILE), ROW_ALIGN), TILE)

            return c1

        return lax.fori_loop(0, GROUP, part, carry)

    lax.fori_loop(0, active, expert, 0)

    def restore(j, k, dst):
        first = jnp.where(core == k, 0, half * rows)
        for s in range(half):
            hot = hot_s[j * slots:(j + 1) * slots, pl.ds(pl.multiple_of(first + s * rows, rows), rows)]
            got = lax.dot_general(hot, out_s[j * room:j * room + slots, :], (((0,), (0,)), ((), ())), preferred_element_type=F32)
            dst[s] = got.astype(BF16)

    for j in range(GROUP):
        for k in range(2):
            restore(j, k, outs[k * GROUP + j])
    for cp in pushes:
        cp.wait()


def solution(mesh):
    act_spec = P(None, "dp", None)
    state_spec = P("dp", "tp", None)
    in_specs = (act_spec, state_spec, state_spec, act_spec, P(None), P(None, None, "tp"), P("tp", None), P("tp"), P("tp", None), P(None), P(None), P(None), P(None, "tp"), P("tp"), P("tp", None), P("tp"), P("tp", None), P(None), P(None, None), P(None, None, "tp"), P(None, None, "tp"), P(None, "tp", None))
    out_specs = (act_spec, state_spec, state_spec)
    across = [(0, 2), (2, 0), (1, 3), (3, 1)]
    beside = [(0, 1), (1, 0), (2, 3), (3, 2)]

    def layer_steps(x_steps, conv_state, ssm_state, expert_ids, g_in, w_in, conv_w, conv_b, w_xp, g_dt, g_b, g_c, w_dt, b_dt, a_log, d_skip, w_out, g_ff, w_router, w_gate, w_up, w_down):
        steps, batch, d_model = x_steps.shape
        inner = w_in.shape[2]
        rank = w_dt.shape[0]
        state = a_log.shape[1]
        experts, _, ffn = w_gate.shape
        width = rank + 2 * state
        half = steps // 2
        rows = batch // CHUNKS
        tokens = steps * rows
        slots = tokens + experts * ROW_ALIGN
        core = lax.rem(lax.axis_index("tp"), 2)

        conv_t = jnp.transpose(conv_state, (2, 0, 1))
        h_rows = jnp.transpose(ssm_state, (0, 2, 1)).reshape(batch * state, inner)
        alog_t = a_log.T

        ids = jnp.transpose(expert_ids, (0, 2, 1))
        pos, table = pl.pallas_call(
            routes_kernel,
            out_shape=(jax.ShapeDtypeStruct((CHUNKS, 1, tokens), jnp.int32), jax.ShapeDtypeStruct((CHUNKS // GROUP, 16 * GROUP + 8, 128), jnp.int32)),
            compiler_params=params(),
            name="routes",
        )(ids)

        vmem = pl.BlockSpec(memory_space=pltpu.VMEM)
        piece = (half, rows, d_model)
        u_first, u_second, *chips, conv_mid, h_mid = pl.pallas_call(
            mamba_kernel,
            in_specs=[HBM, HBM, HBM] + [vmem] * 13,
            out_specs=[HBM] * 6,
            out_shape=[
                jax.ShapeDtypeStruct((WHOLE,) + piece, BF16),
                jax.ShapeDtypeStruct((WHOLE,) + piece, BF16),
                jax.ShapeDtypeStruct(piece, BF16),
                jax.ShapeDtypeStruct(piece, BF16),
                jax.ShapeDtypeStruct((3, batch, inner), BF16),
                jax.ShapeDtypeStruct((batch * state, inner), F32),
            ],
            scratch_shapes=[
                pltpu.VMEM((steps, batch, d_model), BF16),
                pltpu.VMEM((3, batch, inner), BF16),
                pltpu.VMEM((3, batch, inner), BF16),
                pltpu.VMEM((inner // 128, batch * state, 128), F32),
                pltpu.VMEM((steps, batch, inner), BF16),
                pltpu.VMEM((steps, batch, inner), BF16),
                pltpu.VMEM((7, CHUNKS, rows, 2 * width), F32),
                pltpu.VMEM((5, CHUNKS) + piece, BF16),
                pltpu.VMEM((2, CHUNKS) + piece, BF16),
                pltpu.VMEM((d_model, 2 * inner), BF16),
                pltpu.VMEM((1, steps * width), F32),
                pltpu.VMEM((steps * width, steps * inner), BF16),
                pltpu.VMEM((steps * width, steps * width), BF16),
                pltpu.VMEM((steps, 2 * state, 8, 128), F32),
                pltpu.VMEM((steps, 2 * state, 8, 128), F32),
                pltpu.VMEM((state, inner), F32),
                pltpu.VMEM((steps, 128, 128), F32),
                pltpu.VMEM((steps, 128, inner), F32),
                pltpu.VMEM((steps, 128, inner), F32),
                pltpu.VMEM((steps, 128, inner), F32),
                pltpu.SemaphoreType.DMA((2, CHUNKS)),
                pltpu.SemaphoreType.DMA((inner // 128, CHUNKS)),
                pltpu.SemaphoreType.DMA((3, CHUNKS)),
                pltpu.SemaphoreType.DMA((inner // 128, CHUNKS)),
                pltpu.SemaphoreType.DMA((3, CHUNKS)),
                pltpu.SemaphoreType.DMA((3, CHUNKS)),
                pltpu.SemaphoreType.DMA((3, CHUNKS)),
                pltpu.SemaphoreType.DMA((3, CHUNKS)),
            ],
            compiler_params=params(collective_id=0, has_side_effects=True),
            cost_estimate=pl.CostEstimate(flops=int(8e9), bytes_accessed=int(45e6), transcendentals=0),
            name="mamba",
        )(x_steps, conv_t, h_rows, g_in, w_in, conv_w.T, conv_b, w_xp.T, g_dt, g_b, g_c, w_dt, b_dt, alog_t, d_skip, w_out)

        calls = CHUNKS // GROUP
        room = slots + 2 * TILE

        def run_moe(g, u_args, u_specs, states):
            extra = [] if states is None else list(states)
            return pl.pallas_call(
                functools.partial(moe_kernel, g),
                grid=(1,),
                in_specs=[pl.BlockSpec((1, 16 * GROUP + 8, 128), lambda i: (g, 0, 0), memory_space=pltpu.SMEM), pl.BlockSpec((GROUP, 1, tokens), lambda i: (g, 0, 0))] + u_specs + [vmem, vmem] + [HBM] * (5 + len(extra)),
                out_specs=[vmem] * (2 * GROUP) + [HBM, HBM],
                out_shape=[jax.ShapeDtypeStruct(piece, BF16)] * (2 * GROUP) + [jax.ShapeDtypeStruct(h_mid.shape, F32), jax.ShapeDtypeStruct(conv_mid.shape, BF16)],
                scratch_shapes=[
                    pltpu.VMEM((RING, d_model, ffn), BF16),
                    pltpu.VMEM((RING, d_model, ffn), BF16),
                    pltpu.VMEM((RING, ffn, d_model), BF16),
                    pltpu.SemaphoreType.DMA((3, RING)),
                    pltpu.VMEM((GROUP * tokens, d_model), BF16),
                    pltpu.VMEM((GROUP * slots, tokens), BF16),
                    pltpu.VMEM((GROUP * room, d_model), BF16),
                    pltpu.VMEM((GROUP * room, d_model), BF16),
                    pltpu.VMEM((GROUP * room, experts), F32),
                    pltpu.VMEM((batch * state // calls, inner), F32),
                    pltpu.VMEM((3, batch // calls, inner), BF16),
                    pltpu.SemaphoreType.DMA((4,)),
                ],
                input_output_aliases={9 + 2 * GROUP: 2 * GROUP, 10 + 2 * GROUP: 2 * GROUP + 1} if extra else {},
                compiler_params=params(),
                cost_estimate=pl.CostEstimate(flops=int(6e9), bytes_accessed=int(40e6), transcendentals=0),
            )(table, pos, *u_args, g_ff, w_router.T, w_gate, w_up, w_down, h_mid, conv_mid, *extra)

        def both(keep, send, dtype):
            got = lax.ppermute(send, "tp", beside)
            chip = (keep.astype(F32) + got.astype(F32)).astype(dtype)
            return chip, lax.ppermute(chip, "tp", across)

        owns = {}
        spot = {}
        for c in range(WHOLE):
            spot[c] = (u_first, u_second, pl.BlockSpec((1,) + piece, lambda i, c=c: (c, 0, 0, 0)))
            owns[c] = lambda c=c: u_first[c]
        for c in range(WHOLE, CHUNKS):
            chip = chips[c - WHOLE]
            far = lax.ppermute(chip, "tp", across)
            x_own = lax.dynamic_slice(x_steps, (half * core, c * rows, 0), (half, rows, d_model))
            u_own = (x_own.astype(F32) + (chip.astype(F32) + far.astype(F32))).astype(BF16)
            u_sib = lax.ppermute(u_own, "tp", beside)
            spot[c] = (u_own[None], u_sib[None], pl.BlockSpec((1,) + piece, lambda i: (0, 0, 0, 0)))
            owns[c] = lambda u_own=u_own: u_own

        y_steps = jnp.zeros((steps, batch, d_model), BF16)
        states = None
        for g in range(calls):
            group = [spot[g * GROUP + j] for j in range(GROUP)]
            got = run_moe(g, [v[0] for v in group] + [v[1] for v in group], [v[2] for v in group] * 2, states)
            states = got[2 * GROUP:]
            for j in range(GROUP):
                c = g * GROUP + j
                chip, far = both(got[j], got[GROUP + j], BF16)
                y_own = (owns[c]().astype(F32) + (chip.astype(F32) + far.astype(F32))).astype(BF16)
                y_sib = lax.ppermute(y_own, "tp", beside)
                y_steps = lax.dynamic_update_slice(y_steps, y_own, (half * core, c * rows, 0))
                y_steps = lax.dynamic_update_slice(y_steps, y_sib, (half * (1 - core), c * rows, 0))
        ssm_out, conv_out = states
        ssm_fin = jnp.transpose(ssm_out.reshape(batch, state, inner), (0, 2, 1))
        return y_steps, jnp.transpose(conv_out, (1, 2, 0)), ssm_fin

    return jax.shard_map(layer_steps, mesh=mesh, in_specs=in_specs, out_specs=out_specs, check_vma=False)
```

profile of v0, /device:TPU:0, one launch (start us, length us, event | category | flops | bytes accessed | tf_op | source)
XLA Modules:
  0.0 213.3 jit_solution(7736867221957993187)
XLA Ops:
  0.6 2.3 %routes.1 = (s32[4,1,1024]{2,1,0:T(1,128)}, s32[2,40,128]{2,1,0:T(8,128)}) custom-call(s32[4,1,1024]{2,1,0:T(1,128)} %bitcast.33), custom_call_target="tpu_custom_call" | custom-call | tf_op jit(solution)/shard_map/routes/pallas_call | solution.py:510
  3.0 72.0 %mamba.1 = (bf16[2,2,256,512]{3,2,1,0:T(8,128)(2,1)}, bf16[2,2,256,512]{3,2,1,0:T(8,128)(2,1)}, bf16[2,256,512]{2,1,0:T(8,128)(2,1)}, bf16[2,256,512]{2,1,0:T(8,...) custom-call(bf16[4,1024,512]{2,1,0:T(8,128)(2,1)} %x_hbm.1, bf16[3,1024,256]{2,1,0:T(8,128)(2,1)} %bitcast.35, ...), custom_call_target="tpu_custom_call" | custom-call | flops 8000000000 | bytes 45000000 | tf_op jit(solution)/shard_map/mamba/pallas_call | solution.py:519
  74.9 0.0 copy-start.10
  74.9 0.0 copy-start.11
  74.9 31.4 %shard_map.229 = (bf16[2,256,512]{2,1,0:T(8,128)(2,1)}, bf16[2,256,512]{2,1,0:T(8,128)(2,1)}, bf16[2,256,512]{2,1,0:T(8,128)(2,1)}, bf16[2,256,512]{2,1,0:T(8,12...) custom-call(s32[2,40,128]{2,1,0:T(8,128)} %get-tuple-element.24.refs_0_, ...), custom_call_target="tpu_custom_call" | custom-call | flops 6000000000 | bytes 40000000 | tf_op jit(solution)/shard_map/pallas_call | solution.py:571
  106.3 0.0 copy-start.9
  106.3 1.2 collective-permute-start
  107.5 0.0 copy-done.10
  107.5 0.0 collective-permute-start.6
  107.5 0.0 copy-done.11
  107.5 2.0 collective-permute-start.7
  109.6 0.0 collective-permute-start.3
  109.6 0.0 collective-permute-done
  109.6 1.2 add_convert_fusion.7
  110.8 0.0 copy-start
  110.8 0.1 collective-permute-start.1
  110.8 11.6 %collective-permute-done.6 = bf16[2,256,512]{2,1,0:T(8,128)(2,1)} collective-permute-done((bf16[2,256,512]{2,1,0:T(8,128)(2,1)S(1)}, bf16[2,256,512]{2,1,0:T(8,128)(2,1)}, u32[]{:S(2)}, u32[]{:S(2)}) %collective-permute-start.6) | collective-permute-done | bytes 524320 | tf_op jit(solution)/shard_map/ppermute | solution.py:608
  122.4 11.2 %collective-permute-done.7 = bf16[2,256,512]{2,1,0:T(8,128)(2,1)} collective-permute-done((bf16[2,256,512]{2,1,0:T(8,128)(2,1)S(1)}, bf16[2,256,512]{2,1,0:T(8,128)(2,1)}, u32[]{:S(2)}, u32[]{:S(2)}) %collective-permute-start.7) | collective-permute-done | bytes 524320 | tf_op jit(solution)/shard_map/ppermute | solution.py:608
  133.7 1.9 add_convert_fusion.4
  135.6 0.0 copy-start.1
  135.6 0.0 copy-start.3
  135.6 0.0 collective-permute-start.8
  135.7 0.5 collective-permute-start.9
  136.2 0.0 collective-permute-done.3
  136.2 0.0 copy-done.9
  136.2 1.2 add_convert_fusion.6
  137.4 0.0 collective-permute-start.4
  137.4 7.4 %collective-permute-done.1 = bf16[2,256,512]{2,1,0:T(8,128)(2,1)S(1)} collective-permute-done((bf16[2,256,512]{2,1,0:T(8,128)(2,1)S(1)}, bf16[2,256,512]{2,1,0:T(8,128)(2,1)S(1)}, u32[]{:S(2)}, u32[]{:S(2)}) %collective-permute-start.1) | collective-permute-done | bytes 524320 | tf_op jit(solution)/shard_map/ppermute | solution.py:599
  144.8 0.3 broadcast_in_dim.15
  145.1 1.0 constant_dynamic-update-slice_fusion.7
  146.2 0.0 collective-permute-start.2
  146.2 0.0 collective-permute-done.8
  146.2 0.0 collective-permute-done.9
  146.2 2.0 copy-done.5
  148.2 0.2 copy-done.6
  148.3 0.6 copy-done.7
  149.0 26.4 %shard_map.230 = (bf16[2,256,512]{2,1,0:T(8,128)(2,1)}, bf16[2,256,512]{2,1,0:T(8,128)(2,1)}, bf16[2,256,512]{2,1,0:T(8,128)(2,1)}, bf16[2,256,512]{2,1,0:T(8,12...) custom-call(s32[2,40,128]{2,1,0:T(8,128)} %get-tuple-element.24.refs, ...), custom_call_target="tpu_custom_call", output_to_operand_aliasing={{4}: (13, {}), {5}: (14, {})} | custom-call | flops 6000000000 | bytes 40000000 | tf_op jit(solution)/shard_map/pallas_call | solution.py:571
  175.4 0.0 collective-permute-start.10
  175.5 0.0 copy-start.12
  175.5 0.0 collective-permute-done.2
  175.5 0.8 constant_dynamic-update-slice_fusion.6
  176.3 0.0 collective-permute-done.4
  176.3 2.1 constant_dynamic-update-slice_fusion.5
  178.4 0.5 collective-permute-start.5
  178.9 0.0 collective-permute-done.10
  178.9 1.2 add_convert_fusion.3
  180.1 0.0 collective-permute-start.11
  180.1 0.0 copy-done.12
  180.1 0.1 collective-permute-start.13
  180.3 0.2 collective-permute-done.5
  180.4 0.8 constant_dynamic-update-slice_fusion.4
  181.3 12.8 %collective-permute-done.11 = bf16[2,256,512]{2,1,0:T(8,128)(2,1)S(1)} collective-permute-done((bf16[2,256,512]{2,1,0:T(8,128)(2,1)S(1)}, bf16[2,256,512]{2,1,0:T(8,128)(2,1)S(1)}, u32[]{:S(2)}, u32[]{:S(2)}) %collective-permute-start.11) | collective-permute-done | bytes 524320 | tf_op jit(solution)/shard_map/ppermute | solution.py:599
  194.0 1.0 constant_dynamic-update-slice_fusion.3
  195.1 0.0 collective-permute-start.12
  195.1 0.0 collective-permute-done.13
  195.1 0.1 add_convert_fusion.1
  195.2 0.3 collective-permute-start.14
  195.5 1.4 collective-permute-done.12
  197.0 0.8 constant_dynamic-update-slice_fusion.2
  197.8 11.8 %collective-permute-done.14 = bf16[2,256,512]{2,1,0:T(8,128)(2,1)S(1)} collective-permute-done((bf16[2,256,512]{2,1,0:T(8,128)(2,1)S(1)}, bf16[2,256,512]{2,1,0:T(8,128)(2,1)S(1)}, u32[]{:S(2)}, u32[]{:S(2)}) %collective-permute-start.14) | collective-permute-done | bytes 524320 | tf_op jit(solution)/shard_map/ppermute | solution.py:599
  209.6 1.0 constant_dynamic-update-slice_fusion.1
  210.6 0.0 collective-permute-start.15
  210.6 1.9 collective-permute-done.15
  212.5 0.8 constant_dynamic-update-slice_fusion
  (12 shorter events, 0.0 us)
Async XLA Ops:
  74.9 32.6 %copy-start.10 = (bf16[2,256,512]{2,1,0:T(8,128)(2,1)S(1)}, bf16[2,256,512]{2,1,0:T(8,128)(2,1)}, u32[]{:S(2)}) copy-start(bf16[2,256,512]{2,1,0:T(8,128)(2,1)} %get-tuple-element.33) | copy-start | bytes 1572868
  74.9 32.6 %copy-start.11 = (bf16[2,256,512]{2,1,0:T(8,128)(2,1)S(1)}, bf16[2,256,512]{2,1,0:T(8,128)(2,1)}, u32[]{:S(2)}) copy-start(bf16[2,256,512]{2,1,0:T(8,128)(2,1)} %get-tuple-element.34) | copy-start | bytes 1572868
  106.3 29.9 %copy-start.9 = (bf16[2,256,512]{2,1,0:T(8,128)(2,1)S(1)}, bf16[2,256,512]{2,1,0:T(8,128)(2,1)}, u32[]{:S(2)}) copy-start(bf16[2,256,512]{2,1,0:T(8,128)(2,1)} %get-tuple-element.31) | copy-start | bytes 1572868
  106.3 3.2 %collective-permute-start = (bf16[2,256,512]{2,1,0:T(8,128)(2,1)}, bf16[2,256,512]{2,1,0:T(8,128)(2,1)S(1)}, u32[]{:S(2)}, u32[]{:S(2)}) collective-permute-start(bf16[2,256,512]{2,1,0:T(8,128)(2,1)} %get-tuple-element.30), channel_id=1, source_target_pairs={{0,1},{1,0},{2,3},{3,2},{4,5},{5,4},{6,7},{7,6},{8,9},{9,8},{10,11... | collective-permute-start | bytes 1572872 | tf_op jit(solution)/shard_map/ppermute | solution.py:597
  107.5 14.9 %collective-permute-start.6 = (bf16[2,256,512]{2,1,0:T(8,128)(2,1)S(1)}, bf16[2,256,512]{2,1,0:T(8,128)(2,1)}, u32[]{:S(2)}, u32[]{:S(2)}) collective-permute-start(bf16[2,256,512]{2,1,0:T(8,128)(2,1)S(1)} %copy-done.10), channel_id=1, source_target_pairs={{0,2},{2,0},{1,3},{3,1},{4,6},{6,4},{5,7},{7,5},{8,10},{10,8},{9,1... | collective-permute-start | bytes 1572872 | tf_op jit(solution)/shard_map/ppermute | solution.py:608
  107.5 26.1 %collective-permute-start.7 = (bf16[2,256,512]{2,1,0:T(8,128)(2,1)S(1)}, bf16[2,256,512]{2,1,0:T(8,128)(2,1)}, u32[]{:S(2)}, u32[]{:S(2)}) collective-permute-start(bf16[2,256,512]{2,1,0:T(8,128)(2,1)S(1)} %copy-done.11), channel_id=1, source_target_pairs={{0,2},{2,0},{1,3},{3,1},{4,6},{6,4},{5,7},{7,5},{8,10},{10,8},{9,1... | collective-permute-start | bytes 1572872 | tf_op jit(solution)/shard_map/ppermute | solution.py:608
  109.6 26.6 %collective-permute-start.3 = (bf16[2,256,512]{2,1,0:T(8,128)(2,1)}, bf16[2,256,512]{2,1,0:T(8,128)(2,1)}, u32[]{:S(2)}, u32[]{:S(2)}) collective-permute-start(bf16[2,256,512]{2,1,0:T(8,128)(2,1)} %get-tuple-element.32), channel_id=1, source_target_pairs={{0,1},{1,0},{2,3},{3,2},{4,5},{5,4},{6,7},{7,6},{8,9},{9,8},{10,11... | collective-permute-start | bytes 1572872 | tf_op jit(solution)/shard_map/ppermute | solution.py:597
  110.8 34.4 %copy-start = (bf16[2,2,256,512]{3,2,1,0:T(8,128)(2,1)S(1)}, bf16[2,2,256,512]{3,2,1,0:T(8,128)(2,1)}, u32[]{:S(2)}) copy-start(bf16[2,2,256,512]{3,2,1,0:T(8,128)(2,1)} %get-tuple-element.23.refs_2_.refs_3_) | copy-start | bytes 3145732
  110.8 34.0 %collective-permute-start.1 = (bf16[2,256,512]{2,1,0:T(8,128)(2,1)S(1)}, bf16[2,256,512]{2,1,0:T(8,128)(2,1)S(1)}, u32[]{:S(2)}, u32[]{:S(2)}) collective-permute-start(bf16[2,256,512]{2,1,0:T(8,128)(2,1)S(1)} %add_convert_fusion.7), channel_id=1, source_target_pairs={{0,2},{2,0},{1,3},{3,1},{4,6},{6,4},{5,7},{7,5},{8,10},{10,8},{9,1... | collective-permute-start | bytes 1572872 | tf_op jit(solution)/shard_map/ppermute | solution.py:599
  135.6 10.5 %copy-start.1 = (bf16[2,256,512]{2,1,0:T(8,128)(2,1)}, bf16[2,256,512]{2,1,0:T(8,128)(2,1)S(1)}, u32[]{:S(2)}) copy-start(bf16[2,256,512]{2,1,0:T(8,128)(2,1)S(1)} %get-tuple-element.51) | copy-start | bytes 1572868
  135.6 10.5 %copy-start.3 = (bf16[2,256,512]{2,1,0:T(8,128)(2,1)}, bf16[2,256,512]{2,1,0:T(8,128)(2,1)S(1)}, u32[]{:S(2)}) copy-start(bf16[2,256,512]{2,1,0:T(8,128)(2,1)S(1)} %get-tuple-element.52) | copy-start | bytes 1572868
  135.6 10.5 %collective-permute-start.8 = (bf16[2,256,512]{2,1,0:T(8,128)(2,1)S(1)}, bf16[2,256,512]{2,1,0:T(8,128)(2,1)S(1)}, u32[]{:S(2)}, u32[]{:S(2)}) collective-permute-start(bf16[2,256,512]{2,1,0:T(8,128)(2,1)S(1)} %get-tuple-element.52), channel_id=1, source_target_pairs={{0,1},{1,0},{2,3},{3,2},{4,5},{5,4},{6,7},{7,6},{8,9},{9,8},{10,11... | collective-permute-start | bytes 1572872 | tf_op jit(solution)/shard_map/ppermute | solution.py:611
  135.7 10.5 %collective-permute-start.9 = (bf16[2,256,512]{2,1,0:T(8,128)(2,1)S(1)}, bf16[2,256,512]{2,1,0:T(8,128)(2,1)S(1)}, u32[]{:S(2)}, u32[]{:S(2)}) collective-permute-start(bf16[2,256,512]{2,1,0:T(8,128)(2,1)S(1)} %get-tuple-element.51), channel_id=1, source_target_pairs={{0,1},{1,0},{2,3},{3,2},{4,5},{5,4},{6,7},{7,6},{8,9},{9,8},{10,11... | collective-permute-start | bytes 1572872 | tf_op jit(solution)/shard_map/ppermute | solution.py:611
  137.4 38.9 %collective-permute-start.4 = (bf16[2,256,512]{2,1,0:T(8,128)(2,1)S(1)}, bf16[2,256,512]{2,1,0:T(8,128)(2,1)}, u32[]{:S(2)}, u32[]{:S(2)}) collective-permute-start(bf16[2,256,512]{2,1,0:T(8,128)(2,1)S(1)} %add_convert_fusion.6), channel_id=1, source_target_pairs={{0,2},{2,0},{1,3},{3,1},{4,6},{6,4},{5,7},{7,5},{8,10},{10,8},{9,1... | collective-permute-start | bytes 1572872 | tf_op jit(solution)/shard_map/ppermute | solution.py:599
  146.2 2.0 copy-start.5
  146.2 29.3 %collective-permute-start.2 = (bf16[2,256,512]{2,1,0:T(8,128)(2,1)}, bf16[2,256,512]{2,1,0:T(8,128)(2,1)S(1)}, u32[]{:S(2)}, u32[]{:S(2)}) collective-permute-start(bf16[2,256,512]{2,1,0:T(8,128)(2,1)} %get-tuple-element.50), channel_id=1, source_target_pairs={{0,1},{1,0},{2,3},{3,2},{4,5},{5,4},{6,7},{7,6},{8,9},{9,8},{10,11... | collective-permute-start | bytes 1572872 | tf_op jit(solution)/shard_map/ppermute | solution.py:625
  146.2 2.2 %copy-start.6 = (bf16[2,256,512]{2,1,0:T(8,128)(2,1)}, bf16[2,256,512]{2,1,0:T(8,128)(2,1)S(1)}, u32[]{:S(2)}) copy-start(bf16[2,256,512]{2,1,0:T(8,128)(2,1)S(1)} %collective-permute-done.8) | copy-start | bytes 1572868
  148.2 0.8 copy-start.7
  175.4 18.6 %copy-start.4 = (bf16[2,256,512]{2,1,0:T(8,128)(2,1)S(1)}, bf16[2,256,512]{2,1,0:T(8,128)(2,1)}, u32[]{:S(2)}) copy-start(bf16[2,256,512]{2,1,0:T(8,128)(2,1)} %copy-done.3) | copy-start | bytes 1572868
  175.4 3.5 %collective-permute-start.10 = (bf16[2,256,512]{2,1,0:T(8,128)(2,1)}, bf16[2,256,512]{2,1,0:T(8,128)(2,1)S(1)}, u32[]{:S(2)}, u32[]{:S(2)}) collective-permute-start(bf16[2,256,512]{2,1,0:T(8,128)(2,1)} %get-tuple-element.38), channel_id=1, source_target_pairs={{0,1},{1,0},{2,3},{3,2},{4,5},{5,4},{6,7},{7,6},{8,9},{9,8},{10,11... | collective-permute-start | bytes 1572872 | tf_op jit(solution)/shard_map/ppermute | solution.py:597
  175.5 4.7 %copy-start.12 = (bf16[2,256,512]{2,1,0:T(8,128)(2,1)S(1)}, bf16[2,256,512]{2,1,0:T(8,128)(2,1)}, u32[]{:S(2)}) copy-start(bf16[2,256,512]{2,1,0:T(8,128)(2,1)} %get-tuple-element.40) | copy-start | bytes 1572868
  176.3 18.8 %copy-start.8 = (bf16[2,256,512]{2,1,0:T(8,128)(2,1)S(1)}, bf16[2,256,512]{2,1,0:T(8,128)(2,1)}, u32[]{:S(2)}) copy-start(bf16[2,256,512]{2,1,0:T(8,128)(2,1)} %get-tuple-element.39) | copy-start | bytes 1572868
  178.4 31.1 %copy-start.2 = (bf16[2,256,512]{2,1,0:T(8,128)(2,1)S(1)}, bf16[2,256,512]{2,1,0:T(8,128)(2,1)}, u32[]{:S(2)}) copy-start(bf16[2,256,512]{2,1,0:T(8,128)(2,1)} %copy-done.1) | copy-start | bytes 1572868
  178.4 2.0 collective-permute-start.5
  180.1 14.0 %collective-permute-start.11 = (bf16[2,256,512]{2,1,0:T(8,128)(2,1)S(1)}, bf16[2,256,512]{2,1,0:T(8,128)(2,1)S(1)}, u32[]{:S(2)}, u32[]{:S(2)}) collective-permute-start(bf16[2,256,512]{2,1,0:T(8,128)(2,1)S(1)} %add_convert_fusion.3), channel_id=1, source_target_pairs={{0,2},{2,0},{1,3},{3,1},{4,6},{6,4},{5,7},{7,5},{8,10},{10,8},{9,1... | collective-permute-start | bytes 1572872 | tf_op jit(solution)/shard_map/ppermute | solution.py:599
  180.1 14.9 %collective-permute-start.13 = (bf16[2,256,512]{2,1,0:T(8,128)(2,1)S(1)}, bf16[2,256,512]{2,1,0:T(8,128)(2,1)S(1)}, u32[]{:S(2)}, u32[]{:S(2)}) collective-permute-start(bf16[2,256,512]{2,1,0:T(8,128)(2,1)S(1)} %copy-done.12), channel_id=1, source_target_pairs={{0,1},{1,0},{2,3},{3,2},{4,5},{5,4},{6,7},{7,6},{8,9},{9,8},{10,11... | collective-permute-start | bytes 1572872 | tf_op jit(solution)/shard_map/ppermute | solution.py:597
  195.1 1.9 collective-permute-start.12
  195.2 14.4 %collective-permute-start.14 = (bf16[2,256,512]{2,1,0:T(8,128)(2,1)S(1)}, bf16[2,256,512]{2,1,0:T(8,128)(2,1)S(1)}, u32[]{:S(2)}, u32[]{:S(2)}) collective-permute-start(bf16[2,256,512]{2,1,0:T(8,128)(2,1)S(1)} %add_convert_fusion.1), channel_id=1, source_target_pairs={{0,2},{2,0},{1,3},{3,1},{4,6},{6,4},{5,7},{7,5},{8,10},{10,8},{9,1... | collective-permute-start | bytes 1572872 | tf_op jit(solution)/shard_map/ppermute | solution.py:599
  210.6 1.9 collective-permute-start.15
where the time goes:
time: 215 us; the launch traced here: 213 us
  Pallas kernels  132 us (61%)
  waiting for transfers between devices  58.3 us (27%)
  other arithmetic  10.7 us (5%)
  local copies, waits for them, and re-layouts  6.45 us (3%)
  starting transfers between devices  4.89 us (2%)
    pallas_call x1, Pallas kernels, layer_steps(): pl.pallas_call(mamba_kernel, in_specs=[HBM, HBM, HBM] + [vmem] * 13, out_...  72 us
    pallas_call x2, Pallas kernels, run_moe(): pl.pallas_call(functools.partial(moe_kernel, g), grid=(1,), in_specs=[pl....  57.8 us
    ppermute x4, waiting for transfers between devices, both(): return (chip, lax.ppermute(chip, 'tp', across))  31.9 us
    ppermute x2, waiting for transfers between devices, layer_steps(): far = lax.ppermute(chip, 'tp', across)  22.8 us
    dynamic_update_slice x4, other arithmetic, layer_steps(): lax.dynamic_update_slice(y_steps, y_own, (half * core, c * rows, 0))  5.14 us
  transfers between devices with their start and end apart: 16, of which 8 were waited for; matrix products, arithmetic and copies ran while one was open for 6% of the time, Pallas kernels for 12%

commit v1 on v0

--- a/solution.py
+++ b/solution.py
@@ -368,8 +368,10 @@
     tab_ref, pos_ref = refs[:2]
     us = refs[2:2 + 2 * GROUP]
     gff_ref, wr_ref, wg_ref, wu_ref, wd_ref, h_hbm, cv_hbm = refs[2 + 2 * GROUP:9 + 2 * GROUP]
-    outs = refs[-14 - 2 * GROUP:-14]
-    ho_hbm, co_hbm, wg, wu, wd, sems, m_s, hot_s, in_s, out_s, prob_s, h_s, cv_s, st_sem = refs[-14:]
+    refs = refs[9 + 2 * GROUP + (2 if g else 0):]
+    outs = refs[:2 * GROUP]
+    ho_hbm, co_hbm = refs[2 * GROUP:2 * GROUP + 2]
+    wg, wu, wd, sems, m_s, hot_s, in_s, out_s, prob_s, h_s, cv_s, st_sem = refs[-12:]
     _, half, rows, d_model = us[0].shape
     experts = wr_ref.shape[0]
     tokens = 2 * half * rows
@@ -572,8 +574,8 @@
                 functools.partial(moe_kernel, g),
                 grid=(1,),
                 in_specs=[pl.BlockSpec((1, 16 * GROUP + 8, 128), lambda i: (g, 0, 0), memory_space=pltpu.SMEM), pl.BlockSpec((GROUP, 1, tokens), lambda i: (g, 0, 0))] + u_specs + [vmem, vmem] + [HBM] * (5 + len(extra)),
-                out_specs=[vmem] * (2 * GROUP) + [HBM, HBM],
-                out_shape=[jax.ShapeDtypeStruct(piece, BF16)] * (2 * GROUP) + [jax.ShapeDtypeStruct(h_mid.shape, F32), jax.ShapeDtypeStruct(conv_mid.shape, BF16)],
+                out_specs=[vmem] * (2 * GROUP) + [HBM, HBM] + ([] if extra else [HBM]),
+                out_shape=[jax.ShapeDtypeStruct(piece, BF16)] * (2 * GROUP) + [jax.ShapeDtypeStruct(h_mid.shape, F32), jax.ShapeDtypeStruct(conv_mid.shape, BF16)] + ([] if extra else [jax.ShapeDtypeStruct(x_steps.shape, BF16)]),
                 scratch_shapes=[
                     pltpu.VMEM((RING, d_model, ffn), BF16),
                     pltpu.VMEM((RING, d_model, ffn), BF16),
@@ -612,12 +614,13 @@
             spot[c] = (u_own[None], u_sib[None], pl.BlockSpec((1,) + piece, lambda i: (0, 0, 0, 0)))
             owns[c] = lambda u_own=u_own: u_own
 
-        y_steps = jnp.zeros((steps, batch, d_model), BF16)
         states = None
         for g in range(calls):
             group = [spot[g * GROUP + j] for j in range(GROUP)]
             got = run_moe(g, [v[0] for v in group] + [v[1] for v in group], [v[2] for v in group] * 2, states)
-            states = got[2 * GROUP:]
+            states = got[2 * GROUP:2 * GROUP + 2]
+            if g == 0:
+                y_steps = got[-1]
             for j in range(GROUP):
                 c = g * GROUP + j
                 chip, far = both(got[j], got[GROUP + j], BF16)

time: 215 us -> 214 us (level)
  local copies, waits for them, and re-layouts: 6.45 us -> 4.3 us
  transfers between devices with their start and end apart: 16 -> 16, of which waited for: 8 -> 8; matrix products, arithmetic and copies ran while one was open for 6% -> 5% of each run, Pallas kernels for 12% -> 12%
where the time goes in v1:
time: 214 us; the launch traced here: 212 us
  Pallas kernels  132 us (62%)
  waiting for transfers between devices  59.2 us (28%)
  other arithmetic  10.1 us (5%)
  starting transfers between devices  5.29 us (2%)
  local copies, waits for them, and re-layouts  4.3 us (2%)
    pallas_call x1, Pallas kernels, layer_steps(): pl.pallas_call(mamba_kernel, in_specs=[HBM, HBM, HBM] + [vmem] * 13, out_...  72 us
    pallas_call x2, Pallas kernels, run_moe(): pl.pallas_call(functools.partial(moe_kernel, g), grid=(1,), in_specs=[pl....  57.8 us
    ppermute x4, waiting for transfers between devices, both(): return (chip, lax.ppermute(chip, 'tp', across))  33 us
    ppermute x2, waiting for transfers between devices, layer_steps(): far = lax.ppermute(chip, 'tp', across)  22.7 us
    dynamic_update_slice x4, other arithmetic, layer_steps(): lax.dynamic_update_slice(y_steps, y_own, (half * core, c * rows, 0))  5.31 us
  transfers between devices with their start and end apart: 16, of which 8 were waited for; matrix products, arithmetic and copies ran while one was open for 5% of the time, Pallas kernels for 12%

profile of v1, /device:TPU:0, one launch (start us, length us, event | category | flops | bytes accessed | tf_op | source)
XLA Modules:
  0.0 211.8 jit_solution(17652429361161958575)
XLA Ops:
  0.6 2.3 %routes.1 = (s32[4,1,1024]{2,1,0:T(1,128)}, s32[2,40,128]{2,1,0:T(8,128)}) custom-call(s32[4,1,1024]{2,1,0:T(1,128)} %bitcast.33), custom_call_target="tpu_custom_call" | custom-call | tf_op jit(solution)/shard_map/routes/pallas_call | solution.py:512
  3.0 72.0 %mamba.1 = (bf16[2,2,256,512]{3,2,1,0:T(8,128)(2,1)}, bf16[2,2,256,512]{3,2,1,0:T(8,128)(2,1)}, bf16[2,256,512]{2,1,0:T(8,128)(2,1)}, bf16[2,256,512]{2,1,0:T(8,...) custom-call(bf16[4,1024,512]{2,1,0:T(8,128)(2,1)} %x_hbm.1, bf16[3,1024,256]{2,1,0:T(8,128)(2,1)} %bitcast.35, ...), custom_call_target="tpu_custom_call" | custom-call | flops 8000000000 | bytes 45000000 | tf_op jit(solution)/shard_map/mamba/pallas_call | solution.py:521
  74.9 0.0 copy-start.9
  74.9 0.0 copy-start.10
  74.9 31.4 %shard_map.229 = (bf16[2,256,512]{2,1,0:T(8,128)(2,1)}, bf16[2,256,512]{2,1,0:T(8,128)(2,1)}, bf16[2,256,512]{2,1,0:T(8,128)(2,1)}, bf16[2,256,512]{2,1,0:T(8,12...) custom-call(s32[2,40,128]{2,1,0:T(8,128)} %get-tuple-element.24.refs_0_, ...), custom_call_target="tpu_custom_call" | custom-call | flops 6000000000 | bytes 40000000 | tf_op jit(solution)/shard_map/pallas_call | solution.py:573
  106.4 0.0 copy-start.8
  106.4 0.0 copy-start
  106.4 1.2 collective-permute-start
  107.6 0.0 copy-done.9
  107.6 0.0 collective-permute-start.6
  107.6 0.0 copy-done.10
  107.6 2.0 collective-permute-start.7
  109.6 0.0 collective-permute-start.3
  109.6 0.0 collective-permute-done
  109.6 1.3 add_convert_fusion.7
  110.9 0.1 collective-permute-start.1
  111.0 11.4 %collective-permute-done.6 = bf16[2,256,512]{2,1,0:T(8,128)(2,1)} collective-permute-done((bf16[2,256,512]{2,1,0:T(8,128)(2,1)S(1)}, bf16[2,256,512]{2,1,0:T(8,128)(2,1)}, u32[]{:S(2)}, u32[]{:S(2)}) %collective-permute-start.6) | collective-permute-done | bytes 524320 | tf_op jit(solution)/shard_map/ppermute | solution.py:610
  122.5 11.2 %collective-permute-done.7 = bf16[2,256,512]{2,1,0:T(8,128)(2,1)} collective-permute-done((bf16[2,256,512]{2,1,0:T(8,128)(2,1)S(1)}, bf16[2,256,512]{2,1,0:T(8,128)(2,1)}, u32[]{:S(2)}, u32[]{:S(2)}) %collective-permute-start.7) | collective-permute-done | bytes 524320 | tf_op jit(solution)/shard_map/ppermute | solution.py:610
  133.7 1.9 add_convert_fusion.4
  135.6 0.0 copy-start.1
  135.7 0.0 copy-start.3
  135.7 0.0 collective-permute-start.9
  135.7 0.5 collective-permute-start.8
  136.2 0.0 collective-permute-done.3
  136.2 0.0 copy-done.8
  136.2 0.1 add_convert_fusion.6
  136.4 0.0 collective-permute-start.4
  136.4 8.4 %collective-permute-done.1 = bf16[2,256,512]{2,1,0:T(8,128)(2,1)S(1)} collective-permute-done((bf16[2,256,512]{2,1,0:T(8,128)(2,1)S(1)}, bf16[2,256,512]{2,1,0:T(8,128)(2,1)S(1)}, u32[]{:S(2)}, u32[]{:S(2)}) %collective-permute-start.1) | collective-permute-done | bytes 524320 | tf_op jit(solution)/shard_map/ppermute | solution.py:601
  144.8 0.0 copy-done
  144.8 1.2 constant_dynamic-update-slice_fusion.7
  146.0 0.0 collective-permute-start.2
  146.0 0.0 collective-permute-done.9
  146.0 0.0 collective-permute-done.8
  146.1 0.8 copy-done.5
  146.8 0.2 copy-done.6
  147.0 26.4 %shard_map.230 = (bf16[2,256,512]{2,1,0:T(8,128)(2,1)}, bf16[2,256,512]{2,1,0:T(8,128)(2,1)}, bf16[2,256,512]{2,1,0:T(8,128)(2,1)}, bf16[2,256,512]{2,1,0:T(8,12...) custom-call(s32[2,40,128]{2,1,0:T(8,128)} %get-tuple-element.24.refs, ...), custom_call_target="tpu_custom_call", output_to_operand_aliasing={{4}: (13, {}), {5}: (14, {})} | custom-call | flops 6000000000 | bytes 40000000 | tf_op jit(solution)/shard_map/pallas_call | solution.py:573
  173.4 0.0 copy-start.4
  173.4 0.5 collective-permute-start.10
  174.0 0.0 collective-permute-done.2
  174.0 0.8 constant_dynamic-update-slice_fusion.6
  174.8 0.0 collective-permute-done.4
  174.8 2.1 constant_dynamic-update-slice_fusion.5
  176.9 0.0 collective-permute-start.5
  177.0 0.0 collective-permute-done.10
  177.0 1.2 add_convert_fusion.3
  178.2 0.0 collective-permute-start.11
  178.3 0.5 collective-permute-start.13
  178.7 0.1 collective-permute-done.5
  178.8 0.8 constant_dynamic-update-slice_fusion.4
  179.7 12.8 %collective-permute-done.11 = bf16[2,256,512]{2,1,0:T(8,128)(2,1)S(1)} collective-permute-done((bf16[2,256,512]{2,1,0:T(8,128)(2,1)S(1)}, bf16[2,256,512]{2,1,0:T(8,128)(2,1)S(1)}, u32[]{:S(2)}, u32[]{:S(2)}) %collective-permute-start.11) | collective-permute-done | bytes 524320 | tf_op jit(solution)/shard_map/ppermute | solution.py:601
  192.5 0.0 copy-done.4
  192.5 1.0 constant_dynamic-update-slice_fusion.3
  193.5 0.0 collective-permute-start.12
  193.5 0.0 collective-permute-done.13
  193.5 0.1 add_convert_fusion.1
  193.7 0.3 collective-permute-start.14
  194.0 1.4 collective-permute-done.12
  195.4 0.8 constant_dynamic-update-slice_fusion.2
  196.2 11.8 %collective-permute-done.14 = bf16[2,256,512]{2,1,0:T(8,128)(2,1)S(1)} collective-permute-done((bf16[2,256,512]{2,1,0:T(8,128)(2,1)S(1)}, bf16[2,256,512]{2,1,0:T(8,128)(2,1)S(1)}, u32[]{:S(2)}, u32[]{:S(2)}) %collective-permute-start.14) | collective-permute-done | bytes 524320 | tf_op jit(solution)/shard_map/ppermute | solution.py:601
  208.0 0.0 copy-done.2
  208.0 1.0 constant_dynamic-update-slice_fusion.1
  209.0 0.0 collective-permute-start.15
  209.0 1.9 collective-permute-done.15
  210.9 0.8 constant_dynamic-update-slice_fusion
  (9 shorter events, 0.0 us)
Async XLA Ops:
  74.9 32.6 %copy-start.9 = (bf16[2,256,512]{2,1,0:T(8,128)(2,1)S(1)}, bf16[2,256,512]{2,1,0:T(8,128)(2,1)}, u32[]{:S(2)}) copy-start(bf16[2,256,512]{2,1,0:T(8,128)(2,1)} %get-tuple-element.35) | copy-start | bytes 1572868
  74.9 32.6 %copy-start.10 = (bf16[2,256,512]{2,1,0:T(8,128)(2,1)S(1)}, bf16[2,256,512]{2,1,0:T(8,128)(2,1)}, u32[]{:S(2)}) copy-start(bf16[2,256,512]{2,1,0:T(8,128)(2,1)} %get-tuple-element.36) | copy-start | bytes 1572868
  106.4 29.9 %copy-start.8 = (bf16[2,256,512]{2,1,0:T(8,128)(2,1)S(1)}, bf16[2,256,512]{2,1,0:T(8,128)(2,1)}, u32[]{:S(2)}) copy-start(bf16[2,256,512]{2,1,0:T(8,128)(2,1)} %get-tuple-element.33) | copy-start | bytes 1572868
  106.4 38.5 %copy-start = (bf16[2,2,256,512]{3,2,1,0:T(8,128)(2,1)S(1)}, bf16[2,2,256,512]{3,2,1,0:T(8,128)(2,1)}, u32[]{:S(2)}) copy-start(bf16[2,2,256,512]{3,2,1,0:T(8,128)(2,1)} %get-tuple-element.26.refs_2_.refs_3_) | copy-start | bytes 3145732
  106.4 3.2 %collective-permute-start = (bf16[2,256,512]{2,1,0:T(8,128)(2,1)}, bf16[2,256,512]{2,1,0:T(8,128)(2,1)}, u32[]{:S(2)}, u32[]{:S(2)}) collective-permute-start(bf16[2,256,512]{2,1,0:T(8,128)(2,1)} %get-tuple-element.32), channel_id=1, source_target_pairs={{0,1},{1,0},{2,3},{3,2},{4,5},{5,4},{6,7},{7,6},{8,9},{9,8},{10,11... | collective-permute-start | bytes 1572872 | tf_op jit(solution)/shard_map/ppermute | solution.py:599
  107.6 14.9 %collective-permute-start.6 = (bf16[2,256,512]{2,1,0:T(8,128)(2,1)S(1)}, bf16[2,256,512]{2,1,0:T(8,128)(2,1)}, u32[]{:S(2)}, u32[]{:S(2)}) collective-permute-start(bf16[2,256,512]{2,1,0:T(8,128)(2,1)S(1)} %copy-done.9), channel_id=1, source_target_pairs={{0,2},{2,0},{1,3},{3,1},{4,6},{6,4},{5,7},{7,5},{8,10},{10,8},{9,1... | collective-permute-start | bytes 1572872 | tf_op jit(solution)/shard_map/ppermute | solution.py:610
  107.6 26.1 %collective-permute-start.7 = (bf16[2,256,512]{2,1,0:T(8,128)(2,1)S(1)}, bf16[2,256,512]{2,1,0:T(8,128)(2,1)}, u32[]{:S(2)}, u32[]{:S(2)}) collective-permute-start(bf16[2,256,512]{2,1,0:T(8,128)(2,1)S(1)} %copy-done.10), channel_id=1, source_target_pairs={{0,2},{2,0},{1,3},{3,1},{4,6},{6,4},{5,7},{7,5},{8,10},{10,8},{9,1... | collective-permute-start | bytes 1572872 | tf_op jit(solution)/shard_map/ppermute | solution.py:610
  109.6 26.6 %collective-permute-start.3 = (bf16[2,256,512]{2,1,0:T(8,128)(2,1)}, bf16[2,256,512]{2,1,0:T(8,128)(2,1)S(1)}, u32[]{:S(2)}, u32[]{:S(2)}) collective-permute-start(bf16[2,256,512]{2,1,0:T(8,128)(2,1)} %get-tuple-element.34), channel_id=1, source_target_pairs={{0,1},{1,0},{2,3},{3,2},{4,5},{5,4},{6,7},{7,6},{8,9},{9,8},{10,11... | collective-permute-start | bytes 1572872 | tf_op jit(solution)/shard_map/ppermute | solution.py:599
  110.9 33.9 %collective-permute-start.1 = (bf16[2,256,512]{2,1,0:T(8,128)(2,1)S(1)}, bf16[2,256,512]{2,1,0:T(8,128)(2,1)S(1)}, u32[]{:S(2)}, u32[]{:S(2)}) collective-permute-start(bf16[2,256,512]{2,1,0:T(8,128)(2,1)S(1)} %add_convert_fusion.7), channel_id=1, source_target_pairs={{0,2},{2,0},{1,3},{3,1},{4,6},{6,4},{5,7},{7,5},{8,10},{10,8},{9,1... | collective-permute-start | bytes 1572872 | tf_op jit(solution)/shard_map/ppermute | solution.py:601
  135.6 10.4 %copy-start.1 = (bf16[2,256,512]{2,1,0:T(8,128)(2,1)}, bf16[2,256,512]{2,1,0:T(8,128)(2,1)S(1)}, u32[]{:S(2)}) copy-start(bf16[2,256,512]{2,1,0:T(8,128)(2,1)S(1)} %get-tuple-element.53) | copy-start | bytes 1572868
  135.7 10.4 %copy-start.3 = (bf16[2,256,512]{2,1,0:T(8,128)(2,1)}, bf16[2,256,512]{2,1,0:T(8,128)(2,1)S(1)}, u32[]{:S(2)}) copy-start(bf16[2,256,512]{2,1,0:T(8,128)(2,1)S(1)} %get-tuple-element.54) | copy-start | bytes 1572868
  135.7 10.4 %collective-permute-start.9 = (bf16[2,256,512]{2,1,0:T(8,128)(2,1)S(1)}, bf16[2,256,512]{2,1,0:T(8,128)(2,1)S(1)}, u32[]{:S(2)}, u32[]{:S(2)}) collective-permute-start(bf16[2,256,512]{2,1,0:T(8,128)(2,1)S(1)} %get-tuple-element.53), channel_id=1, source_target_pairs={{0,1},{1,0},{2,3},{3,2},{4,5},{5,4},{6,7},{7,6},{8,9},{9,8},{10,11... | collective-permute-start | bytes 1572872 | tf_op jit(solution)/shard_map/ppermute | solution.py:613
  135.7 10.3 %collective-permute-start.8 = (bf16[2,256,512]{2,1,0:T(8,128)(2,1)S(1)}, bf16[2,256,512]{2,1,0:T(8,128)(2,1)S(1)}, u32[]{:S(2)}, u32[]{:S(2)}) collective-permute-start(bf16[2,256,512]{2,1,0:T(8,128)(2,1)S(1)} %get-tuple-element.54), channel_id=1, source_target_pairs={{0,1},{1,0},{2,3},{3,2},{4,5},{5,4},{6,7},{7,6},{8,9},{9,8},{10,11... | collective-permute-start | bytes 1572872 | tf_op jit(solution)/shard_map/ppermute | solution.py:613
  136.4 38.4 %collective-permute-start.4 = (bf16[2,256,512]{2,1,0:T(8,128)(2,1)S(1)}, bf16[2,256,512]{2,1,0:T(8,128)(2,1)}, u32[]{:S(2)}, u32[]{:S(2)}) collective-permute-start(bf16[2,256,512]{2,1,0:T(8,128)(2,1)S(1)} %add_convert_fusion.6), channel_id=1, source_target_pairs={{0,2},{2,0},{1,3},{3,1},{4,6},{6,4},{5,7},{7,5},{8,10},{10,8},{9,1... | collective-permute-start | bytes 1572872 | tf_op jit(solution)/shard_map/ppermute | solution.py:601
  146.0 28.0 %collective-permute-start.2 = (bf16[2,256,512]{2,1,0:T(8,128)(2,1)}, bf16[2,256,512]{2,1,0:T(8,128)(2,1)S(1)}, u32[]{:S(2)}, u32[]{:S(2)}) collective-permute-start(bf16[2,256,512]{2,1,0:T(8,128)(2,1)} %get-tuple-element.52), channel_id=1, source_target_pairs={{0,1},{1,0},{2,3},{3,2},{4,5},{5,4},{6,7},{7,6},{8,9},{9,8},{10,11... | collective-permute-start | bytes 1572872 | tf_op jit(solution)/shard_map/ppermute | solution.py:628
  146.0 0.8 copy-start.5
  146.0 1.0 copy-start.6
  173.4 19.1 %copy-start.4 = (bf16[2,256,512]{2,1,0:T(8,128)(2,1)S(1)}, bf16[2,256,512]{2,1,0:T(8,128)(2,1)}, u32[]{:S(2)}) copy-start(bf16[2,256,512]{2,1,0:T(8,128)(2,1)} %copy-done.3) | copy-start | bytes 1572868
  173.4 3.5 %collective-permute-start.10 = (bf16[2,256,512]{2,1,0:T(8,128)(2,1)}, bf16[2,256,512]{2,1,0:T(8,128)(2,1)S(1)}, u32[]{:S(2)}, u32[]{:S(2)}) collective-permute-start(bf16[2,256,512]{2,1,0:T(8,128)(2,1)} %get-tuple-element.40), channel_id=1, source_target_pairs={{0,1},{1,0},{2,3},{3,2},{4,5},{5,4},{6,7},{7,6},{8,9},{9,8},{10,11... | collective-permute-start | bytes 1572872 | tf_op jit(solution)/shard_map/ppermute | solution.py:599
  174.0 4.3 %copy-start.11 = (bf16[2,256,512]{2,1,0:T(8,128)(2,1)S(1)}, bf16[2,256,512]{2,1,0:T(8,128)(2,1)}, u32[]{:S(2)}) copy-start(bf16[2,256,512]{2,1,0:T(8,128)(2,1)} %get-tuple-element.42) | copy-start | bytes 1572868
  174.8 18.7 %copy-start.7 = (bf16[2,256,512]{2,1,0:T(8,128)(2,1)S(1)}, bf16[2,256,512]{2,1,0:T(8,128)(2,1)}, u32[]{:S(2)}) copy-start(bf16[2,256,512]{2,1,0:T(8,128)(2,1)} %get-tuple-element.41) | copy-start | bytes 1572868
  176.9 31.1 %copy-start.2 = (bf16[2,256,512]{2,1,0:T(8,128)(2,1)S(1)}, bf16[2,256,512]{2,1,0:T(8,128)(2,1)}, u32[]{:S(2)}) copy-start(bf16[2,256,512]{2,1,0:T(8,128)(2,1)} %copy-done.1) | copy-start | bytes 1572868
  176.9 1.9 collective-permute-start.5
  178.2 14.3 %collective-permute-start.11 = (bf16[2,256,512]{2,1,0:T(8,128)(2,1)S(1)}, bf16[2,256,512]{2,1,0:T(8,128)(2,1)S(1)}, u32[]{:S(2)}, u32[]{:S(2)}) collective-permute-start(bf16[2,256,512]{2,1,0:T(8,128)(2,1)S(1)} %add_convert_fusion.3), channel_id=1, source_target_pairs={{0,2},{2,0},{1,3},{3,1},{4,6},{6,4},{5,7},{7,5},{8,10},{10,8},{9,1... | collective-permute-start | bytes 1572872 | tf_op jit(solution)/shard_map/ppermute | solution.py:601
  178.3 15.2 %collective-permute-start.13 = (bf16[2,256,512]{2,1,0:T(8,128)(2,1)S(1)}, bf16[2,256,512]{2,1,0:T(8,128)(2,1)S(1)}, u32[]{:S(2)}, u32[]{:S(2)}) collective-permute-start(bf16[2,256,512]{2,1,0:T(8,128)(2,1)S(1)} %copy-done.11), channel_id=1, source_target_pairs={{0,1},{1,0},{2,3},{3,2},{4,5},{5,4},{6,7},{7,6},{8,9},{9,8},{10,11... | collective-permute-start | bytes 1572872 | tf_op jit(solution)/shard_map/ppermute | solution.py:599
  193.5 1.9 collective-permute-start.12
  193.7 14.4 %collective-permute-start.14 = (bf16[2,256,512]{2,1,0:T(8,128)(2,1)S(1)}, bf16[2,256,512]{2,1,0:T(8,128)(2,1)S(1)}, u32[]{:S(2)}, u32[]{:S(2)}) collective-permute-start(bf16[2,256,512]{2,1,0:T(8,128)(2,1)S(1)} %add_convert_fusion.1), channel_id=1, source_target_pairs={{0,2},{2,0},{1,3},{3,1},{4,6},{6,4},{5,7},{7,5},{8,10},{10,8},{9,1... | collective-permute-start | bytes 1572872 | tf_op jit(solution)/shard_map/ppermute | solution.py:601
  209.0 1.9 collective-permute-start.15

commit v2 on v1

--- a/solution.py
+++ b/solution.py
@@ -12,7 +12,9 @@
 CHUNKS = 4
 ROW_ALIGN = 16
 TILE = 128
-GROUP = 2
+GROUPS = ((0, 1), (2,), (3,))
+LISTED = 32
+ACTIVE = 33
 RING = 6
 WHOLE = 2
 F32 = jnp.float32
@@ -41,7 +43,7 @@
 
 
 def routes_kernel(ids_ref, pos_ref, tab_ref):
-    chunks, _, tokens = pos_ref.shape
+    _, _, tokens = pos_ref.shape
     steps = ids_ref.shape[0]
     rows = tokens // steps
     experts = 16
@@ -49,8 +51,7 @@
     before = (lax.broadcasted_iota(jnp.int32, (experts, experts), 1) < lax.broadcasted_iota(jnp.int32, (experts, experts), 0)).astype(F32).astype(BF16)
     lane = lax.broadcasted_iota(jnp.int32, (experts, 128), 1)
     number = lax.broadcasted_iota(jnp.int32, (experts, 128), 0).astype(F32)
-    for c in range(chunks):
-        g, k = c // GROUP, c % GROUP
+    for g, k, c in [(g, k, c) for g, group in enumerate(GROUPS) for k, c in enumerate(group)]:
         ids = jnp.concatenate([ids_ref[s, :, c * rows:(c + 1) * rows] for s in range(steps)], axis=1)
         hit = lax.broadcasted_iota(jnp.int32, (experts, tokens), 0) == ids
         hot = hit.astype(F32)
@@ -61,12 +62,12 @@
         pos_ref[c] = jnp.sum(hot * (start[:, :1] + rank - 1.0), axis=0, keepdims=True).astype(jnp.int32)
         tab_ref[g, 16 * k:16 * k + 16, :] = jnp.where(lane == 0, start, count).astype(jnp.int32)
         total = count if k == 0 else total + count
-        if k == GROUP - 1:
+        if c == GROUPS[g][-1]:
             active = (total > 0.0).astype(F32)
             place = jnp.dot(before, active.astype(BF16), preferred_element_type=F32)
             listed = jnp.sum(jnp.where((place == lane.astype(F32)) & (active > 0.0), number, 0.0), axis=0, keepdims=True)
-            tab_ref[g, 16 * GROUP:16 * GROUP + 1, :] = listed.astype(jnp.int32)
-            tab_ref[g, 16 * GROUP + 1:16 * GROUP + 2, :] = jnp.sum(active, axis=0, keepdims=True).astype(jnp.int32)
+            tab_ref[g, LISTED:LISTED + 1, :] = listed.astype(jnp.int32)
+            tab_ref[g, ACTIVE:ACTIVE + 1, :] = jnp.sum(active, axis=0, keepdims=True).astype(jnp.int32)
 
 
 LOG2E = 1.4426950408889634
@@ -364,24 +365,25 @@
             chip_out(c).wait()
 
 
-def moe_kernel(g, *refs):
+def moe_kernel(g, size, *refs):
+    count_in = 2 + 2 * size
     tab_ref, pos_ref = refs[:2]
-    us = refs[2:2 + 2 * GROUP]
-    gff_ref, wr_ref, wg_ref, wu_ref, wd_ref, h_hbm, cv_hbm = refs[2 + 2 * GROUP:9 + 2 * GROUP]
-    refs = refs[9 + 2 * GROUP + (2 if g else 0):]
-    outs = refs[:2 * GROUP]
-    ho_hbm, co_hbm = refs[2 * GROUP:2 * GROUP + 2]
+    us = refs[2:count_in]
+    gff_ref, wr_ref, wg_ref, wu_ref, wd_ref, h_hbm, cv_hbm = refs[count_in:count_in + 7]
+    refs = refs[count_in + (9 if g else 7):]
+    outs = refs[:2 * size]
+    ho_hbm, co_hbm = refs[2 * size:count_in]
     wg, wu, wd, sems, m_s, hot_s, in_s, out_s, prob_s, h_s, cv_s, st_sem = refs[-12:]
     _, half, rows, d_model = us[0].shape
     experts = wr_ref.shape[0]
     tokens = 2 * half * rows
-    slots = hot_s.shape[0] // GROUP
-    room = in_s.shape[0] // GROUP
+    slots = hot_s.shape[0] // size
+    room = in_s.shape[0] // size
     core = lax.rem(lax.axis_index("tp"), 2)
-    active = tab_ref[0, 16 * GROUP + 1, 0]
+    active = tab_ref[0, ACTIVE, 0]
 
     def copies(i):
-        e = tab_ref[0, 16 * GROUP, i]
+        e = tab_ref[0, LISTED, i]
         slot = lax.rem(i, RING)
         return [pltpu.make_async_copy(src.at[e], dst.at[slot], sems.at[k, slot]) for k, (src, dst) in enumerate(((wg_ref, wg), (wu_ref, wu), (wd_ref, wd)))]
 
@@ -393,16 +395,16 @@
 
     for i in range(RING - 1):
         fetch(i)
-    h_span = pl.ds(g * h_s.shape[0], h_s.shape[0])
-    cv_span = pl.ds(g * cv_s.shape[1], cv_s.shape[1])
+    h_span = pl.ds(GROUPS[g][0] * h_s.shape[0] // size, h_s.shape[0])
+    cv_span = pl.ds(GROUPS[g][0] * cv_s.shape[1] // size, cv_s.shape[1])
     pulls = [pltpu.make_async_copy(h_hbm.at[h_span, :], h_s, st_sem.at[0]), pltpu.make_async_copy(cv_hbm.at[:, cv_span, :], cv_s, st_sem.at[1])]
     pushes = [pltpu.make_async_copy(h_s, ho_hbm.at[h_span, :], st_sem.at[2]), pltpu.make_async_copy(cv_s, co_hbm.at[:, cv_span, :], st_sem.at[3])]
     for cp in pulls:
         cp.start()
     gain = row(gff_ref)
-    for j in range(GROUP):
+    for j in range(size):
         for k in range(2):
-            src = us[k * GROUP + j]
+            src = us[k * size + j]
             first = j * tokens + jnp.where(core == k, 0, half * rows)
             for s in range(half):
                 u = src[0, s].astype(F32)
@@ -410,7 +412,7 @@
                 m_s[pl.ds(pl.multiple_of(first + s * rows, rows), rows), :] = m.astype(BF16)
 
     down = lax.broadcasted_iota(jnp.int32, (256, tokens), 0).astype(F32).astype(BF16)
-    for j in range(GROUP):
+    for j in range(size):
         pos = pos_ref[j]
 
         def order(i, carry):
@@ -442,7 +444,7 @@
         out_s[pl.ds(r, size), :] = (prob * jnp.dot(q, wd[slot], preferred_element_type=F32)).astype(BF16)
 
     def expert(i, carry):
-        e = tab_ref[0, 16 * GROUP, i]
+        e = tab_ref[0, LISTED, i]
         slot = lax.rem(i, RING)
         fetch(i + RING - 1)
         for cp in copies(i):
@@ -465,7 +467,7 @@
 
             return c1
 
-        return lax.fori_loop(0, GROUP, part, carry)
+        return lax.fori_loop(0, size, part, carry)
 
     lax.fori_loop(0, active, expert, 0)
 
@@ -476,9 +478,9 @@
             got = lax.dot_general(hot, out_s[j * room:j * room + slots, :], (((0,), (0,)), ((), ())), preferred_element_type=F32)
             dst[s] = got.astype(BF16)
 
-    for j in range(GROUP):
+    for j in range(size):
         for k in range(2):
-            restore(j, k, outs[k * GROUP + j])
+            restore(j, k, outs[k * size + j])
     for cp in pushes:
         cp.wait()
 
@@ -511,7 +513,7 @@
         ids = jnp.transpose(expert_ids, (0, 2, 1))
         pos, table = pl.pallas_call(
             routes_kernel,
-            out_shape=(jax.ShapeDtypeStruct((CHUNKS, 1, tokens), jnp.int32), jax.ShapeDtypeStruct((CHUNKS // GROUP, 16 * GROUP + 8, 128), jnp.int32)),
+            out_shape=(jax.ShapeDtypeStruct((CHUNKS, 1, tokens), jnp.int32), jax.ShapeDtypeStruct((len(GROUPS), ACTIVE + 7, 128), jnp.int32)),
             compiler_params=params(),
             name="routes",
         )(ids)
@@ -565,34 +567,36 @@
             name="mamba",
         )(x_steps, conv_t, h_rows, g_in, w_in, conv_w.T, conv_b, w_xp.T, g_dt, g_b, g_c, w_dt, b_dt, alog_t, d_skip, w_out)
 
-        calls = CHUNKS // GROUP
         room = slots + 2 * TILE
 
         def run_moe(g, u_args, u_specs, states):
             extra = [] if states is None else list(states)
+            size = len(GROUPS[g])
+            first = GROUPS[g][0] // size
+            count_in = 2 + 2 * size
             return pl.pallas_call(
-                functools.partial(moe_kernel, g),
+                functools.partial(moe_kernel, g, size),
                 grid=(1,),
-                in_specs=[pl.BlockSpec((1, 16 * GROUP + 8, 128), lambda i: (g, 0, 0), memory_space=pltpu.SMEM), pl.BlockSpec((GROUP, 1, tokens), lambda i: (g, 0, 0))] + u_specs + [vmem, vmem] + [HBM] * (5 + len(extra)),
-                out_specs=[vmem] * (2 * GROUP) + [HBM, HBM] + ([] if extra else [HBM]),
-                out_shape=[jax.ShapeDtypeStruct(piece, BF16)] * (2 * GROUP) + [jax.ShapeDtypeStruct(h_mid.shape, F32), jax.ShapeDtypeStruct(conv_mid.shape, BF16)] + ([] if extra else [jax.ShapeDtypeStruct(x_steps.shape, BF16)]),
+                in_specs=[pl.BlockSpec((1, ACTIVE + 7, 128), lambda i: (g, 0, 0), memory_space=pltpu.SMEM), pl.BlockSpec((size, 1, tokens), lambda i: (first, 0, 0))] + u_specs + [vmem, vmem] + [HBM] * (5 + len(extra)),
+                out_specs=[vmem] * (2 * size) + [HBM, HBM] + ([] if extra else [HBM]),
+                out_shape=[jax.ShapeDtypeStruct(piece, BF16)] * (2 * size) + [jax.ShapeDtypeStruct(h_mid.shape, F32), jax.ShapeDtypeStruct(conv_mid.shape, BF16)] + ([] if extra else [jax.ShapeDtypeStruct(x_steps.shape, BF16)]),
                 scratch_shapes=[
                     pltpu.VMEM((RING, d_model, ffn), BF16),
                     pltpu.VMEM((RING, d_model, ffn), BF16),
                     pltpu.VMEM((RING, ffn, d_model), BF16),
                     pltpu.SemaphoreType.DMA((3, RING)),
-                    pltpu.VMEM((GROUP * tokens, d_model), BF16),
-                    pltpu.VMEM((GROUP * slots, tokens), BF16),
-                    pltpu.VMEM((GROUP * room, d_model), BF16),
-                    pltpu.VMEM((GROUP * room, d_model), BF16),
-                    pltpu.VMEM((GROUP * room, experts), F32),
-                    pltpu.VMEM((batch * state // calls, inner), F32),
-                    pltpu.VMEM((3, batch // calls, inner), BF16),
+                    pltpu.VMEM((size * tokens, d_model), BF16),
+                    pltpu.VMEM((size * slots, tokens), BF16),
+                    pltpu.VMEM((size * room, d_model), BF16),
+                    pltpu.VMEM((size * room, d_model), BF16),
+                    pltpu.VMEM((size * room, experts), F32),
+                    pltpu.VMEM((size * rows * state, inner), F32),
+                    pltpu.VMEM((3, size * rows, inner), BF16),
                     pltpu.SemaphoreType.DMA((4,)),
                 ],
-                input_output_aliases={9 + 2 * GROUP: 2 * GROUP, 10 + 2 * GROUP: 2 * GROUP + 1} if extra else {},
+                input_output_aliases={count_in + 7: 2 * size, count_in + 8: 2 * size + 1} if extra else {},
                 compiler_params=params(),
-                cost_estimate=pl.CostEstimate(flops=int(6e9), bytes_accessed=int(40e6), transcendentals=0),
+                cost_estimate=pl.CostEstimate(flops=int(3e9) * size, bytes_accessed=int(40e6), transcendentals=0),
             )(table, pos, *u_args, g_ff, w_router.T, w_gate, w_up, w_down, h_mid, conv_mid, *extra)
 
         def both(keep, send, dtype):
@@ -615,15 +619,15 @@
             owns[c] = lambda u_own=u_own: u_own
 
         states = None
-        for g in range(calls):
-            group = [spot[g * GROUP + j] for j in range(GROUP)]
+        for g, members in enumerate(GROUPS):
+            size = len(members)
+            group = [spot[c] for c in members]
             got = run_moe(g, [v[0] for v in group] + [v[1] for v in group], [v[2] for v in group] * 2, states)
-            states = got[2 * GROUP:2 * GROUP + 2]
+            states = got[2 * size:2 * size + 2]
             if g == 0:
                 y_steps = got[-1]
-            for j in range(GROUP):
-                c = g * GROUP + j
-                chip, far = both(got[j], got[GROUP + j], BF16)
+            for j, c in enumerate(members):
+                chip, far = both(got[j], got[size + j], BF16)
                 y_own = (owns[c]().astype(F32) + (chip.astype(F32) + far.astype(F32))).astype(BF16)
                 y_sib = lax.ppermute(y_own, "tp", beside)
                 y_steps = lax.dynamic_update_slice(y_steps, y_own, (half * core, c * rows, 0))

time: 214 us -> 209 us (0.977)
  waiting for transfers between devices: 59.2 us -> 45.5 us
  Pallas kernels: 132 us -> 135 us
  other arithmetic: 10.1 us -> 13.1 us
    ppermute x4, waiting for transfers between devices: 33 us -> 20.9 us  [both(): return (chip, lax.ppermute(chip, 'tp', across))]
    pallas_call x2 -> x3, Pallas kernels: 57.8 us -> 60.6 us  [run_moe(): pl.pallas_call(functools.partial(moe_kernel, g, size), grid=(1,), in_spec...]
  transfers between devices with their start and end apart: 16 -> 16, of which waited for: 8 -> 5; matrix products, arithmetic and copies ran while one was open for 5% -> 7% of each run, Pallas kernels for 12% -> 14%
where the time goes in v2:
time: 209 us; the launch traced here: 206 us
  Pallas kernels  135 us (65%)
  waiting for transfers between devices  45.5 us (22%)
  other arithmetic  13.1 us (6%)
  starting transfers between devices  7.18 us (3%)
  local copies, waits for them, and re-layouts  4.95 us (2%)
    pallas_call x1, Pallas kernels, layer_steps(): pl.pallas_call(mamba_kernel, in_specs=[HBM, HBM, HBM] + [vmem] * 13, out_...  72 us
    pallas_call x3, Pallas kernels, run_moe(): pl.pallas_call(functools.partial(moe_kernel, g, size), grid=(1,), in_spec...  60.6 us
    ppermute x2, waiting for transfers between devices, layer_steps(): far = lax.ppermute(chip, 'tp', across)  22.7 us
    ppermute x4, waiting for transfers between devices, both(): return (chip, lax.ppermute(chip, 'tp', across))  20.9 us
    dynamic_update_slice x4, other arithmetic, layer_steps(): lax.dynamic_update_slice(y_steps, y_own, (half * core, c * rows, 0))  6.28 us
    convert_element_type x4, other arithmetic, both(): chip = (keep.astype(F32) + got.astype(F32)).astype(dtype)  4.76 us
  transfers between devices with their start and end apart: 16, of which 5 were waited for; matrix products, arithmetic and copies ran while one was open for 7% of the time, Pallas kernels for 14%

profile of v2, /device:TPU:0, one launch (start us, length us, event | category | flops | bytes accessed | tf_op | source)
XLA Modules:
  0.0 206.5 jit_solution(4292205668337173685)
XLA Ops:
  0.6 2.3 %routes.1 = (s32[4,1,1024]{2,1,0:T(1,128)}, s32[3,40,128]{2,1,0:T(8,128)}) custom-call(s32[4,1,1024]{2,1,0:T(1,128)} %bitcast.34), custom_call_target="tpu_custom_call" | custom-call | tf_op jit(solution)/shard_map/routes/pallas_call | solution.py:514
  3.0 72.0 %mamba.1 = (bf16[2,2,256,512]{3,2,1,0:T(8,128)(2,1)}, bf16[2,2,256,512]{3,2,1,0:T(8,128)(2,1)}, bf16[2,256,512]{2,1,0:T(8,128)(2,1)}, bf16[2,256,512]{2,1,0:T(8,...) custom-call(bf16[4,1024,512]{2,1,0:T(8,128)(2,1)} %x_hbm.1, bf16[3,1024,256]{2,1,0:T(8,128)(2,1)} %bitcast.36, ...), custom_call_target="tpu_custom_call" | custom-call | flops 8000000000 | bytes 45000000 | tf_op jit(solution)/shard_map/mamba/pallas_call | solution.py:523
  74.9 0.0 copy-start.9
  74.9 0.0 copy-start.8
  75.0 31.4 %shard_map.229 = (bf16[2,256,512]{2,1,0:T(8,128)(2,1)}, bf16[2,256,512]{2,1,0:T(8,128)(2,1)}, bf16[2,256,512]{2,1,0:T(8,128)(2,1)}, bf16[2,256,512]{2,1,0:T(8,12...) custom-call(s32[3,40,128]{2,1,0:T(8,128)} %get-tuple-element.26.refs_0_, ...), custom_call_target="tpu_custom_call" | custom-call | flops 6000000000 | bytes 40000000 | tf_op jit(solution)/shard_map/pallas_call | solution.py:577
  106.4 0.0 copy-start
  106.4 1.2 collective-permute-start
  107.6 0.0 copy-done.9
  107.6 0.0 collective-permute-start.11
  107.6 0.0 copy-done.8
  107.6 2.0 collective-permute-start.6
  109.6 0.0 collective-permute-done
  109.6 1.2 add_convert_fusion.7
  110.8 0.1 collective-permute-start.1
  110.9 0.1 collective-permute-start.3
  111.0 11.5 %collective-permute-done.11 = bf16[2,256,512]{2,1,0:T(8,128)(2,1)} collective-permute-done((bf16[2,256,512]{2,1,0:T(8,128)(2,1)S(1)}, bf16[2,256,512]{2,1,0:T(8,128)(2,1)}, u32[]{:S(2)}, u32[]{:S(2)}) %collective-permute-start.11) | collective-permute-done | bytes 524320 | tf_op jit(solution)/shard_map/ppermute | solution.py:614
  122.5 11.2 %collective-permute-done.6 = bf16[2,256,512]{2,1,0:T(8,128)(2,1)} collective-permute-done((bf16[2,256,512]{2,1,0:T(8,128)(2,1)S(1)}, bf16[2,256,512]{2,1,0:T(8,128)(2,1)}, u32[]{:S(2)}, u32[]{:S(2)}) %collective-permute-start.6) | collective-permute-done | bytes 524320 | tf_op jit(solution)/shard_map/ppermute | solution.py:614
  133.7 2.1 %add_convert_fusion.2 = (bf16[2,256,512]{2,1,0:T(8,128)(2,1)S(1)}, bf16[2,256,512]{2,1,0:T(8,128)(2,1)S(1)}) fusion(bf16[2,256,512]{2,1,0:T(8,128)(2,1)} %collective-permute-done.11, bf16[2,256,512]{2,1,0:T(8,128)(2,1)} %get-tuple-element.42, bf16[4,1024,512]{2,1,0:T(8,128)(2,1)} %x_hbm.1, s32[]{:T(128)S(6)} %select_n.4, ...), kind=kLoop, calls=%fused_computation.6 | loop fusion | flops 3145728 | bytes 4194308 | tf_op jit(solution)/shard_map/convert_element_type | solution.py:616
  135.8 0.0 copy-start.3
  135.8 0.0 copy-start.1
  135.8 0.0 collective-permute-start.7
  135.9 8.2 %collective-permute-done.1 = bf16[2,256,512]{2,1,0:T(8,128)(2,1)} collective-permute-done((bf16[2,256,512]{2,1,0:T(8,128)(2,1)S(1)}, bf16[2,256,512]{2,1,0:T(8,128)(2,1)}, u32[]{:S(2)}, u32[]{:S(2)}) %collective-permute-start.1) | collective-permute-done | bytes 524320 | tf_op jit(solution)/shard_map/ppermute | solution.py:605
  144.0 0.0 copy-done
  144.0 2.2 %constant_dynamic-update-slice_fusion.7 = (bf16[4,1024,512]{2,1,0:T(8,128)(2,1)}, bf16[2,256,512]{2,1,0:T(8,128)(2,1)}) fusion(bf16[4,1024,512]{2,1,0:T(8,128)(2,1)} %get-tuple-element.32, s32[]{:T(128)S(6)} %select_n.4, bf16[2,256,512]{2,1,0:T(8,128)(2,1)} %collective-permute-done.1, bf16[2,256,512]{2,1,0:T(8,128)(2,1)S(1)} %add_convert_fusion.7, ...), kind=kLoop, calls=%fused_computation.19 | loop fusion | flops 1572864 | bytes 2621444 | tf_op jit(solution)/shard_map/dynamic_update_slice | solution.py:633
  146.3 0.0 collective-permute-start.2
  146.3 0.0 collective-permute-done.3
  146.3 0.0 copy-done.7
  146.3 1.2 add_convert_fusion.6
  147.4 0.3 collective-permute-start.4
  147.8 0.0 collective-permute-done.7
  147.8 0.0 copy-done.3
  147.8 0.8 copy-done.6
  148.6 14.6 %shard_map.230 = (bf16[2,256,512]{2,1,0:T(8,128)(2,1)}, bf16[2,256,512]{2,1,0:T(8,128)(2,1)}, f32[16384,256]{1,0:T(8,128)}, bf16[3,1024,256]{2,1,0:T(8,128)(2,1)}) custom-call(s32[3,40,128]{2,1,0:T(8,128)} %get-tuple-element.26.refs_0_, s32[4,1,1024]{2,1,0:T(1,128)} %get-tuple-element.27.refs_1_, ...), custom_call_target="tpu_custom_call", output_to_operand_aliasing={{2}: (11, {}), {3}: (12, {})} | custom-call | flops 3000000000 | bytes 40000000 | tf_op jit(solution)/shard_map/pallas_call | solution.py:577
  163.2 0.3 collective-permute-start.8
  163.5 0.0 copy-done.1
  163.5 0.3 collective-permute-start.12
  163.7 0.0 collective-permute-done.2
  163.7 0.8 constant_dynamic-update-slice_fusion.6
  164.6 0.0 collective-permute-done.4
  164.6 2.0 constant_dynamic-update-slice_fusion.5
  166.6 0.2 collective-permute-start.5
  166.9 0.0 collective-permute-done.8
  166.9 1.2 add_convert_fusion.4
  168.0 1.8 collective-permute-start.9
  169.8 0.0 collective-permute-done.12
  169.8 0.8 copy-done.5
  170.6 14.7 %shard_map.231 = (bf16[2,256,512]{2,1,0:T(8,128)(2,1)}, bf16[2,256,512]{2,1,0:T(8,128)(2,1)}, f32[16384,256]{1,0:T(8,128)}, bf16[3,1024,256]{2,1,0:T(8,128)(2,1)}) custom-call(s32[3,40,128]{2,1,0:T(8,128)} %get-tuple-element.26.refs_0_, s32[4,1,1024]{2,1,0:T(1,128)} %get-tuple-element.27.refs_1_, ...), custom_call_target="tpu_custom_call", output_to_operand_aliasing={{2}: (11, {}), {3}: (12, {})} | custom-call | flops 3000000000 | bytes 40000000 | tf_op jit(solution)/shard_map/pallas_call | solution.py:577
  185.2 0.0 copy-start.2
  185.3 0.0 collective-permute-start.13
  185.3 0.0 collective-permute-done.5
  185.3 0.8 constant_dynamic-update-slice_fusion.4
  186.2 0.0 collective-permute-done.9
  186.2 1.0 constant_dynamic-update-slice_fusion.3
  187.2 0.5 collective-permute-start.10
  187.7 0.0 collective-permute-done.13
  187.7 1.2 add_convert_fusion.1
  188.8 0.3 collective-permute-start.14
  189.2 0.0 collective-permute-done.10
  189.2 0.8 constant_dynamic-update-slice_fusion.2
  190.0 12.7 %collective-permute-done.14 = bf16[2,256,512]{2,1,0:T(8,128)(2,1)S(1)} collective-permute-done((bf16[2,256,512]{2,1,0:T(8,128)(2,1)S(1)}, bf16[2,256,512]{2,1,0:T(8,128)(2,1)S(1)}, u32[]{:S(2)}, u32[]{:S(2)}) %collective-permute-start.14) | collective-permute-done | bytes 524320 | tf_op jit(solution)/shard_map/ppermute | solution.py:605
  202.7 1.0 constant_dynamic-update-slice_fusion.1
  203.7 0.0 collective-permute-start.15
  203.7 1.9 collective-permute-done.15
  205.7 0.8 constant_dynamic-update-slice_fusion
  (6 shorter events, 0.0 us)
Async XLA Ops:
  74.9 32.6 %copy-start.9 = (bf16[2,256,512]{2,1,0:T(8,128)(2,1)S(1)}, bf16[2,256,512]{2,1,0:T(8,128)(2,1)}, u32[]{:S(2)}) copy-start(bf16[2,256,512]{2,1,0:T(8,128)(2,1)} %get-tuple-element.42) | copy-start | bytes 1572868
  74.9 32.6 %copy-start.8 = (bf16[2,256,512]{2,1,0:T(8,128)(2,1)S(1)}, bf16[2,256,512]{2,1,0:T(8,128)(2,1)}, u32[]{:S(2)}) copy-start(bf16[2,256,512]{2,1,0:T(8,128)(2,1)} %get-tuple-element.37) | copy-start | bytes 1572868
  106.4 37.7 %copy-start = (bf16[2,2,256,512]{3,2,1,0:T(8,128)(2,1)S(1)}, bf16[2,2,256,512]{3,2,1,0:T(8,128)(2,1)}, u32[]{:S(2)}) copy-start(bf16[2,2,256,512]{3,2,1,0:T(8,128)(2,1)} %get-tuple-element.28.refs_2_.refs_3_) | copy-start | bytes 3145732
  106.4 3.2 %collective-permute-start = (bf16[2,256,512]{2,1,0:T(8,128)(2,1)}, bf16[2,256,512]{2,1,0:T(8,128)(2,1)S(1)}, u32[]{:S(2)}, u32[]{:S(2)}) collective-permute-start(bf16[2,256,512]{2,1,0:T(8,128)(2,1)} %get-tuple-element.34), channel_id=1, source_target_pairs={{0,1},{1,0},{2,3},{3,2},{4,5},{5,4},{6,7},{7,6},{8,9},{9,8},{10,11... | collective-permute-start | bytes 1572872 | tf_op jit(solution)/shard_map/ppermute | solution.py:603
  107.6 14.9 %collective-permute-start.11 = (bf16[2,256,512]{2,1,0:T(8,128)(2,1)S(1)}, bf16[2,256,512]{2,1,0:T(8,128)(2,1)}, u32[]{:S(2)}, u32[]{:S(2)}) collective-permute-start(bf16[2,256,512]{2,1,0:T(8,128)(2,1)S(1)} %copy-done.9), channel_id=1, source_target_pairs={{0,2},{2,0},{1,3},{3,1},{4,6},{6,4},{5,7},{7,5},{8,10},{10,8},{9,1... | collective-permute-start | bytes 1572872 | tf_op jit(solution)/shard_map/ppermute | solution.py:614
  107.6 26.1 %collective-permute-start.6 = (bf16[2,256,512]{2,1,0:T(8,128)(2,1)S(1)}, bf16[2,256,512]{2,1,0:T(8,128)(2,1)}, u32[]{:S(2)}, u32[]{:S(2)}) collective-permute-start(bf16[2,256,512]{2,1,0:T(8,128)(2,1)S(1)} %copy-done.8), channel_id=1, source_target_pairs={{0,2},{2,0},{1,3},{3,1},{4,6},{6,4},{5,7},{7,5},{8,10},{10,8},{9,1... | collective-permute-start | bytes 1572872 | tf_op jit(solution)/shard_map/ppermute | solution.py:614
  109.6 36.7 %copy-start.7 = (bf16[2,256,512]{2,1,0:T(8,128)(2,1)S(1)}, bf16[2,256,512]{2,1,0:T(8,128)(2,1)}, u32[]{:S(2)}) copy-start(bf16[2,256,512]{2,1,0:T(8,128)(2,1)} %get-tuple-element.35) | copy-start | bytes 1572868
  110.8 33.2 %collective-permute-start.1 = (bf16[2,256,512]{2,1,0:T(8,128)(2,1)S(1)}, bf16[2,256,512]{2,1,0:T(8,128)(2,1)}, u32[]{:S(2)}, u32[]{:S(2)}) collective-permute-start(bf16[2,256,512]{2,1,0:T(8,128)(2,1)S(1)} %add_convert_fusion.7), channel_id=1, source_target_pairs={{0,2},{2,0},{1,3},{3,1},{4,6},{6,4},{5,7},{7,5},{8,10},{10,8},{9,1... | collective-permute-start | bytes 1572872 | tf_op jit(solution)/shard_map/ppermute | solution.py:605
  110.9 35.3 %collective-permute-start.3 = (bf16[2,256,512]{2,1,0:T(8,128)(2,1)}, bf16[2,256,512]{2,1,0:T(8,128)(2,1)}, u32[]{:S(2)}, u32[]{:S(2)}) collective-permute-start(bf16[2,256,512]{2,1,0:T(8,128)(2,1)} %get-tuple-element.36), channel_id=1, source_target_pairs={{0,1},{1,0},{2,3},{3,2},{4,5},{5,4},{6,7},{7,6},{8,9},{9,8},{10,11... | collective-permute-start | bytes 1572872 | tf_op jit(solution)/shard_map/ppermute | solution.py:603
  135.8 12.0 %copy-start.3 = (bf16[2,256,512]{2,1,0:T(8,128)(2,1)}, bf16[2,256,512]{2,1,0:T(8,128)(2,1)S(1)}, u32[]{:S(2)}) copy-start(bf16[2,256,512]{2,1,0:T(8,128)(2,1)S(1)} %get-tuple-element.58) | copy-start | bytes 1572868
  135.8 27.7 %copy-start.1 = (bf16[2,256,512]{2,1,0:T(8,128)(2,1)}, bf16[2,256,512]{2,1,0:T(8,128)(2,1)S(1)}, u32[]{:S(2)}) copy-start(bf16[2,256,512]{2,1,0:T(8,128)(2,1)S(1)} %get-tuple-element.57) | copy-start | bytes 1572868
  135.8 11.9 %collective-permute-start.7 = (bf16[2,256,512]{2,1,0:T(8,128)(2,1)S(1)}, bf16[2,256,512]{2,1,0:T(8,128)(2,1)S(1)}, u32[]{:S(2)}, u32[]{:S(2)}) collective-permute-start(bf16[2,256,512]{2,1,0:T(8,128)(2,1)S(1)} %get-tuple-element.58), channel_id=1, source_target_pairs={{0,1},{1,0},{2,3},{3,2},{4,5},{5,4},{6,7},{7,6},{8,9},{9,8},{10,11... | collective-permute-start | bytes 1572872 | tf_op jit(solution)/shard_map/ppermute | solution.py:617
  146.3 17.5 %collective-permute-start.2 = (bf16[2,256,512]{2,1,0:T(8,128)(2,1)}, bf16[2,256,512]{2,1,0:T(8,128)(2,1)S(1)}, u32[]{:S(2)}, u32[]{:S(2)}) collective-permute-start(bf16[2,256,512]{2,1,0:T(8,128)(2,1)} %get-tuple-element.56), channel_id=1, source_target_pairs={{0,1},{1,0},{2,3},{3,2},{4,5},{5,4},{6,7},{7,6},{8,9},{9,8},{10,11... | collective-permute-start | bytes 1572872 | tf_op jit(solution)/shard_map/ppermute | solution.py:632
  147.4 17.1 %collective-permute-start.4 = (bf16[2,256,512]{2,1,0:T(8,128)(2,1)S(1)}, bf16[2,256,512]{2,1,0:T(8,128)(2,1)}, u32[]{:S(2)}, u32[]{:S(2)}) collective-permute-start(bf16[2,256,512]{2,1,0:T(8,128)(2,1)S(1)} %add_convert_fusion.6), channel_id=1, source_target_pairs={{0,2},{2,0},{1,3},{3,1},{4,6},{6,4},{5,7},{7,5},{8,10},{10,8},{9,1... | collective-permute-start | bytes 1572872 | tf_op jit(solution)/shard_map/ppermute | solution.py:605
  147.8 0.8 copy-start.6
  163.2 3.7 %collective-permute-start.8 = (bf16[2,256,512]{2,1,0:T(8,128)(2,1)}, bf16[2,256,512]{2,1,0:T(8,128)(2,1)S(1)}, u32[]{:S(2)}, u32[]{:S(2)}) collective-permute-start(bf16[2,256,512]{2,1,0:T(8,128)(2,1)} %get-tuple-element.41), channel_id=1, source_target_pairs={{0,1},{1,0},{2,3},{3,2},{4,5},{5,4},{6,7},{7,6},{8,9},{9,8},{10,11... | collective-permute-start | bytes 1572872 | tf_op jit(solution)/shard_map/ppermute | solution.py:603
  163.5 6.3 %collective-permute-start.12 = (bf16[2,256,512]{2,1,0:T(8,128)(2,1)S(1)}, bf16[2,256,512]{2,1,0:T(8,128)(2,1)S(1)}, u32[]{:S(2)}, u32[]{:S(2)}) collective-permute-start(bf16[2,256,512]{2,1,0:T(8,128)(2,1)S(1)} %get-tuple-element.57), channel_id=1, source_target_pairs={{0,1},{1,0},{2,3},{3,2},{4,5},{5,4},{6,7},{7,6},{8,9},{9,8},{10,11... | collective-permute-start | bytes 1572872 | tf_op jit(solution)/shard_map/ppermute | solution.py:617
  166.6 18.7 %collective-permute-start.5 = (bf16[2,256,512]{2,1,0:T(8,128)(2,1)S(1)}, bf16[2,256,512]{2,1,0:T(8,128)(2,1)S(1)}, u32[]{:S(2)}, u32[]{:S(2)}) collective-permute-start(bf16[2,256,512]{2,1,0:T(8,128)(2,1)S(1)} %get-tuple-element.54), channel_id=1, source_target_pairs={{0,1},{1,0},{2,3},{3,2},{4,5},{5,4},{6,7},{7,6},{8,9},{9,8},{10,11... | collective-permute-start | bytes 1572872 | tf_op jit(solution)/shard_map/ppermute | solution.py:632
  168.0 18.1 %collective-permute-start.9 = (bf16[2,256,512]{2,1,0:T(8,128)(2,1)S(1)}, bf16[2,256,512]{2,1,0:T(8,128)(2,1)S(1)}, u32[]{:S(2)}, u32[]{:S(2)}) collective-permute-start(bf16[2,256,512]{2,1,0:T(8,128)(2,1)S(1)} %add_convert_fusion.4), channel_id=1, source_target_pairs={{0,2},{2,0},{1,3},{3,1},{4,6},{6,4},{5,7},{7,5},{8,10},{10,8},{9,1... | collective-permute-start | bytes 1572872 | tf_op jit(solution)/shard_map/ppermute | solution.py:605
  169.8 0.8 copy-start.5
  170.6 15.6 %copy-start.4 = (bf16[2,256,512]{2,1,0:T(8,128)(2,1)S(1)}, bf16[2,256,512]{2,1,0:T(8,128)(2,1)}, u32[]{:S(2)}) copy-start(bf16[2,256,512]{2,1,0:T(8,128)(2,1)} %copy-done.3) | copy-start | bytes 1572868
  185.2 17.5 %copy-start.2 = (bf16[2,256,512]{2,1,0:T(8,128)(2,1)S(1)}, bf16[2,256,512]{2,1,0:T(8,128)(2,1)}, u32[]{:S(2)}) copy-start(bf16[2,256,512]{2,1,0:T(8,128)(2,1)} %copy-done.1) | copy-start | bytes 1572868
  185.3 2.4 %collective-permute-start.13 = (bf16[2,256,512]{2,1,0:T(8,128)(2,1)}, bf16[2,256,512]{2,1,0:T(8,128)(2,1)S(1)}, u32[]{:S(2)}, u32[]{:S(2)}) collective-permute-start(bf16[2,256,512]{2,1,0:T(8,128)(2,1)} %get-tuple-element.46), channel_id=1, source_target_pairs={{0,1},{1,0},{2,3},{3,2},{4,5},{5,4},{6,7},{7,6},{8,9},{9,8},{10,11... | collective-permute-start | bytes 1572872 | tf_op jit(solution)/shard_map/ppermute | solution.py:603
  187.2 2.0 collective-permute-start.10
  188.8 13.9 %collective-permute-start.14 = (bf16[2,256,512]{2,1,0:T(8,128)(2,1)S(1)}, bf16[2,256,512]{2,1,0:T(8,128)(2,1)S(1)}, u32[]{:S(2)}, u32[]{:S(2)}) collective-permute-start(bf16[2,256,512]{2,1,0:T(8,128)(2,1)S(1)} %add_convert_fusion.1), channel_id=1, source_target_pairs={{0,2},{2,0},{1,3},{3,1},{4,6},{6,4},{5,7},{7,5},{8,10},{10,8},{9,1... | collective-permute-start | bytes 1572872 | tf_op jit(solution)/shard_map/ppermute | solution.py:605
  203.7 1.9 collective-permute-start.15

commit v3 on v2

--- a/solution.py
+++ b/solution.py
@@ -13,6 +13,7 @@
 ROW_ALIGN = 16
 TILE = 128
 GROUPS = ((0, 1), (2,), (3,))
+LAST = CHUNKS - 1
 LISTED = 32
 ACTIVE = 33
 RING = 6
@@ -75,7 +76,7 @@
 
 def mamba_kernel(x_hbm, cs_hbm, h_hbm, g_ref, win3_ref, cw_ref, cb_ref, wxp_ref, gdt_ref, gb_ref, gc_ref, wdt_ref, bdt_ref, alog_ref, dskip_ref, wout_ref,
                  uo_hbm, us_hbm, chip2_hbm, chip3_hbm, co_hbm, ho_hbm,
-                 x_s, cs_s, co_s, h_s, xc_s, z_s, p_s, m_s, u_s, win_ref, g4_ref, wdt4, ones_s, even_s, odd_s, a_s, q_s, delta_s, dx_s, y_s,
+                 x_s, cs_s, co_s, h_s, xc_s, z_s, p_s, m_s, u_s, win_ref, g4_ref, wdt4, ones_s, a_s, q_s, delta_s, dx_s, y_s,
                  in_sem, h_sem, out_sem, ho_sem, psend, precv, msend, mrecv):
     steps, batch, _ = x_s.shape
     inner = cs_s.shape[2]
@@ -195,7 +196,7 @@
         p_s[5, c] = p_s[3, c] + p_s[4, c]
         p_back(c).start()
 
-    def scan(c):
+    def scan(c, between=None):
         p_back(c).wait_recv()
         for cp in h_loads(c):
             cp.wait()
@@ -223,44 +224,32 @@
                 delta_s[s] = delta
                 dx_s[s] = delta * xc_s[s, pl.ds(g, 128), :].astype(F32)
 
-            def spread(t, wide):
-                b = pl.multiple_of(t * 8, 8)
-                qs = [q_s[s, pl.ds(b, 8), :] for s in range(steps)]
-                for n in range(2 * state):
-                    for s in range(steps):
-                        wide[s, n] = jnp.broadcast_to(qs[s][:, n:n + 1], (8, 128))
-
-            def advance(t, wide):
+            def tile(t, carry2):
                 b = pl.multiple_of(t * 8, 8)
                 base = (g + b) * state
                 cut = [slice(l * 128, (l + 1) * 128) for l in range(tiles)]
                 dl = [[delta_s[s, pl.ds(b, 8), k] for k in cut] for s in range(steps)]
                 dx = [[dx_s[s, pl.ds(b, 8), k] for k in cut] for s in range(steps)]
+                qs = [q_s[s, pl.ds(b, 8), :] for s in range(steps)]
                 ys = [[None] * tiles for _ in range(steps)]
                 for n in range(state):
+                    bs = [jnp.broadcast_to(qs[s][:, n:n + 1], (8, 128)) for s in range(steps)]
+                    cs = [jnp.broadcast_to(qs[s][:, n + state:n + state + 1], (8, 128)) for s in range(steps)]
                     for l in range(tiles):
                         a = a_s[n:n + 1, cut[l]]
                         spot = (l, pl.ds(base + n, 8, stride=state))
                         h = h_s[spot]
                         for s in range(steps):
-                            h = jnp.exp2(dl[s][l] * a) * h + dx[s][l] * wide[s, n]
-                            hc = h * wide[s, n + state]
+                            h = jnp.exp2(dl[s][l] * a) * h + dx[s][l] * bs[s]
+                            hc = h * cs[s]
                             ys[s][l] = hc if n == 0 else ys[s][l] + hc
                         h_s[spot] = h
                 for s in range(steps):
                     for l in range(tiles):
                         y_s[s, pl.ds(b, 8), cut[l]] = ys[s][l]
-
-            def pair(i, carry2):
-                t = 2 * i
-                spread(t + 1, odd_s)
-                advance(t, even_s)
-                spread(jnp.minimum(t + 2, 14), even_s)
-                advance(t + 1, odd_s)
                 return carry2
 
-            spread(0, even_s)
-            lax.fori_loop(0, 8, pair, 0)
+            lax.fori_loop(0, 16, tile, 0, unroll=2)
             for s in range(steps):
                 xc = xc_s[s, pl.ds(g, 128), :].astype(F32)
                 yg = ((y_s[s] + row(dskip_ref) * xc) * silu(z_s[s, pl.ds(g, 128), :].astype(F32))).astype(BF16)
@@ -268,7 +257,12 @@
                 m_s[lax.rem(core + s // half, 2), c, s % half, pl.ds(r, 128), :] = out
             return carry
 
-        lax.fori_loop(0, rows // 128, block, 0)
+        if between is None:
+            lax.fori_loop(0, rows // 128, block, 0)
+        else:
+            lax.fori_loop(0, 1, block, 0)
+            between()
+            lax.fori_loop(1, rows // 128, block, 0)
         for cp in h_stores(c):
             cp.start()
         m_beside(c).start()
@@ -331,20 +325,18 @@
     a_s[...] = -LOG2E * jnp.exp(alog_ref[...])
 
     p_sum(3)
+    scan(0)
     p_whole(1)
-    scan(0)
     p_whole(2)
+    m_sum(0)
     p_whole(3)
-    m_sum(0)
     scan(1)
     m_sum(1)
     scan(2)
     m_sum(2)
     m_whole(0)
-    scan(3)
+    scan(3, lambda: m_whole(1))
     m_sum(3)
-    for c in range(1, WHOLE):
-        m_whole(c)
     for c in range(WHOLE):
         u_back(c).wait_recv()
         us_out(c).start()
@@ -429,7 +421,7 @@
             prob_s[at, :] = ex / jnp.sum(ex, axis=-1, keepdims=True)
             return carry
 
-        lax.fori_loop(0, slots // 256, order, 0)
+        lax.fori_loop(0, slots // 256, order, 0, unroll=True)
     for pull, push in zip(pulls, pushes):
         pull.wait()
         push.start()
@@ -546,8 +538,6 @@
                 pltpu.VMEM((1, steps * width), F32),
                 pltpu.VMEM((steps * width, steps * inner), BF16),
                 pltpu.VMEM((steps * width, steps * width), BF16),
-                pltpu.VMEM((steps, 2 * state, 8, 128), F32),
-                pltpu.VMEM((steps, 2 * state, 8, 128), F32),
                 pltpu.VMEM((state, inner), F32),
                 pltpu.VMEM((steps, 128, 128), F32),
                 pltpu.VMEM((steps, 128, inner), F32),
@@ -619,6 +609,7 @@
             owns[c] = lambda u_own=u_own: u_own
 
         states = None
+        pieces = {}
         for g, members in enumerate(GROUPS):
             size = len(members)
             group = [spot[c] for c in members]
@@ -630,8 +621,11 @@
                 chip, far = both(got[j], got[size + j], BF16)
                 y_own = (owns[c]().astype(F32) + (chip.astype(F32) + far.astype(F32))).astype(BF16)
                 y_sib = lax.ppermute(y_own, "tp", beside)
-                y_steps = lax.dynamic_update_slice(y_steps, y_own, (half * core, c * rows, 0))
-                y_steps = lax.dynamic_update_slice(y_steps, y_sib, (half * (1 - core), c * rows, 0))
+                pieces[c] = (y_own, y_sib)
+        for some in (range(LAST), (LAST,)):
+            for k in range(2):
+                for c in some:
+                    y_steps = lax.dynamic_update_slice(y_steps, pieces[c][k], (half * lax.rem(core + k, 2), c * rows, 0))
         ssm_out, conv_out = states
         ssm_fin = jnp.transpose(ssm_out.reshape(batch, state, inner), (0, 2, 1))
         return y_steps, jnp.transpose(conv_out, (1, 2, 0)), ssm_fin

time: 209 us -> 169 us (0.81)
  waiting for transfers between devices: 45.5 us -> 18.1 us
  Pallas kernels: 135 us -> 127 us
  other arithmetic: 13.1 us -> 7.94 us
    ppermute x2, waiting for transfers between devices: 22.7 us -> 0.01 us  [layer_steps(): far = lax.ppermute(chip, 'tp', across)]
    pallas_call x1, Pallas kernels: 72 us -> 63.5 us  [layer_steps(): pl.pallas_call(mamba_kernel, in_specs=[HBM, HBM, HBM] + [vmem] * 13, out_...]
    ppermute x4, waiting for transfers between devices: 20.9 us -> 15.3 us  [both(): return (chip, lax.ppermute(chip, 'tp', across))]
    convert_element_type x4, other arithmetic: 4.76 us -> 0.54 us  [both(): chip = (keep.astype(F32) + got.astype(F32)).astype(dtype)]
  transfers between devices with their start and end apart: 16 -> 16, of which waited for: 5 -> 4; matrix products, arithmetic and copies ran while one was open for 7% -> 5% of each run, Pallas kernels for 14% -> 38%
where the time goes in v3:
time: 169 us; the launch traced here: 167 us
  Pallas kernels  127 us (75%)
  waiting for transfers between devices  18.1 us (11%)
  other arithmetic  7.94 us (5%)
  starting transfers between devices  7.85 us (5%)
  local copies, waits for them, and re-layouts  5.75 us (3%)
    pallas_call x1, Pallas kernels, layer_steps(): pl.pallas_call(mamba_kernel, in_specs=[HBM, HBM, HBM] + [vmem] * 13, out_...  63.5 us
    pallas_call x3, Pallas kernels, run_moe(): pl.pallas_call(functools.partial(moe_kernel, g, size), grid=(1,), in_spec...  61.2 us
    ppermute x4, waiting for transfers between devices, both(): return (chip, lax.ppermute(chip, 'tp', across))  15.3 us
    dynamic_update_slice x4, other arithmetic, layer_steps(): lax.dynamic_update_slice(y_steps, pieces[c][k], (half * lax.rem(core + k,...  5.46 us
  transfers between devices with their start and end apart: 16, of which 4 were waited for; matrix products, arithmetic and copies ran while one was open for 5% of the time, Pallas kernels for 38%

profile of v3, /device:TPU:0, one launch (start us, length us, event | category | flops | bytes accessed | tf_op | source)
XLA Modules:
  0.0 167.4 jit_solution(1090233198611796023)
XLA Ops:
  0.6 63.5 %mamba.1 = (bf16[2,2,256,512]{3,2,1,0:T(8,128)(2,1)}, bf16[2,2,256,512]{3,2,1,0:T(8,128)(2,1)}, bf16[2,256,512]{2,1,0:T(8,128)(2,1)}, bf16[2,256,512]{2,1,0:T(8,...) custom-call(bf16[4,1024,512]{2,1,0:T(8,128)(2,1)} %x_hbm.1, bf16[3,1024,256]{2,1,0:T(8,128)(2,1)} %bitcast.36, ...), custom_call_target="tpu_custom_call" | custom-call | flops 8000000000 | bytes 45000000 | tf_op jit(solution)/shard_map/mamba/pallas_call | solution.py:515
  64.1 0.0 collective-permute-start.11
  64.2 2.0 %collective-permute-start.4 = (bf16[2,256,512]{2,1,0:T(8,128)(2,1)}, bf16[2,256,512]{2,1,0:T(8,128)(2,1)}, u32[]{:S(2)}, u32[]{:S(2)}) collective-permute-start(bf16[2,256,512]{2,1,0:T(8,128)(2,1)} %get-tuple-element.37), channel_id=1, source_target_pairs={{0,2},{2,0},{1,3},{3,1},{4,6},{6,4},{5,7},{7,5},{8,10},{10,8},{9,1... | collective-permute-start | bytes 1572872 | tf_op jit(solution)/shard_map/ppermute | solution.py:604
  66.2 2.3 %routes.1 = (s32[4,1,1024]{2,1,0:T(1,128)}, s32[3,40,128]{2,1,0:T(8,128)}) custom-call(s32[4,1,1024]{2,1,0:T(1,128)} %bitcast.34), custom_call_target="tpu_custom_call" | custom-call | tf_op jit(solution)/shard_map/routes/pallas_call | solution.py:506
  68.5 31.2 %shard_map.229 = (bf16[2,256,512]{2,1,0:T(8,128)(2,1)}, bf16[2,256,512]{2,1,0:T(8,128)(2,1)}, bf16[2,256,512]{2,1,0:T(8,128)(2,1)}, bf16[2,256,512]{2,1,0:T(8,12...) custom-call(s32[3,40,128]{2,1,0:T(8,128)} %get-tuple-element.26.refs_0_, ...), custom_call_target="tpu_custom_call" | custom-call | flops 6000000000 | bytes 40000000 | tf_op jit(solution)/shard_map/pallas_call | solution.py:567
  99.7 0.0 copy-start.8
  99.7 0.7 collective-permute-start
  100.4 0.0 collective-permute-done.11
  100.4 0.8 copy-done.11
  101.2 0.0 collective-permute-done.4
  101.2 0.0 copy-done.9
  101.2 0.0 copy-done.10
  101.2 1.9 %add_convert_fusion.2 = (bf16[2,256,512]{2,1,0:T(8,128)(2,1)S(1)}, bf16[2,256,512]{2,1,0:T(8,128)(2,1)S(1)}) fusion(bf16[2,256,512]{2,1,0:T(8,128)(2,1)} %copy-done.11, bf16[2,256,512]{2,1,0:T(8,128)(2,1)S(1)} %copy-done.10, bf16[4,1024,512]{2,1,0:T(8,128)(2,1)} %x_hbm.1, s32[]{:T(128)S(6)} %select_n.7, bf16[2,256,512]{2,1,0:T(8,128)(2,1)} %collective-permute-done.4, ...), kind=kLoop, calls=%fused_computation.6 | loop fusion | flops 3145728 | bytes 4194308 | tf_op jit(solution)/shard_map/convert_element_type | solution.py:606
  103.2 0.0 copy-start.3
  103.2 0.0 copy-start.1
  103.2 0.1 collective-permute-start.5
  103.3 0.5 collective-permute-start.2
  103.8 0.0 collective-permute-done
  103.8 0.0 copy-done.8
  103.8 0.1 add_convert_fusion.7
  103.9 0.4 collective-permute-start.1
  104.3 0.9 collective-permute-done.5
  105.2 0.0 copy-done.3
  105.2 0.8 copy-done.5
  106.0 15.0 %shard_map.230 = (bf16[2,256,512]{2,1,0:T(8,128)(2,1)}, bf16[2,256,512]{2,1,0:T(8,128)(2,1)}, f32[16384,256]{1,0:T(8,128)}, bf16[3,1024,256]{2,1,0:T(8,128)(2,1)}) custom-call(s32[3,40,128]{2,1,0:T(8,128)} %get-tuple-element.26.refs_0_, s32[4,1,1024]{2,1,0:T(1,128)} %get-tuple-element.27.refs_1_, ...), custom_call_target="tpu_custom_call", output_to_operand_aliasing={{2}: (11, {}), {3}: (12, {})} | custom-call | flops 3000000000 | bytes 40000000 | tf_op jit(solution)/shard_map/pallas_call | solution.py:567
  121.0 0.2 collective-permute-start.6
  121.2 0.0 collective-permute-done.2
  121.2 0.0 copy-done.7
  121.2 0.1 add_convert_fusion.6
  121.4 0.7 collective-permute-start.3
  122.1 0.0 copy-done.1
  122.1 0.2 collective-permute-start.12
  122.3 0.0 collective-permute-done.1
  122.3 1.0 constant_dynamic-update-slice_fusion.7
  123.3 0.3 collective-permute-start.8
  123.6 0.0 collective-permute-done.6
  123.6 0.1 add_convert_fusion.4
  123.8 1.4 collective-permute-start.7
  125.1 0.0 collective-permute-done.12
  125.1 0.8 copy-done.6
  126.0 15.0 %shard_map.231 = (bf16[2,256,512]{2,1,0:T(8,128)(2,1)}, bf16[2,256,512]{2,1,0:T(8,128)(2,1)}, f32[16384,256]{1,0:T(8,128)}, bf16[3,1024,256]{2,1,0:T(8,128)(2,1)}) custom-call(s32[3,40,128]{2,1,0:T(8,128)} %get-tuple-element.26.refs_0_, s32[4,1,1024]{2,1,0:T(1,128)} %get-tuple-element.27.refs_1_, ...), custom_call_target="tpu_custom_call", output_to_operand_aliasing={{2}: (11, {}), {3}: (12, {})} | custom-call | flops 3000000000 | bytes 40000000 | tf_op jit(solution)/shard_map/pallas_call | solution.py:567
  140.9 0.0 collective-permute-start.13
  141.0 0.0 collective-permute-done.3
  141.0 1.2 constant_dynamic-update-slice_fusion.6
  142.2 0.5 collective-permute-start.9
  142.7 4.1 %collective-permute-done.7 = bf16[2,256,512]{2,1,0:T(8,128)(2,1)S(1)} collective-permute-done((bf16[2,256,512]{2,1,0:T(8,128)(2,1)S(1)}, bf16[2,256,512]{2,1,0:T(8,128)(2,1)S(1)}, u32[]{:S(2)}, u32[]{:S(2)}) %collective-permute-start.7) | collective-permute-done | bytes 524320 | tf_op jit(solution)/shard_map/ppermute | solution.py:595
  146.8 0.0 copy-done.4
  146.8 1.2 constant_dynamic-update-slice_fusion.5
  148.0 0.0 collective-permute-start.10
  148.0 0.0 collective-permute-done.13
  148.0 0.1 add_convert_fusion.1
  148.2 0.8 collective-permute-start.14
  149.0 0.0 collective-permute-done.8
  149.0 0.8 constant_dynamic-update-slice_fusion.4
  149.9 0.0 collective-permute-done.9
  149.9 0.8 constant_dynamic-update-slice_fusion.3
  150.7 0.0 collective-permute-done.10
  150.7 0.8 constant_dynamic-update-slice_fusion.2
  151.5 11.1 %collective-permute-done.14 = bf16[2,256,512]{2,1,0:T(8,128)(2,1)} collective-permute-done((bf16[2,256,512]{2,1,0:T(8,128)(2,1)S(1)}, bf16[2,256,512]{2,1,0:T(8,128)(2,1)}, u32[]{:S(2)}, u32[]{:S(2)}) %collective-permute-start.14) | collective-permute-done | bytes 524320 | tf_op jit(solution)/shard_map/ppermute | solution.py:595
  162.6 0.0 copy-done.2
  162.7 2.1 %constant_dynamic-update-slice_fusion.1 = (bf16[4,1024,512]{2,1,0:T(8,128)(2,1)}, bf16[2,256,512]{2,1,0:T(8,128)(2,1)S(1)}) fusion(bf16[4,1024,512]{2,1,0:T(8,128)(2,1)} %constant_dynamic-update-slice_fusion.2, s32[]{:T(128)S(6)} %select_n.6, bf16[2,256,512]{2,1,0:T(8,128)(2,1)} %collective-permute-done.14, bf16[2,256,512]{2,1,0:T(8,128)(2,1)S(1)} %add_convert_fusion.1, ...), kind=kLoop, calls=%fused_computation.13 | loop fusion | flops 1572864 | bytes 2621444 | tf_op jit(solution)/shard_map/dynamic_update_slice | solution.py:628
  164.7 0.0 collective-permute-start.15
  164.7 1.9 %collective-permute-done.15 = bf16[2,256,512]{2,1,0:T(8,128)(2,1)S(1)} collective-permute-done((bf16[2,256,512]{2,1,0:T(8,128)(2,1)S(1)}, bf16[2,256,512]{2,1,0:T(8,128)(2,1)S(1)}, u32[]{:S(2)}, u32[]{:S(2)}) %collective-permute-start.15) | collective-permute-done | bytes 524320 | tf_op jit(solution)/shard_map/ppermute | solution.py:623
  166.6 0.8 constant_dynamic-update-slice_fusion
  (14 shorter events, 0.0 us)
Async XLA Ops:
  64.1 36.3 %collective-permute-start.11 = (bf16[2,256,512]{2,1,0:T(8,128)(2,1)}, bf16[2,256,512]{2,1,0:T(8,128)(2,1)S(1)}, u32[]{:S(2)}, u32[]{:S(2)}) collective-permute-start(bf16[2,256,512]{2,1,0:T(8,128)(2,1)} %get-tuple-element.42), channel_id=1, source_target_pairs={{0,2},{2,0},{1,3},{3,1},{4,6},{6,4},{5,7},{7,5},{8,10},{10,8},{9,1... | collective-permute-start | bytes 1572872 | tf_op jit(solution)/shard_map/ppermute | solution.py:604
  64.2 37.1 %collective-permute-start.4 = (bf16[2,256,512]{2,1,0:T(8,128)(2,1)}, bf16[2,256,512]{2,1,0:T(8,128)(2,1)}, u32[]{:S(2)}, u32[]{:S(2)}) collective-permute-start(bf16[2,256,512]{2,1,0:T(8,128)(2,1)} %get-tuple-element.37), channel_id=1, source_target_pairs={{0,2},{2,0},{1,3},{3,1},{4,6},{6,4},{5,7},{7,5},{8,10},{10,8},{9,1... | collective-permute-start | bytes 1572872 | tf_op jit(solution)/shard_map/ppermute | solution.py:604
  68.5 32.7 %copy-start.9 = (bf16[2,256,512]{2,1,0:T(8,128)(2,1)S(1)}, bf16[2,256,512]{2,1,0:T(8,128)(2,1)}, u32[]{:S(2)}) copy-start(bf16[2,256,512]{2,1,0:T(8,128)(2,1)} %get-tuple-element.37) | copy-start | bytes 1572868
  68.5 32.7 %copy-start.10 = (bf16[2,256,512]{2,1,0:T(8,128)(2,1)S(1)}, bf16[2,256,512]{2,1,0:T(8,128)(2,1)}, u32[]{:S(2)}) copy-start(bf16[2,256,512]{2,1,0:T(8,128)(2,1)} %get-tuple-element.42) | copy-start | bytes 1572868
  99.7 4.1 %copy-start.8 = (bf16[2,256,512]{2,1,0:T(8,128)(2,1)S(1)}, bf16[2,256,512]{2,1,0:T(8,128)(2,1)}, u32[]{:S(2)}) copy-start(bf16[2,256,512]{2,1,0:T(8,128)(2,1)} %get-tuple-element.33) | copy-start | bytes 1572868
  99.7 4.0 %collective-permute-start = (bf16[2,256,512]{2,1,0:T(8,128)(2,1)}, bf16[2,256,512]{2,1,0:T(8,128)(2,1)S(1)}, u32[]{:S(2)}, u32[]{:S(2)}) collective-permute-start(bf16[2,256,512]{2,1,0:T(8,128)(2,1)} %get-tuple-element.34), channel_id=1, source_target_pairs={{0,1},{1,0},{2,3},{3,2},{4,5},{5,4},{6,7},{7,6},{8,9},{9,8},{10,11... | collective-permute-start | bytes 1572872 | tf_op jit(solution)/shard_map/ppermute | solution.py:593
  100.4 0.8 copy-start.11
  103.2 2.0 %copy-start.3 = (bf16[2,256,512]{2,1,0:T(8,128)(2,1)}, bf16[2,256,512]{2,1,0:T(8,128)(2,1)S(1)}, u32[]{:S(2)}) copy-start(bf16[2,256,512]{2,1,0:T(8,128)(2,1)S(1)} %get-tuple-element.58) | copy-start | bytes 1572868
  103.2 18.9 %copy-start.1 = (bf16[2,256,512]{2,1,0:T(8,128)(2,1)}, bf16[2,256,512]{2,1,0:T(8,128)(2,1)S(1)}, u32[]{:S(2)}) copy-start(bf16[2,256,512]{2,1,0:T(8,128)(2,1)S(1)} %get-tuple-element.57) | copy-start | bytes 1572868
  103.2 1.9 %collective-permute-start.5 = (bf16[2,256,512]{2,1,0:T(8,128)(2,1)S(1)}, bf16[2,256,512]{2,1,0:T(8,128)(2,1)S(1)}, u32[]{:S(2)}, u32[]{:S(2)}) collective-permute-start(bf16[2,256,512]{2,1,0:T(8,128)(2,1)S(1)} %get-tuple-element.58), channel_id=1, source_target_pairs={{0,1},{1,0},{2,3},{3,2},{4,5},{5,4},{6,7},{7,6},{8,9},{9,8},{10,11... | collective-permute-start | bytes 1572872 | tf_op jit(solution)/shard_map/ppermute | solution.py:607
  103.3 18.0 %collective-permute-start.2 = (bf16[2,256,512]{2,1,0:T(8,128)(2,1)}, bf16[2,256,512]{2,1,0:T(8,128)(2,1)S(1)}, u32[]{:S(2)}, u32[]{:S(2)}) collective-permute-start(bf16[2,256,512]{2,1,0:T(8,128)(2,1)} %get-tuple-element.36), channel_id=1, source_target_pairs={{0,1},{1,0},{2,3},{3,2},{4,5},{5,4},{6,7},{7,6},{8,9},{9,8},{10,11... | collective-permute-start | bytes 1572872 | tf_op jit(solution)/shard_map/ppermute | solution.py:593
  103.9 18.4 %collective-permute-start.1 = (bf16[2,256,512]{2,1,0:T(8,128)(2,1)S(1)}, bf16[2,256,512]{2,1,0:T(8,128)(2,1)S(1)}, u32[]{:S(2)}, u32[]{:S(2)}) collective-permute-start(bf16[2,256,512]{2,1,0:T(8,128)(2,1)S(1)} %add_convert_fusion.7), channel_id=1, source_target_pairs={{0,2},{2,0},{1,3},{3,1},{4,6},{6,4},{5,7},{7,5},{8,10},{10,8},{9,1... | collective-permute-start | bytes 1572872 | tf_op jit(solution)/shard_map/ppermute | solution.py:595
  105.2 0.8 copy-start.5
  106.0 15.3 %copy-start.7 = (bf16[2,256,512]{2,1,0:T(8,128)(2,1)S(1)}, bf16[2,256,512]{2,1,0:T(8,128)(2,1)}, u32[]{:S(2)}) copy-start(bf16[2,256,512]{2,1,0:T(8,128)(2,1)} %get-tuple-element.35) | copy-start | bytes 1572868
  106.0 16.3 %copy-start = (bf16[2,2,256,512]{3,2,1,0:T(8,128)(2,1)S(1)}, bf16[2,2,256,512]{3,2,1,0:T(8,128)(2,1)}, u32[]{:S(2)}) copy-start(bf16[2,2,256,512]{3,2,1,0:T(8,128)(2,1)} %get-tuple-element.28.refs_2_.refs_3_) | copy-start | bytes 3145732
  121.0 2.6 %copy-start.13 = (bf16[2,256,512]{2,1,0:T(8,128)(2,1)S(1)}, bf16[2,256,512]{2,1,0:T(8,128)(2,1)}, u32[]{:S(2)}) copy-start(bf16[2,256,512]{2,1,0:T(8,128)(2,1)} %get-tuple-element.40) | copy-start | bytes 1572868
  121.0 2.6 %collective-permute-start.6 = (bf16[2,256,512]{2,1,0:T(8,128)(2,1)}, bf16[2,256,512]{2,1,0:T(8,128)(2,1)S(1)}, u32[]{:S(2)}, u32[]{:S(2)}) collective-permute-start(bf16[2,256,512]{2,1,0:T(8,128)(2,1)} %get-tuple-element.41), channel_id=1, source_target_pairs={{0,1},{1,0},{2,3},{3,2},{4,5},{5,4},{6,7},{7,6},{8,9},{9,8},{10,11... | collective-permute-start | bytes 1572872 | tf_op jit(solution)/shard_map/ppermute | solution.py:593
  121.4 19.6 %collective-permute-start.3 = (bf16[2,256,512]{2,1,0:T(8,128)(2,1)S(1)}, bf16[2,256,512]{2,1,0:T(8,128)(2,1)S(1)}, u32[]{:S(2)}, u32[]{:S(2)}) collective-permute-start(bf16[2,256,512]{2,1,0:T(8,128)(2,1)S(1)} %add_convert_fusion.6), channel_id=1, source_target_pairs={{0,2},{2,0},{1,3},{3,1},{4,6},{6,4},{5,7},{7,5},{8,10},{10,8},{9,1... | collective-permute-start | bytes 1572872 | tf_op jit(solution)/shard_map/ppermute | solution.py:595
  122.1 3.1 %collective-permute-start.12 = (bf16[2,256,512]{2,1,0:T(8,128)(2,1)S(1)}, bf16[2,256,512]{2,1,0:T(8,128)(2,1)S(1)}, u32[]{:S(2)}, u32[]{:S(2)}) collective-permute-start(bf16[2,256,512]{2,1,0:T(8,128)(2,1)S(1)} %get-tuple-element.57), channel_id=1, source_target_pairs={{0,1},{1,0},{2,3},{3,2},{4,5},{5,4},{6,7},{7,6},{8,9},{9,8},{10,11... | collective-permute-start | bytes 1572872 | tf_op jit(solution)/shard_map/ppermute | solution.py:607
  123.3 25.7 %collective-permute-start.8 = (bf16[2,256,512]{2,1,0:T(8,128)(2,1)S(1)}, bf16[2,256,512]{2,1,0:T(8,128)(2,1)S(1)}, u32[]{:S(2)}, u32[]{:S(2)}) collective-permute-start(bf16[2,256,512]{2,1,0:T(8,128)(2,1)S(1)} %get-tuple-element.56), channel_id=1, source_target_pairs={{0,1},{1,0},{2,3},{3,2},{4,5},{5,4},{6,7},{7,6},{8,9},{9,8},{10,11... | collective-permute-start | bytes 1572872 | tf_op jit(solution)/shard_map/ppermute | solution.py:623
  123.8 23.1 %collective-permute-start.7 = (bf16[2,256,512]{2,1,0:T(8,128)(2,1)S(1)}, bf16[2,256,512]{2,1,0:T(8,128)(2,1)S(1)}, u32[]{:S(2)}, u32[]{:S(2)}) collective-permute-start(bf16[2,256,512]{2,1,0:T(8,128)(2,1)S(1)} %add_convert_fusion.4), channel_id=1, source_target_pairs={{0,2},{2,0},{1,3},{3,1},{4,6},{6,4},{5,7},{7,5},{8,10},{10,8},{9,1... | collective-permute-start | bytes 1572872 | tf_op jit(solution)/shard_map/ppermute | solution.py:595
  125.1 0.8 copy-start.6
  125.9 20.9 %copy-start.4 = (bf16[2,256,512]{2,1,0:T(8,128)(2,1)S(1)}, bf16[2,256,512]{2,1,0:T(8,128)(2,1)}, u32[]{:S(2)}) copy-start(bf16[2,256,512]{2,1,0:T(8,128)(2,1)} %copy-done.3) | copy-start | bytes 1572868
  140.9 7.1 %copy-start.12 = (bf16[2,256,512]{2,1,0:T(8,128)(2,1)S(1)}, bf16[2,256,512]{2,1,0:T(8,128)(2,1)}, u32[]{:S(2)}) copy-start(bf16[2,256,512]{2,1,0:T(8,128)(2,1)} %get-tuple-element.45) | copy-start | bytes 1572868
  140.9 7.1 %collective-permute-start.13 = (bf16[2,256,512]{2,1,0:T(8,128)(2,1)}, bf16[2,256,512]{2,1,0:T(8,128)(2,1)S(1)}, u32[]{:S(2)}, u32[]{:S(2)}) collective-permute-start(bf16[2,256,512]{2,1,0:T(8,128)(2,1)} %get-tuple-element.46), channel_id=1, source_target_pairs={{0,1},{1,0},{2,3},{3,2},{4,5},{5,4},{6,7},{7,6},{8,9},{9,8},{10,11... | collective-permute-start | bytes 1572872 | tf_op jit(solution)/shard_map/ppermute | solution.py:593
  142.2 20.4 %copy-start.2 = (bf16[2,256,512]{2,1,0:T(8,128)(2,1)S(1)}, bf16[2,256,512]{2,1,0:T(8,128)(2,1)}, u32[]{:S(2)}) copy-start(bf16[2,256,512]{2,1,0:T(8,128)(2,1)} %copy-done.1) | copy-start | bytes 1572868
  142.2 7.6 %collective-permute-start.9 = (bf16[2,256,512]{2,1,0:T(8,128)(2,1)}, bf16[2,256,512]{2,1,0:T(8,128)(2,1)S(1)}, u32[]{:S(2)}, u32[]{:S(2)}) collective-permute-start(bf16[2,256,512]{2,1,0:T(8,128)(2,1)} %get-tuple-element.54), channel_id=1, source_target_pairs={{0,1},{1,0},{2,3},{3,2},{4,5},{5,4},{6,7},{7,6},{8,9},{9,8},{10,11... | collective-permute-start | bytes 1572872 | tf_op jit(solution)/shard_map/ppermute | solution.py:623
  148.0 2.7 %collective-permute-start.10 = (bf16[2,256,512]{2,1,0:T(8,128)(2,1)}, bf16[2,256,512]{2,1,0:T(8,128)(2,1)S(1)}, u32[]{:S(2)}, u32[]{:S(2)}) collective-permute-start(bf16[2,256,512]{2,1,0:T(8,128)(2,1)} %get-tuple-element.52), channel_id=1, source_target_pairs={{0,1},{1,0},{2,3},{3,2},{4,5},{5,4},{6,7},{7,6},{8,9},{9,8},{10,11... | collective-permute-start | bytes 1572872 | tf_op jit(solution)/shard_map/ppermute | solution.py:623
  148.2 14.5 %collective-permute-start.14 = (bf16[2,256,512]{2,1,0:T(8,128)(2,1)S(1)}, bf16[2,256,512]{2,1,0:T(8,128)(2,1)}, u32[]{:S(2)}, u32[]{:S(2)}) collective-permute-start(bf16[2,256,512]{2,1,0:T(8,128)(2,1)S(1)} %add_convert_fusion.1), channel_id=1, source_target_pairs={{0,2},{2,0},{1,3},{3,1},{4,6},{6,4},{5,7},{7,5},{8,10},{10,8},{9,1... | collective-permute-start | bytes 1572872 | tf_op jit(solution)/shard_map/ppermute | solution.py:595
  164.7 1.9 %collective-permute-start.15 = (bf16[2,256,512]{2,1,0:T(8,128)(2,1)S(1)}, bf16[2,256,512]{2,1,0:T(8,128)(2,1)S(1)}, u32[]{:S(2)}, u32[]{:S(2)}) collective-permute-start(bf16[2,256,512]{2,1,0:T(8,128)(2,1)S(1)} %get-tuple-element.50), channel_id=1, source_target_pairs={{0,1},{1,0},{2,3},{3,2},{4,5},{5,4},{6,7},{7,6},{8,9},{9,8},{10,11... | collective-permute-start | bytes 1572872 | tf_op jit(solution)/shard_map/ppermute | solution.py:623

commit v4 on v3

--- a/solution.py
+++ b/solution.py
@@ -13,7 +13,7 @@
 ROW_ALIGN = 16
 TILE = 128
 GROUPS = ((0, 1), (2,), (3,))
-LAST = CHUNKS - 1
+LAST = len(GROUPS) - 1
 LISTED = 32
 ACTIVE = 33
 RING = 6
@@ -21,6 +21,10 @@
 F32 = jnp.float32
 BF16 = jnp.bfloat16
 HBM = pl.BlockSpec(memory_space=pl.ANY)
+
+
+def whole(shape):
+    return pl.BlockSpec(shape, lambda *_: (0,) * len(shape))
 
 
 def params(**kw):
@@ -280,10 +284,10 @@
             chip_out(c).start()
 
     def uo_out(c):
-        return pltpu.make_async_copy(u_s.at[0, c], uo_hbm.at[c], out_sem.at[1, c])
+        return pltpu.make_async_copy(u_s.at[0, c], uo_hbm.at[:, span(c), :], out_sem.at[1, c])
 
     def us_out(c):
-        return pltpu.make_async_copy(u_s.at[1, c], us_hbm.at[c], out_sem.at[2, c])
+        return pltpu.make_async_copy(u_s.at[1, c], us_hbm.at[:, span(c), :], out_sem.at[2, c])
 
     def m_whole(c):
         m_across(c).wait_recv()
@@ -363,10 +367,10 @@
     us = refs[2:count_in]
     gff_ref, wr_ref, wg_ref, wu_ref, wd_ref, h_hbm, cv_hbm = refs[count_in:count_in + 7]
     refs = refs[count_in + (9 if g else 7):]
-    outs = refs[:2 * size]
-    ho_hbm, co_hbm = refs[2 * size:count_in]
+    outs = refs[:2]
+    ho_hbm, co_hbm = refs[2:4]
     wg, wu, wd, sems, m_s, hot_s, in_s, out_s, prob_s, h_s, cv_s, st_sem = refs[-12:]
-    _, half, rows, d_model = us[0].shape
+    half, rows, d_model = us[0].shape
     experts = wr_ref.shape[0]
     tokens = 2 * half * rows
     slots = hot_s.shape[0] // size
@@ -399,7 +403,7 @@
             src = us[k * size + j]
             first = j * tokens + jnp.where(core == k, 0, half * rows)
             for s in range(half):
-                u = src[0, s].astype(F32)
+                u = src[s].astype(F32)
                 m = norm_rows(u, gain)
                 m_s[pl.ds(pl.multiple_of(first + s * rows, rows), rows), :] = m.astype(BF16)
 
@@ -468,11 +472,11 @@
         for s in range(half):
             hot = hot_s[j * slots:(j + 1) * slots, pl.ds(pl.multiple_of(first + s * rows, rows), rows)]
             got = lax.dot_general(hot, out_s[j * room:j * room + slots, :], (((0,), (0,)), ((), ())), preferred_element_type=F32)
-            dst[s] = got.astype(BF16)
+            dst[s, j * rows:(j + 1) * rows, :] = got.astype(BF16)
 
     for j in range(size):
         for k in range(2):
-            restore(j, k, outs[k * size + j])
+            restore(j, k, outs[k])
     for cp in pushes:
         cp.wait()
 
@@ -517,8 +521,8 @@
             in_specs=[HBM, HBM, HBM] + [vmem] * 13,
             out_specs=[HBM] * 6,
             out_shape=[
-                jax.ShapeDtypeStruct((WHOLE,) + piece, BF16),
-                jax.ShapeDtypeStruct((WHOLE,) + piece, BF16),
+                jax.ShapeDtypeStruct((half, WHOLE * rows, d_model), BF16),
+                jax.ShapeDtypeStruct((half, WHOLE * rows, d_model), BF16),
                 jax.ShapeDtypeStruct(piece, BF16),
                 jax.ShapeDtypeStruct(piece, BF16),
                 jax.ShapeDtypeStruct((3, batch, inner), BF16),
@@ -568,8 +572,8 @@
                 functools.partial(moe_kernel, g, size),
                 grid=(1,),
                 in_specs=[pl.BlockSpec((1, ACTIVE + 7, 128), lambda i: (g, 0, 0), memory_space=pltpu.SMEM), pl.BlockSpec((size, 1, tokens), lambda i: (first, 0, 0))] + u_specs + [vmem, vmem] + [HBM] * (5 + len(extra)),
-                out_specs=[vmem] * (2 * size) + [HBM, HBM] + ([] if extra else [HBM]),
-                out_shape=[jax.ShapeDtypeStruct(piece, BF16)] * (2 * size) + [jax.ShapeDtypeStruct(h_mid.shape, F32), jax.ShapeDtypeStruct(conv_mid.shape, BF16)] + ([] if extra else [jax.ShapeDtypeStruct(x_steps.shape, BF16)]),
+                out_specs=[vmem] * 2 + [HBM, HBM] + ([] if extra else [HBM]),
+                out_shape=[jax.ShapeDtypeStruct((half, size * rows, d_model), BF16)] * 2 + [jax.ShapeDtypeStruct(h_mid.shape, F32), jax.ShapeDtypeStruct(conv_mid.shape, BF16)] + ([] if extra else [jax.ShapeDtypeStruct(x_steps.shape, BF16)]),
                 scratch_shapes=[
                     pltpu.VMEM((RING, d_model, ffn), BF16),
                     pltpu.VMEM((RING, d_model, ffn), BF16),
@@ -584,7 +588,7 @@
                     pltpu.VMEM((3, size * rows, inner), BF16),
                     pltpu.SemaphoreType.DMA((4,)),
                 ],
-                input_output_aliases={count_in + 7: 2 * size, count_in + 8: 2 * size + 1} if extra else {},
+                input_output_aliases={count_in + 7: 2, count_in + 8: 3} if extra else {},
                 compiler_params=params(),
                 cost_estimate=pl.CostEstimate(flops=int(3e9) * size, bytes_accessed=int(40e6), transcendentals=0),
             )(table, pos, *u_args, g_ff, w_router.T, w_gate, w_up, w_down, h_mid, conv_mid, *extra)
@@ -594,38 +598,30 @@
             chip = (keep.astype(F32) + got.astype(F32)).astype(dtype)
             return chip, lax.ppermute(chip, "tp", across)
 
-        owns = {}
-        spot = {}
-        for c in range(WHOLE):
-            spot[c] = (u_first, u_second, pl.BlockSpec((1,) + piece, lambda i, c=c: (c, 0, 0, 0)))
-            owns[c] = lambda c=c: u_first[c]
+        spot = {c: (u_first, u_second, pl.BlockSpec(piece, lambda i, c=c: (0, c, 0))) for c in range(WHOLE)}
         for c in range(WHOLE, CHUNKS):
             chip = chips[c - WHOLE]
             far = lax.ppermute(chip, "tp", across)
             x_own = lax.dynamic_slice(x_steps, (half * core, c * rows, 0), (half, rows, d_model))
             u_own = (x_own.astype(F32) + (chip.astype(F32) + far.astype(F32))).astype(BF16)
             u_sib = lax.ppermute(u_own, "tp", beside)
-            spot[c] = (u_own[None], u_sib[None], pl.BlockSpec((1,) + piece, lambda i: (0, 0, 0, 0)))
-            owns[c] = lambda u_own=u_own: u_own
+            spot[c] = (u_own, u_sib, whole(piece))
 
         states = None
         pieces = {}
         for g, members in enumerate(GROUPS):
-            size = len(members)
             group = [spot[c] for c in members]
             got = run_moe(g, [v[0] for v in group] + [v[1] for v in group], [v[2] for v in group] * 2, states)
-            states = got[2 * size:2 * size + 2]
+            states = got[2:4]
             if g == 0:
                 y_steps = got[-1]
-            for j, c in enumerate(members):
-                chip, far = both(got[j], got[size + j], BF16)
-                y_own = (owns[c]().astype(F32) + (chip.astype(F32) + far.astype(F32))).astype(BF16)
-                y_sib = lax.ppermute(y_own, "tp", beside)
-                pieces[c] = (y_own, y_sib)
+            chip, far = both(got[0], got[1], BF16)
+            y_own = (group[0][0].astype(F32) + (chip.astype(F32) + far.astype(F32))).astype(BF16)
+            pieces[g] = (y_own, lax.ppermute(y_own, "tp", beside))
         for some in (range(LAST), (LAST,)):
             for k in range(2):
-                for c in some:
-                    y_steps = lax.dynamic_update_slice(y_steps, pieces[c][k], (half * lax.rem(core + k, 2), c * rows, 0))
+                for g in some:
+                    y_steps = lax.dynamic_update_slice(y_steps, pieces[g][k], (half * lax.rem(core + k, 2), GROUPS[g][0] * rows, 0))
         ssm_out, conv_out = states
         ssm_fin = jnp.transpose(ssm_out.reshape(batch, state, inner), (0, 2, 1))
         return y_steps, jnp.transpose(conv_out, (1, 2, 0)), ssm_fin

time: 169 us -> 200 us (1.18)
  waiting for transfers between devices: 18.1 us -> 46.3 us
    ppermute x2, waiting for transfers between devices: 0.01 us -> 23.2 us  [layer_steps(): far = lax.ppermute(chip, 'tp', across)]
    ppermute x4 -> x3, waiting for transfers between devices: 15.3 us -> 21.1 us  [both(): return (chip, lax.ppermute(chip, 'tp', across))]
    convert_element_type x4 -> x3, other arithmetic: 0.54 us -> 2.9 us  [both(): chip = (keep.astype(F32) + got.astype(F32)).astype(dtype)]
    dynamic_update_slice x4 -> x3, other arithmetic: 5.46 us -> 4.82 us  [layer_steps(): lax.dynamic_update_slice(y_steps, pieces[g][k], (half * lax.rem(core + k,...]
  transfers between devices with their start and end apart: 16 -> 13, of which waited for: 4 -> 5; matrix products, arithmetic and copies ran while one was open for 5% -> 5% of each run, Pallas kernels for 38% -> 15%
where the time goes in v4:
time: 200 us; the launch traced here: 198 us
  Pallas kernels  127 us (64%)
  waiting for transfers between devices  46.3 us (23%)
  other arithmetic  9.82 us (5%)
  starting transfers between devices  8.28 us (4%)
  local copies, waits for them, and re-layouts  5.3 us (3%)
    pallas_call x1, Pallas kernels, layer_steps(): pl.pallas_call(mamba_kernel, in_specs=[HBM, HBM, HBM] + [vmem] * 13, out_...  63.5 us
    pallas_call x3, Pallas kernels, run_moe(): pl.pallas_call(functools.partial(moe_kernel, g, size), grid=(1,), in_spec...  61.4 us
    ppermute x2, waiting for transfers between devices, layer_steps(): far = lax.ppermute(chip, 'tp', across)  23.2 us
    ppermute x3, waiting for transfers between devices, both(): return (chip, lax.ppermute(chip, 'tp', across))  21.1 us
    dynamic_update_slice x3, other arithmetic, layer_steps(): lax.dynamic_update_slice(y_steps, pieces[g][k], (half * lax.rem(core + k,...  4.82 us
  transfers between devices with their start and end apart: 13, of which 5 were waited for; matrix products, arithmetic and copies ran while one was open for 5% of the time, Pallas kernels for 15%

profile of v4, /device:TPU:0, one launch (start us, length us, event | category | flops | bytes accessed | tf_op | source)
XLA Modules:
  0.0 197.7 jit_solution(15634381211345420611)
XLA Ops:
  0.6 2.3 %routes.1 = (s32[4,1,1024]{2,1,0:T(1,128)}, s32[3,40,128]{2,1,0:T(8,128)}) custom-call(s32[4,1,1024]{2,1,0:T(1,128)} %bitcast.18), custom_call_target="tpu_custom_call" | custom-call | tf_op jit(solution)/shard_map/routes/pallas_call | solution.py:510
  3.0 63.5 %mamba.1 = (bf16[2,512,512]{2,1,0:T(8,128)(2,1)}, bf16[2,512,512]{2,1,0:T(8,128)(2,1)}, bf16[2,256,512]{2,1,0:T(8,128)(2,1)}, bf16[2,256,512]{2,1,0:T(8,128)(2,1...) custom-call(bf16[4,1024,512]{2,1,0:T(8,128)(2,1)} %x_hbm.1, bf16[3,1024,256]{2,1,0:T(8,128)(2,1)} %bitcast.20, ...), custom_call_target="tpu_custom_call" | custom-call | flops 8000000000 | bytes 45000000 | tf_op jit(solution)/shard_map/mamba/pallas_call | solution.py:519
  66.5 0.0 copy-start.11
  66.5 0.0 copy-start.10
  66.5 31.2 %shard_map.229 = (bf16[2,512,512]{2,1,0:T(8,128)(2,1)}, bf16[2,512,512]{2,1,0:T(8,128)(2,1)}, f32[16384,256]{1,0:T(8,128)}, bf16[3,1024,256]{2,1,0:T(8,128)(2,1)}, bf16[4,1024,512]{2,1,0:T(8,128)(2,1)}) custom-call(s32[3,40,128]{2,1,0:T(8,128)} %get-tuple-element.24.refs_0_, s32[4,1,1024]{2,1,0:T(1,128)} %get-tuple-element.25.refs_1_, ...), custom_call_target="tpu_custom_call" | custom-call | flops 6000000000 | bytes 40000000 | tf_op jit(solution)/shard_map/pallas_call | solution.py:571
  97.7 0.0 copy-start.5
  97.7 1.3 collective-permute-start
  99.0 0.0 copy-done.11
  99.0 0.0 collective-permute-start.8
  99.0 0.0 copy-done.10
  99.0 2.0 %collective-permute-start.2 = (bf16[2,256,512]{2,1,0:T(8,128)(2,1)S(1)}, bf16[2,256,512]{2,1,0:T(8,128)(2,1)}, u32[]{:S(2)}, u32[]{:S(2)}) collective-permute-start(bf16[2,256,512]{2,1,0:T(8,128)(2,1)S(1)} %copy-done.10), channel_id=1, source_target_pairs={{0,2},{2,0},{1,3},{3,1},{4,6},{6,4},{5,7},{7,5},{8,10},{10,8},{9,1... | collective-permute-start | bytes 1572872 | tf_op jit(solution)/shard_map/ppermute | solution.py:604
  101.0 12.9 %collective-permute-done.8 = bf16[2,256,512]{2,1,0:T(8,128)(2,1)} collective-permute-done((bf16[2,256,512]{2,1,0:T(8,128)(2,1)S(1)}, bf16[2,256,512]{2,1,0:T(8,128)(2,1)}, u32[]{:S(2)}, u32[]{:S(2)}) %collective-permute-start.8) | collective-permute-done | bytes 524320 | tf_op jit(solution)/shard_map/ppermute | solution.py:604
  113.9 10.3 %collective-permute-done.2 = bf16[2,256,512]{2,1,0:T(8,128)(2,1)} collective-permute-done((bf16[2,256,512]{2,1,0:T(8,128)(2,1)S(1)}, bf16[2,256,512]{2,1,0:T(8,128)(2,1)}, u32[]{:S(2)}, u32[]{:S(2)}) %collective-permute-start.2) | collective-permute-done | bytes 524320 | tf_op jit(solution)/shard_map/ppermute | solution.py:604
  124.2 2.1 %add_convert_fusion.4 = (bf16[2,256,512]{2,1,0:T(8,128)(2,1)S(1)}, bf16[2,256,512]{2,1,0:T(8,128)(2,1)S(1)}) fusion(bf16[2,256,512]{2,1,0:T(8,128)(2,1)} %collective-permute-done.8, bf16[2,256,512]{2,1,0:T(8,128)(2,1)} %get-tuple-element.38, bf16[4,1024,512]{2,1,0:T(8,128)(2,1)} %x_hbm.1, s32[]{:T(128)S(6)} %select_n.7, ...), kind=kLoop, calls=%fused_computation.4 | loop fusion | flops 3145728 | bytes 4194308 | tf_op jit(solution)/shard_map/convert_element_type | solution.py:606
  126.3 0.0 copy-start.3
  126.3 0.0 copy-start.1
  126.4 0.0 collective-permute-start.3
  126.4 0.5 collective-permute-start.9
  126.9 0.0 collective-permute-done
  126.9 1.0 copy-done.6
  127.9 0.0 copy-done.5
  127.9 1.5 add_convert_fusion.1
  129.4 0.3 collective-permute-start.1
  129.7 0.0 collective-permute-done.3.refs_3_
  129.7 0.0 copy-done.3
  129.7 0.8 copy-done.8
  130.5 14.9 %shard_map.230 = (bf16[2,256,512]{2,1,0:T(8,128)(2,1)}, bf16[2,256,512]{2,1,0:T(8,128)(2,1)}, f32[16384,256]{1,0:T(8,128)}, bf16[3,1024,256]{2,1,0:T(8,128)(2,1)}) custom-call(s32[3,40,128]{2,1,0:T(8,128)} %get-tuple-element.24.refs_0_, s32[4,1,1024]{2,1,0:T(1,128)} %get-tuple-element.25.refs_1_, ...), custom_call_target="tpu_custom_call", output_to_operand_aliasing={{2}: (11, {}), {3}: (12, {})} | custom-call | flops 3000000000 | bytes 40000000 | tf_op jit(solution)/shard_map/pallas_call | solution.py:571
  145.4 0.0 copy-done.1
  145.4 0.0 collective-permute-start.4
  145.5 0.0 collective-permute-done.9.refs_3_
  145.5 0.0 copy-start.7
  145.5 0.8 copy-done.7
  146.3 15.3 %shard_map.231 = (bf16[2,256,512]{2,1,0:T(8,128)(2,1)}, bf16[2,256,512]{2,1,0:T(8,128)(2,1)}, f32[16384,256]{1,0:T(8,128)}, bf16[3,1024,256]{2,1,0:T(8,128)(2,1)}) custom-call(s32[3,40,128]{2,1,0:T(8,128)} %get-tuple-element.24.refs_0_, s32[4,1,1024]{2,1,0:T(1,128)} %get-tuple-element.25.refs_1_, ...), custom_call_target="tpu_custom_call", output_to_operand_aliasing={{2}: (11, {}), {3}: (12, {})} | custom-call | flops 3000000000 | bytes 40000000 | tf_op jit(solution)/shard_map/pallas_call | solution.py:571
  161.6 0.0 copy-start.13
  161.7 0.0 copy-start.4
  161.7 0.0 collective-permute-done.4
  161.7 0.0 copy-done.12
  161.7 1.3 add_convert_fusion.6
  162.9 0.0 copy-start.9
  163.0 1.8 collective-permute-start.5
  164.7 0.0 collective-permute-done.1
  164.7 0.0 copy-done
  164.7 1.8 constant_dynamic-update-slice_fusion.5
  166.5 0.2 collective-permute-start.6
  166.7 0.0 copy-done.13
  166.7 0.3 collective-permute-start.10
  167.0 10.3 %collective-permute-done.5 = bf16[2,256,512]{2,1,0:T(8,128)(2,1)S(1)} collective-permute-done((bf16[2,256,512]{2,1,0:T(8,128)(2,1)S(1)}, bf16[2,256,512]{2,1,0:T(8,128)(2,1)S(1)}, u32[]{:S(2)}, u32[]{:S(2)}) %collective-permute-start.5) | collective-permute-done | bytes 524320 | tf_op jit(solution)/shard_map/ppermute | solution.py:599
  177.3 0.0 copy-done.4
  177.3 1.0 constant_dynamic-update-slice_fusion.4
  178.3 0.0 collective-permute-start.7
  178.3 0.0 collective-permute-done.10
  178.3 0.0 copy-done.9
  178.3 0.1 add_convert_fusion.3
  178.5 1.8 collective-permute-start.11
  180.3 0.0 collective-permute-done.6
  180.3 1.0 constant_dynamic-update-slice_fusion.3
  181.3 0.0 collective-permute-done.7
  181.3 0.8 constant_dynamic-update-slice_fusion.2
  182.1 10.8 %collective-permute-done.11 = bf16[2,256,512]{2,1,0:T(8,128)(2,1)} collective-permute-done((bf16[2,256,512]{2,1,0:T(8,128)(2,1)S(1)}, bf16[2,256,512]{2,1,0:T(8,128)(2,1)}, u32[]{:S(2)}, u32[]{:S(2)}) %collective-permute-start.11) | collective-permute-done | bytes 524320 | tf_op jit(solution)/shard_map/ppermute | solution.py:599
  193.0 0.0 copy-done.2
  193.0 2.0 %constant_dynamic-update-slice_fusion.1 = (bf16[4,1024,512]{2,1,0:T(8,128)(2,1)}, bf16[2,256,512]{2,1,0:T(8,128)(2,1)S(1)}) fusion(bf16[4,1024,512]{2,1,0:T(8,128)(2,1)} %constant_dynamic-update-slice_fusion.2, s32[]{:T(128)S(6)} %select_n.6, bf16[2,256,512]{2,1,0:T(8,128)(2,1)} %collective-permute-done.11, bf16[2,256,512]{2,1,0:T(8,128)(2,1)S(1)} %add_convert_fusion.3, ...), kind=kLoop, calls=%fused_computation.9 | loop fusion | flops 1572864 | bytes 2621444 | tf_op jit(solution)/shard_map/dynamic_update_slice | solution.py:624
  195.0 0.0 collective-permute-start.12
  195.0 1.9 collective-permute-done.12
  196.9 0.8 constant_dynamic-update-slice_fusion
  (5 shorter events, 0.0 us)
Async XLA Ops:
  66.5 32.5 %copy-start.11 = (bf16[2,256,512]{2,1,0:T(8,128)(2,1)S(1)}, bf16[2,256,512]{2,1,0:T(8,128)(2,1)}, u32[]{:S(2)}) copy-start(bf16[2,256,512]{2,1,0:T(8,128)(2,1)} %get-tuple-element.38) | copy-start | bytes 1572868
  66.5 32.5 %copy-start.10 = (bf16[2,256,512]{2,1,0:T(8,128)(2,1)S(1)}, bf16[2,256,512]{2,1,0:T(8,128)(2,1)}, u32[]{:S(2)}) copy-start(bf16[2,256,512]{2,1,0:T(8,128)(2,1)} %get-tuple-element.33) | copy-start | bytes 1572868
  97.7 30.2 %copy-start.5 = (bf16[2,512,512]{2,1,0:T(8,128)(2,1)S(1)}, bf16[2,512,512]{2,1,0:T(8,128)(2,1)}, u32[]{:S(2)}) copy-start(bf16[2,512,512]{2,1,0:T(8,128)(2,1)} %get-tuple-element.31) | copy-start | bytes 3145732
  97.7 29.2 %collective-permute-start = (bf16[2,512,512]{2,1,0:T(8,128)(2,1)}, bf16[2,512,512]{2,1,0:T(8,128)(2,1)S(1)}, u32[]{:S(2)}, u32[]{:S(2)}) collective-permute-start(bf16[2,512,512]{2,1,0:T(8,128)(2,1)} %get-tuple-element.32), channel_id=1, source_target_pairs={{0,1},{1,0},{2,3},{3,2},{4,5},{5,4},{6,7},{7,6},{8,9},{9,8},{10,11... | collective-permute-start | bytes 3145736 | tf_op jit(solution)/shard_map/ppermute | solution.py:597
  99.0 14.9 %collective-permute-start.8 = (bf16[2,256,512]{2,1,0:T(8,128)(2,1)S(1)}, bf16[2,256,512]{2,1,0:T(8,128)(2,1)}, u32[]{:S(2)}, u32[]{:S(2)}) collective-permute-start(bf16[2,256,512]{2,1,0:T(8,128)(2,1)S(1)} %copy-done.11), channel_id=1, source_target_pairs={{0,2},{2,0},{1,3},{3,1},{4,6},{6,4},{5,7},{7,5},{8,10},{10,8},{9,1... | collective-permute-start | bytes 1572872 | tf_op jit(solution)/shard_map/ppermute | solution.py:604
  99.0 25.2 %collective-permute-start.2 = (bf16[2,256,512]{2,1,0:T(8,128)(2,1)S(1)}, bf16[2,256,512]{2,1,0:T(8,128)(2,1)}, u32[]{:S(2)}, u32[]{:S(2)}) collective-permute-start(bf16[2,256,512]{2,1,0:T(8,128)(2,1)S(1)} %copy-done.10), channel_id=1, source_target_pairs={{0,2},{2,0},{1,3},{3,1},{4,6},{6,4},{5,7},{7,5},{8,10},{10,8},{9,1... | collective-permute-start | bytes 1572872 | tf_op jit(solution)/shard_map/ppermute | solution.py:604
  126.3 3.4 %copy-start.3 = (bf16[2,256,512]{2,1,0:T(8,128)(2,1)}, bf16[2,256,512]{2,1,0:T(8,128)(2,1)S(1)}, u32[]{:S(2)}) copy-start(bf16[2,256,512]{2,1,0:T(8,128)(2,1)S(1)} %get-tuple-element.52.refs_2_) | copy-start | bytes 1572868
  126.3 19.1 %copy-start.1 = (bf16[2,256,512]{2,1,0:T(8,128)(2,1)}, bf16[2,256,512]{2,1,0:T(8,128)(2,1)S(1)}, u32[]{:S(2)}) copy-start(bf16[2,256,512]{2,1,0:T(8,128)(2,1)S(1)} %get-tuple-element.51.refs_2_) | copy-start | bytes 1572868
  126.4 3.4 %collective-permute-start.3 = (bf16[2,256,512]{2,1,0:T(8,128)(2,1)S(1)}, bf16[2,256,512]{2,1,0:T(8,128)(2,1)S(1)}, u32[]{:S(2)}, u32[]{:S(2)}) collective-permute-start(bf16[2,256,512]{2,1,0:T(8,128)(2,1)S(1)} %get-tuple-element.52.refs_2_), channel_id=1, source_target_pairs={{0,1},{1,0},{2,3},{3,2},{4,5},{5,4},{6,7},{7,6},{8,9},{9,8},{10,11... | collective-permute-start | bytes 1572872 | tf_op jit(solution)/shard_map/ppermute | solution.py:607
  126.4 19.1 %collective-permute-start.9 = (bf16[2,256,512]{2,1,0:T(8,128)(2,1)S(1)}, bf16[2,256,512]{2,1,0:T(8,128)(2,1)S(1)}, u32[]{:S(2)}, u32[]{:S(2)}) collective-permute-start(bf16[2,256,512]{2,1,0:T(8,128)(2,1)S(1)} %get-tuple-element.51.refs_2_), channel_id=1, source_target_pairs={{0,1},{1,0},{2,3},{3,2},{4,5},{5,4},{6,7},{7,6},{8,9},{9,8},{10,11... | collective-permute-start | bytes 1572872 | tf_op jit(solution)/shard_map/ppermute | solution.py:607
  126.9 1.0 copy-start.6
  129.4 35.3 %collective-permute-start.1 = (bf16[2,512,512]{2,1,0:T(8,128)(2,1)S(1)}, bf16[2,512,512]{2,1,0:T(8,128)(2,1)S(1)}, u32[]{:S(2)}, u32[]{:S(2)}) collective-permute-start(bf16[2,512,512]{2,1,0:T(8,128)(2,1)S(1)} %add_convert_fusion.1), channel_id=1, source_target_pairs={{0,2},{2,0},{1,3},{3,1},{4,6},{6,4},{5,7},{7,5},{8,10},{10,8},{9,1... | collective-permute-start | bytes 3145736 | tf_op jit(solution)/shard_map/ppermute | solution.py:599
  129.7 0.8 copy-start.8
  145.4 16.2 %collective-permute-start.4 = (bf16[2,256,512]{2,1,0:T(8,128)(2,1)}, bf16[2,256,512]{2,1,0:T(8,128)(2,1)}, u32[]{:S(2)}, u32[]{:S(2)}) collective-permute-start(bf16[2,256,512]{2,1,0:T(8,128)(2,1)} %get-tuple-element.37), channel_id=1, source_target_pairs={{0,1},{1,0},{2,3},{3,2},{4,5},{5,4},{6,7},{7,6},{8,9},{9,8},{10,11... | collective-permute-start | bytes 1572872 | tf_op jit(solution)/shard_map/ppermute | solution.py:597
  145.5 0.8 copy-start.7
  146.3 15.4 %copy-start.12 = (bf16[2,256,512]{2,1,0:T(8,128)(2,1)S(1)}, bf16[2,256,512]{2,1,0:T(8,128)(2,1)}, u32[]{:S(2)}) copy-start(bf16[2,256,512]{2,1,0:T(8,128)(2,1)} %get-tuple-element.36) | copy-start | bytes 1572868
  146.3 18.4 %copy-start = (bf16[2,512,512]{2,1,0:T(8,128)(2,1)S(1)}, bf16[2,512,512]{2,1,0:T(8,128)(2,1)}, u32[]{:S(2)}) copy-start(bf16[2,512,512]{2,1,0:T(8,128)(2,1)} %get-tuple-element.26.refs_2_.refs_3_) | copy-start | bytes 3145732
  161.6 5.1 %copy-start.13 = (bf16[2,256,512]{2,1,0:T(8,128)(2,1)S(1)}, bf16[2,256,512]{2,1,0:T(8,128)(2,1)}, u32[]{:S(2)}) copy-start(bf16[2,256,512]{2,1,0:T(8,128)(2,1)} %get-tuple-element.42) | copy-start | bytes 1572868
  161.7 15.7 %copy-start.4 = (bf16[2,256,512]{2,1,0:T(8,128)(2,1)S(1)}, bf16[2,256,512]{2,1,0:T(8,128)(2,1)}, u32[]{:S(2)}) copy-start(bf16[2,256,512]{2,1,0:T(8,128)(2,1)} %copy-done.3) | copy-start | bytes 1572868
  162.9 15.4 %copy-start.9 = (bf16[2,256,512]{2,1,0:T(8,128)(2,1)S(1)}, bf16[2,256,512]{2,1,0:T(8,128)(2,1)}, u32[]{:S(2)}) copy-start(bf16[2,256,512]{2,1,0:T(8,128)(2,1)} %get-tuple-element.41) | copy-start | bytes 1572868
  163.0 14.4 %collective-permute-start.5 = (bf16[2,256,512]{2,1,0:T(8,128)(2,1)S(1)}, bf16[2,256,512]{2,1,0:T(8,128)(2,1)S(1)}, u32[]{:S(2)}, u32[]{:S(2)}) collective-permute-start(bf16[2,256,512]{2,1,0:T(8,128)(2,1)S(1)} %add_convert_fusion.6), channel_id=1, source_target_pairs={{0,2},{2,0},{1,3},{3,1},{4,6},{6,4},{5,7},{7,5},{8,10},{10,8},{9,1... | collective-permute-start | bytes 1572872 | tf_op jit(solution)/shard_map/ppermute | solution.py:599
  166.5 26.5 %copy-start.2 = (bf16[2,256,512]{2,1,0:T(8,128)(2,1)S(1)}, bf16[2,256,512]{2,1,0:T(8,128)(2,1)}, u32[]{:S(2)}) copy-start(bf16[2,256,512]{2,1,0:T(8,128)(2,1)} %copy-done.1) | copy-start | bytes 1572868
  166.5 13.8 %collective-permute-start.6 = (bf16[2,512,512]{2,1,0:T(8,128)(2,1)}, bf16[2,512,512]{2,1,0:T(8,128)(2,1)S(1)}, u32[]{:S(2)}, u32[]{:S(2)}) collective-permute-start(bf16[2,512,512]{2,1,0:T(8,128)(2,1)} %get-tuple-element.50), channel_id=1, source_target_pairs={{0,1},{1,0},{2,3},{3,2},{4,5},{5,4},{6,7},{7,6},{8,9},{9,8},{10,11... | collective-permute-start | bytes 3145736 | tf_op jit(solution)/shard_map/ppermute | solution.py:620
  166.7 11.6 %collective-permute-start.10 = (bf16[2,256,512]{2,1,0:T(8,128)(2,1)S(1)}, bf16[2,256,512]{2,1,0:T(8,128)(2,1)S(1)}, u32[]{:S(2)}, u32[]{:S(2)}) collective-permute-start(bf16[2,256,512]{2,1,0:T(8,128)(2,1)S(1)} %copy-done.13), channel_id=1, source_target_pairs={{0,1},{1,0},{2,3},{3,2},{4,5},{5,4},{6,7},{7,6},{8,9},{9,8},{10,11... | collective-permute-start | bytes 1572872 | tf_op jit(solution)/shard_map/ppermute | solution.py:597
  178.3 3.0 %collective-permute-start.7 = (bf16[2,256,512]{2,1,0:T(8,128)(2,1)S(1)}, bf16[2,256,512]{2,1,0:T(8,128)(2,1)S(1)}, u32[]{:S(2)}, u32[]{:S(2)}) collective-permute-start(bf16[2,256,512]{2,1,0:T(8,128)(2,1)S(1)} %get-tuple-element.48), channel_id=1, source_target_pairs={{0,1},{1,0},{2,3},{3,2},{4,5},{5,4},{6,7},{7,6},{8,9},{9,8},{10,11... | collective-permute-start | bytes 1572872 | tf_op jit(solution)/shard_map/ppermute | solution.py:620
  178.5 14.5 %collective-permute-start.11 = (bf16[2,256,512]{2,1,0:T(8,128)(2,1)S(1)}, bf16[2,256,512]{2,1,0:T(8,128)(2,1)}, u32[]{:S(2)}, u32[]{:S(2)}) collective-permute-start(bf16[2,256,512]{2,1,0:T(8,128)(2,1)S(1)} %add_convert_fusion.3), channel_id=1, source_target_pairs={{0,2},{2,0},{1,3},{3,1},{4,6},{6,4},{5,7},{7,5},{8,10},{10,8},{9,1... | collective-permute-start | bytes 1572872 | tf_op jit(solution)/shard_map/ppermute | solution.py:599
  195.0 1.9 collective-permute-start.12

commit v5 on v4

--- a/solution.py
+++ b/solution.py
@@ -12,6 +12,7 @@
 CHUNKS = 4
 ROW_ALIGN = 16
 TILE = 128
+FEW = 32
 GROUPS = ((0, 1), (2,), (3,))
 LAST = len(GROUPS) - 1
 LISTED = 32
@@ -457,9 +458,11 @@
 
             lax.fori_loop(0, big, tile, 0)
 
-            @pl.when(count > big * (2 * TILE))
-            def _():
-                feed(e, slot, pl.multiple_of(start + big * (2 * TILE), ROW_ALIGN), TILE)
+            left = count - big * (2 * TILE)
+            for most, least in ((TILE, FEW), (FEW, 0)):
+                @pl.when((left > least) & (left <= most))
+                def _():
+                    feed(e, slot, pl.multiple_of(start + big * (2 * TILE), ROW_ALIGN), most)
 
             return c1
 

time: 200 us -> 198 us (0.990)
  no operation moved by 1% of the time
where the time goes in v5:
time: 198 us; the launch traced here: 197 us
  Pallas kernels  126 us (64%)
  waiting for transfers between devices  46.3 us (23%)
  other arithmetic  9.82 us (5%)
  starting transfers between devices  8.31 us (4%)
  local copies, waits for them, and re-layouts  5.3 us (3%)
    pallas_call x1, Pallas kernels, layer_steps(): pl.pallas_call(mamba_kernel, in_specs=[HBM, HBM, HBM] + [vmem] * 13, out_...  63.5 us
    pallas_call x3, Pallas kernels, run_moe(): pl.pallas_call(functools.partial(moe_kernel, g, size), grid=(1,), in_spec...  60.6 us
    ppermute x2, waiting for transfers between devices, layer_steps(): far = lax.ppermute(chip, 'tp', across)  23.2 us
    ppermute x3, waiting for transfers between devices, both(): return (chip, lax.ppermute(chip, 'tp', across))  21.1 us
    dynamic_update_slice x3, other arithmetic, layer_steps(): lax.dynamic_update_slice(y_steps, pieces[g][k], (half * lax.rem(core + k,...  4.82 us
  transfers between devices with their start and end apart: 13, of which 5 were waited for; matrix products, arithmetic and copies ran while one was open for 5% of the time, Pallas kernels for 15%

profile of v5, /device:TPU:0, one launch (start us, length us, event | category | flops | bytes accessed | tf_op | source)
XLA Modules:
  0.0 196.9 jit_solution(11006307276514311564)
XLA Ops:
  0.6 2.3 %routes.1 = (s32[4,1,1024]{2,1,0:T(1,128)}, s32[3,40,128]{2,1,0:T(8,128)}) custom-call(s32[4,1,1024]{2,1,0:T(1,128)} %bitcast.18), custom_call_target="tpu_custom_call" | custom-call | tf_op jit(solution)/shard_map/routes/pallas_call | solution.py:513
  3.0 63.5 %mamba.1 = (bf16[2,512,512]{2,1,0:T(8,128)(2,1)}, bf16[2,512,512]{2,1,0:T(8,128)(2,1)}, bf16[2,256,512]{2,1,0:T(8,128)(2,1)}, bf16[2,256,512]{2,1,0:T(8,128)(2,1...) custom-call(bf16[4,1024,512]{2,1,0:T(8,128)(2,1)} %x_hbm.1, bf16[3,1024,256]{2,1,0:T(8,128)(2,1)} %bitcast.20, ...), custom_call_target="tpu_custom_call" | custom-call | flops 8000000000 | bytes 45000000 | tf_op jit(solution)/shard_map/mamba/pallas_call | solution.py:522
  66.5 0.0 copy-start.11
  66.5 0.0 copy-start.10
  66.5 30.7 %shard_map.229 = (bf16[2,512,512]{2,1,0:T(8,128)(2,1)}, bf16[2,512,512]{2,1,0:T(8,128)(2,1)}, f32[16384,256]{1,0:T(8,128)}, bf16[3,1024,256]{2,1,0:T(8,128)(2,1)}, bf16[4,1024,512]{2,1,0:T(8,128)(2,1)}) custom-call(s32[3,40,128]{2,1,0:T(8,128)} %get-tuple-element.24.refs_0_, s32[4,1,1024]{2,1,0:T(1,128)} %get-tuple-element.25.refs_1_, ...), custom_call_target="tpu_custom_call" | custom-call | flops 6000000000 | bytes 40000000 | tf_op jit(solution)/shard_map/pallas_call | solution.py:574
  97.2 0.0 copy-start.5
  97.2 1.3 collective-permute-start
  98.5 0.0 copy-done.11
  98.5 0.0 collective-permute-start.8
  98.5 0.0 copy-done.10
  98.5 2.0 %collective-permute-start.2 = (bf16[2,256,512]{2,1,0:T(8,128)(2,1)S(1)}, bf16[2,256,512]{2,1,0:T(8,128)(2,1)}, u32[]{:S(2)}, u32[]{:S(2)}) collective-permute-start(bf16[2,256,512]{2,1,0:T(8,128)(2,1)S(1)} %copy-done.10), channel_id=1, source_target_pairs={{0,2},{2,0},{1,3},{3,1},{4,6},{6,4},{5,7},{7,5},{8,10},{10,8},{9,1... | collective-permute-start | bytes 1572872 | tf_op jit(solution)/shard_map/ppermute | solution.py:607
  100.6 12.9 %collective-permute-done.8 = bf16[2,256,512]{2,1,0:T(8,128)(2,1)} collective-permute-done((bf16[2,256,512]{2,1,0:T(8,128)(2,1)S(1)}, bf16[2,256,512]{2,1,0:T(8,128)(2,1)}, u32[]{:S(2)}, u32[]{:S(2)}) %collective-permute-start.8) | collective-permute-done | bytes 524320 | tf_op jit(solution)/shard_map/ppermute | solution.py:607
  113.4 10.3 %collective-permute-done.2 = bf16[2,256,512]{2,1,0:T(8,128)(2,1)} collective-permute-done((bf16[2,256,512]{2,1,0:T(8,128)(2,1)S(1)}, bf16[2,256,512]{2,1,0:T(8,128)(2,1)}, u32[]{:S(2)}, u32[]{:S(2)}) %collective-permute-start.2) | collective-permute-done | bytes 524320 | tf_op jit(solution)/shard_map/ppermute | solution.py:607
  123.8 2.1 %add_convert_fusion.4 = (bf16[2,256,512]{2,1,0:T(8,128)(2,1)S(1)}, bf16[2,256,512]{2,1,0:T(8,128)(2,1)S(1)}) fusion(bf16[2,256,512]{2,1,0:T(8,128)(2,1)} %collective-permute-done.8, bf16[2,256,512]{2,1,0:T(8,128)(2,1)} %get-tuple-element.38, bf16[4,1024,512]{2,1,0:T(8,128)(2,1)} %x_hbm.1, s32[]{:T(128)S(6)} %select_n.7, ...), kind=kLoop, calls=%fused_computation.4 | loop fusion | flops 3145728 | bytes 4194308 | tf_op jit(solution)/shard_map/convert_element_type | solution.py:609
  125.9 0.0 copy-start.3
  125.9 0.0 copy-start.1
  125.9 0.0 collective-permute-start.3
  125.9 0.5 collective-permute-start.9
  126.4 0.0 collective-permute-done
  126.4 1.0 copy-done.6
  127.4 0.0 copy-done.5
  127.4 1.5 add_convert_fusion.1
  128.9 0.3 collective-permute-start.1
  129.3 0.0 collective-permute-done.3.refs_3_
  129.3 0.0 copy-done.3
  129.3 0.8 copy-done.8
  130.0 14.8 %shard_map.230 = (bf16[2,256,512]{2,1,0:T(8,128)(2,1)}, bf16[2,256,512]{2,1,0:T(8,128)(2,1)}, f32[16384,256]{1,0:T(8,128)}, bf16[3,1024,256]{2,1,0:T(8,128)(2,1)}) custom-call(s32[3,40,128]{2,1,0:T(8,128)} %get-tuple-element.24.refs_0_, s32[4,1,1024]{2,1,0:T(1,128)} %get-tuple-element.25.refs_1_, ...), custom_call_target="tpu_custom_call", output_to_operand_aliasing={{2}: (11, {}), {3}: (12, {})} | custom-call | flops 3000000000 | bytes 40000000 | tf_op jit(solution)/shard_map/pallas_call | solution.py:574
  144.8 0.0 copy-done.1
  144.8 0.0 collective-permute-start.4
  144.9 0.0 collective-permute-done.9.refs_3_
  144.9 0.0 copy-start.7
  144.9 0.8 copy-done.7
  145.7 15.1 %shard_map.231 = (bf16[2,256,512]{2,1,0:T(8,128)(2,1)}, bf16[2,256,512]{2,1,0:T(8,128)(2,1)}, f32[16384,256]{1,0:T(8,128)}, bf16[3,1024,256]{2,1,0:T(8,128)(2,1)}) custom-call(s32[3,40,128]{2,1,0:T(8,128)} %get-tuple-element.24.refs_0_, s32[4,1,1024]{2,1,0:T(1,128)} %get-tuple-element.25.refs_1_, ...), custom_call_target="tpu_custom_call", output_to_operand_aliasing={{2}: (11, {}), {3}: (12, {})} | custom-call | flops 3000000000 | bytes 40000000 | tf_op jit(solution)/shard_map/pallas_call | solution.py:574
  160.8 0.0 copy-start.13
  160.8 0.0 copy-start.4
  160.8 0.0 collective-permute-done.4
  160.9 0.0 copy-done.12
  160.9 1.3 add_convert_fusion.6
  162.1 0.0 copy-start.9
  162.1 1.8 collective-permute-start.5
  163.9 0.0 collective-permute-done.1
  163.9 0.0 copy-done
  163.9 1.8 constant_dynamic-update-slice_fusion.5
  165.7 0.2 collective-permute-start.6
  165.9 0.0 copy-done.13
  165.9 0.3 collective-permute-start.10
  166.2 10.3 %collective-permute-done.5 = bf16[2,256,512]{2,1,0:T(8,128)(2,1)S(1)} collective-permute-done((bf16[2,256,512]{2,1,0:T(8,128)(2,1)S(1)}, bf16[2,256,512]{2,1,0:T(8,128)(2,1)S(1)}, u32[]{:S(2)}, u32[]{:S(2)}) %collective-permute-start.5) | collective-permute-done | bytes 524320 | tf_op jit(solution)/shard_map/ppermute | solution.py:602
  176.5 0.0 copy-done.4
  176.5 1.0 constant_dynamic-update-slice_fusion.4
  177.5 0.0 collective-permute-start.7
  177.5 0.0 collective-permute-done.10
  177.5 0.0 copy-done.9
  177.5 0.1 add_convert_fusion.3
  177.7 1.8 collective-permute-start.11
  179.5 0.0 collective-permute-done.6
  179.5 1.0 constant_dynamic-update-slice_fusion.3
  180.5 0.0 collective-permute-done.7
  180.5 0.8 constant_dynamic-update-slice_fusion.2
  181.3 10.8 %collective-permute-done.11 = bf16[2,256,512]{2,1,0:T(8,128)(2,1)} collective-permute-done((bf16[2,256,512]{2,1,0:T(8,128)(2,1)S(1)}, bf16[2,256,512]{2,1,0:T(8,128)(2,1)}, u32[]{:S(2)}, u32[]{:S(2)}) %collective-permute-start.11) | collective-permute-done | bytes 524320 | tf_op jit(solution)/shard_map/ppermute | solution.py:602
  192.2 0.0 copy-done.2
  192.2 2.0 %constant_dynamic-update-slice_fusion.1 = (bf16[4,1024,512]{2,1,0:T(8,128)(2,1)}, bf16[2,256,512]{2,1,0:T(8,128)(2,1)S(1)}) fusion(bf16[4,1024,512]{2,1,0:T(8,128)(2,1)} %constant_dynamic-update-slice_fusion.2, s32[]{:T(128)S(6)} %select_n.6, bf16[2,256,512]{2,1,0:T(8,128)(2,1)} %collective-permute-done.11, bf16[2,256,512]{2,1,0:T(8,128)(2,1)S(1)} %add_convert_fusion.3, ...), kind=kLoop, calls=%fused_computation.9 | loop fusion | flops 1572864 | bytes 2621444 | tf_op jit(solution)/shard_map/dynamic_update_slice | solution.py:627
  194.2 0.0 collective-permute-start.12
  194.2 1.9 collective-permute-done.12
  196.1 0.8 constant_dynamic-update-slice_fusion
  (5 shorter events, 0.0 us)
Async XLA Ops:
  66.5 32.1 %copy-start.11 = (bf16[2,256,512]{2,1,0:T(8,128)(2,1)S(1)}, bf16[2,256,512]{2,1,0:T(8,128)(2,1)}, u32[]{:S(2)}) copy-start(bf16[2,256,512]{2,1,0:T(8,128)(2,1)} %get-tuple-element.38) | copy-start | bytes 1572868
  66.5 32.1 %copy-start.10 = (bf16[2,256,512]{2,1,0:T(8,128)(2,1)S(1)}, bf16[2,256,512]{2,1,0:T(8,128)(2,1)}, u32[]{:S(2)}) copy-start(bf16[2,256,512]{2,1,0:T(8,128)(2,1)} %get-tuple-element.33) | copy-start | bytes 1572868
  97.2 30.2 %copy-start.5 = (bf16[2,512,512]{2,1,0:T(8,128)(2,1)S(1)}, bf16[2,512,512]{2,1,0:T(8,128)(2,1)}, u32[]{:S(2)}) copy-start(bf16[2,512,512]{2,1,0:T(8,128)(2,1)} %get-tuple-element.31) | copy-start | bytes 3145732
  97.2 29.2 %collective-permute-start = (bf16[2,512,512]{2,1,0:T(8,128)(2,1)}, bf16[2,512,512]{2,1,0:T(8,128)(2,1)S(1)}, u32[]{:S(2)}, u32[]{:S(2)}) collective-permute-start(bf16[2,512,512]{2,1,0:T(8,128)(2,1)} %get-tuple-element.32), channel_id=1, source_target_pairs={{0,1},{1,0},{2,3},{3,2},{4,5},{5,4},{6,7},{7,6},{8,9},{9,8},{10,11... | collective-permute-start | bytes 3145736 | tf_op jit(solution)/shard_map/ppermute | solution.py:600
  98.5 14.9 %collective-permute-start.8 = (bf16[2,256,512]{2,1,0:T(8,128)(2,1)S(1)}, bf16[2,256,512]{2,1,0:T(8,128)(2,1)}, u32[]{:S(2)}, u32[]{:S(2)}) collective-permute-start(bf16[2,256,512]{2,1,0:T(8,128)(2,1)S(1)} %copy-done.11), channel_id=1, source_target_pairs={{0,2},{2,0},{1,3},{3,1},{4,6},{6,4},{5,7},{7,5},{8,10},{10,8},{9,1... | collective-permute-start | bytes 1572872 | tf_op jit(solution)/shard_map/ppermute | solution.py:607
  98.5 25.2 %collective-permute-start.2 = (bf16[2,256,512]{2,1,0:T(8,128)(2,1)S(1)}, bf16[2,256,512]{2,1,0:T(8,128)(2,1)}, u32[]{:S(2)}, u32[]{:S(2)}) collective-permute-start(bf16[2,256,512]{2,1,0:T(8,128)(2,1)S(1)} %copy-done.10), channel_id=1, source_target_pairs={{0,2},{2,0},{1,3},{3,1},{4,6},{6,4},{5,7},{7,5},{8,10},{10,8},{9,1... | collective-permute-start | bytes 1572872 | tf_op jit(solution)/shard_map/ppermute | solution.py:607
  125.9 3.4 %copy-start.3 = (bf16[2,256,512]{2,1,0:T(8,128)(2,1)}, bf16[2,256,512]{2,1,0:T(8,128)(2,1)S(1)}, u32[]{:S(2)}) copy-start(bf16[2,256,512]{2,1,0:T(8,128)(2,1)S(1)} %get-tuple-element.52.refs_2_) | copy-start | bytes 1572868
  125.9 19.0 %copy-start.1 = (bf16[2,256,512]{2,1,0:T(8,128)(2,1)}, bf16[2,256,512]{2,1,0:T(8,128)(2,1)S(1)}, u32[]{:S(2)}) copy-start(bf16[2,256,512]{2,1,0:T(8,128)(2,1)S(1)} %get-tuple-element.51.refs_2_) | copy-start | bytes 1572868
  125.9 3.4 %collective-permute-start.3 = (bf16[2,256,512]{2,1,0:T(8,128)(2,1)S(1)}, bf16[2,256,512]{2,1,0:T(8,128)(2,1)S(1)}, u32[]{:S(2)}, u32[]{:S(2)}) collective-permute-start(bf16[2,256,512]{2,1,0:T(8,128)(2,1)S(1)} %get-tuple-element.52.refs_2_), channel_id=1, source_target_pairs={{0,1},{1,0},{2,3},{3,2},{4,5},{5,4},{6,7},{7,6},{8,9},{9,8},{10,11... | collective-permute-start | bytes 1572872 | tf_op jit(solution)/shard_map/ppermute | solution.py:610
  125.9 19.0 %collective-permute-start.9 = (bf16[2,256,512]{2,1,0:T(8,128)(2,1)S(1)}, bf16[2,256,512]{2,1,0:T(8,128)(2,1)S(1)}, u32[]{:S(2)}, u32[]{:S(2)}) collective-permute-start(bf16[2,256,512]{2,1,0:T(8,128)(2,1)S(1)} %get-tuple-element.51.refs_2_), channel_id=1, source_target_pairs={{0,1},{1,0},{2,3},{3,2},{4,5},{5,4},{6,7},{7,6},{8,9},{9,8},{10,11... | collective-permute-start | bytes 1572872 | tf_op jit(solution)/shard_map/ppermute | solution.py:610
  126.4 1.0 copy-start.6
  128.9 35.0 %collective-permute-start.1 = (bf16[2,512,512]{2,1,0:T(8,128)(2,1)S(1)}, bf16[2,512,512]{2,1,0:T(8,128)(2,1)S(1)}, u32[]{:S(2)}, u32[]{:S(2)}) collective-permute-start(bf16[2,512,512]{2,1,0:T(8,128)(2,1)S(1)} %add_convert_fusion.1), channel_id=1, source_target_pairs={{0,2},{2,0},{1,3},{3,1},{4,6},{6,4},{5,7},{7,5},{8,10},{10,8},{9,1... | collective-permute-start | bytes 3145736 | tf_op jit(solution)/shard_map/ppermute | solution.py:602
  129.3 0.8 copy-start.8
  144.8 16.0 %collective-permute-start.4 = (bf16[2,256,512]{2,1,0:T(8,128)(2,1)}, bf16[2,256,512]{2,1,0:T(8,128)(2,1)}, u32[]{:S(2)}, u32[]{:S(2)}) collective-permute-start(bf16[2,256,512]{2,1,0:T(8,128)(2,1)} %get-tuple-element.37), channel_id=1, source_target_pairs={{0,1},{1,0},{2,3},{3,2},{4,5},{5,4},{6,7},{7,6},{8,9},{9,8},{10,11... | collective-permute-start | bytes 1572872 | tf_op jit(solution)/shard_map/ppermute | solution.py:600
  144.9 0.8 copy-start.7
  145.7 15.1 %copy-start.12 = (bf16[2,256,512]{2,1,0:T(8,128)(2,1)S(1)}, bf16[2,256,512]{2,1,0:T(8,128)(2,1)}, u32[]{:S(2)}) copy-start(bf16[2,256,512]{2,1,0:T(8,128)(2,1)} %get-tuple-element.36) | copy-start | bytes 1572868
  145.7 18.2 %copy-start = (bf16[2,512,512]{2,1,0:T(8,128)(2,1)S(1)}, bf16[2,512,512]{2,1,0:T(8,128)(2,1)}, u32[]{:S(2)}) copy-start(bf16[2,512,512]{2,1,0:T(8,128)(2,1)} %get-tuple-element.26.refs_2_.refs_3_) | copy-start | bytes 3145732
  160.8 5.1 %copy-start.13 = (bf16[2,256,512]{2,1,0:T(8,128)(2,1)S(1)}, bf16[2,256,512]{2,1,0:T(8,128)(2,1)}, u32[]{:S(2)}) copy-start(bf16[2,256,512]{2,1,0:T(8,128)(2,1)} %get-tuple-element.42) | copy-start | bytes 1572868
  160.8 15.7 %copy-start.4 = (bf16[2,256,512]{2,1,0:T(8,128)(2,1)S(1)}, bf16[2,256,512]{2,1,0:T(8,128)(2,1)}, u32[]{:S(2)}) copy-start(bf16[2,256,512]{2,1,0:T(8,128)(2,1)} %copy-done.3) | copy-start | bytes 1572868
  162.1 15.4 %copy-start.9 = (bf16[2,256,512]{2,1,0:T(8,128)(2,1)S(1)}, bf16[2,256,512]{2,1,0:T(8,128)(2,1)}, u32[]{:S(2)}) copy-start(bf16[2,256,512]{2,1,0:T(8,128)(2,1)} %get-tuple-element.41) | copy-start | bytes 1572868
  162.1 14.4 %collective-permute-start.5 = (bf16[2,256,512]{2,1,0:T(8,128)(2,1)S(1)}, bf16[2,256,512]{2,1,0:T(8,128)(2,1)S(1)}, u32[]{:S(2)}, u32[]{:S(2)}) collective-permute-start(bf16[2,256,512]{2,1,0:T(8,128)(2,1)S(1)} %add_convert_fusion.6), channel_id=1, source_target_pairs={{0,2},{2,0},{1,3},{3,1},{4,6},{6,4},{5,7},{7,5},{8,10},{10,8},{9,1... | collective-permute-start | bytes 1572872 | tf_op jit(solution)/shard_map/ppermute | solution.py:602
  165.7 26.5 %copy-start.2 = (bf16[2,256,512]{2,1,0:T(8,128)(2,1)S(1)}, bf16[2,256,512]{2,1,0:T(8,128)(2,1)}, u32[]{:S(2)}) copy-start(bf16[2,256,512]{2,1,0:T(8,128)(2,1)} %copy-done.1) | copy-start | bytes 1572868
  165.7 13.8 %collective-permute-start.6 = (bf16[2,512,512]{2,1,0:T(8,128)(2,1)}, bf16[2,512,512]{2,1,0:T(8,128)(2,1)S(1)}, u32[]{:S(2)}, u32[]{:S(2)}) collective-permute-start(bf16[2,512,512]{2,1,0:T(8,128)(2,1)} %get-tuple-element.50), channel_id=1, source_target_pairs={{0,1},{1,0},{2,3},{3,2},{4,5},{5,4},{6,7},{7,6},{8,9},{9,8},{10,11... | collective-permute-start | bytes 3145736 | tf_op jit(solution)/shard_map/ppermute | solution.py:623
  165.9 11.6 %collective-permute-start.10 = (bf16[2,256,512]{2,1,0:T(8,128)(2,1)S(1)}, bf16[2,256,512]{2,1,0:T(8,128)(2,1)S(1)}, u32[]{:S(2)}, u32[]{:S(2)}) collective-permute-start(bf16[2,256,512]{2,1,0:T(8,128)(2,1)S(1)} %copy-done.13), channel_id=1, source_target_pairs={{0,1},{1,0},{2,3},{3,2},{4,5},{5,4},{6,7},{7,6},{8,9},{9,8},{10,11... | collective-permute-start | bytes 1572872 | tf_op jit(solution)/shard_map/ppermute | solution.py:600
  177.5 3.0 %collective-permute-start.7 = (bf16[2,256,512]{2,1,0:T(8,128)(2,1)S(1)}, bf16[2,256,512]{2,1,0:T(8,128)(2,1)S(1)}, u32[]{:S(2)}, u32[]{:S(2)}) collective-permute-start(bf16[2,256,512]{2,1,0:T(8,128)(2,1)S(1)} %get-tuple-element.48), channel_id=1, source_target_pairs={{0,1},{1,0},{2,3},{3,2},{4,5},{5,4},{6,7},{7,6},{8,9},{9,8},{10,11... | collective-permute-start | bytes 1572872 | tf_op jit(solution)/shard_map/ppermute | solution.py:623
  177.7 14.5 %collective-permute-start.11 = (bf16[2,256,512]{2,1,0:T(8,128)(2,1)S(1)}, bf16[2,256,512]{2,1,0:T(8,128)(2,1)}, u32[]{:S(2)}, u32[]{:S(2)}) collective-permute-start(bf16[2,256,512]{2,1,0:T(8,128)(2,1)S(1)} %add_convert_fusion.3), channel_id=1, source_target_pairs={{0,2},{2,0},{1,3},{3,1},{4,6},{6,4},{5,7},{7,5},{8,10},{10,8},{9,1... | collective-permute-start | bytes 1572872 | tf_op jit(solution)/shard_map/ppermute | solution.py:602
  194.2 1.9 collective-permute-start.12
